TPU v7x, 32 devices: a whole 2x2x4 slice. The times are simulated.
32 devices in a mesh: batch: 2 (over core), expert: 4 (over y, x), dim: 4 (over z).
Axes of the slice: x: 2, y: 2, z: 4, core: 2. Of those that a mesh axis runs over, the one named last changes fastest.
Arguments:
- inputs: bfloat16 [2048, 4096], P('batch', 'dim'), may hold values from -6 to 6
- expert_ids: int32 [2048, 4], P('batch'), may hold values from 0 to 7, all different within a row; in each aligned block of 1024 rows (0 to 1023, 1024 to 2047, ...) at most 1024 rows name the same one
- gate_weight: bfloat16 [4096, 8], P('dim'), may hold values from -0.09375 to 0.09375
- reduce_weight: bfloat16 [8, 4096, 256], P('expert', ('dim', 'batch')), may hold values from -0.09375 to 0.09375
- middle_weight: bfloat16 [8, 256, 256], P('expert', 'batch'), may hold values from -0.375 to 0.375
- expand_weight: bfloat16 [8, 4096, 256], P('expert', ('dim', 'batch')), may hold values from -0.375 to 0.375
- bias: float32 [4096], P('dim'), may hold values from -3 to 3
Outputs:
- crossed: bfloat16 [2048, 4096], P(('batch', 'expert'), 'dim')
Inputs may be any that keep to these rules, and one draw needn't show every extreme that they name: `expert_ids`: each row names 4 different experts; in each aligned block of 1024 rows (the examples of one index of batch) no expert is named by more than 1024 rows, and in some block one expert is named by exactly 1024 rows.
All inputs are finite; a program needn't handle non-finite values.
Results may differ from a plain program's by a relative error of at most 0.012.
Values may be sent and summed in bfloat16 or wider, within the bound.
No kernel may reach another device: no remote copies, remote signals or barrier semaphores. Data moves between devices by JAX's collectives and lax.ppermute only.
A program may use at most 64 MiB of HBM per device.

v0:
```python
import jax
import jax.numpy as jnp
from jax import lax
from jax.sharding import PartitionSpec as P

CAP = 1024


def pick_rows(expert_rows, slot_pick):
    return expert_rows[slot_pick]


def on_device(inputs, expert_ids, gate_weight, reduce_weight, middle_weight, expand_weight, bias):
    tok_count, feature_width = inputs.shape
    local_count = reduce_weight.shape[0]
    all_experts = gate_weight.shape[1]
    first_expert = lax.axis_index("expert") * local_count
    numbers = jnp.arange(all_experts, dtype=jnp.int32)
    chosen = jnp.sum((expert_ids[:, :, None] == numbers[None, None, :]).astype(jnp.int32), axis=1)
    position = jnp.cumsum(chosen, axis=0) - chosen
    chosen_here = lax.dynamic_slice_in_dim(chosen, first_expert, local_count, 1)
    position_here = lax.dynamic_slice_in_dim(position, first_expert, local_count, 1)
    target = jnp.where(chosen_here > 0, position_here, CAP).T
    expert_grid = jnp.broadcast_to(
        jnp.arange(local_count, dtype=jnp.int32)[:, None], (local_count, tok_count)
    )
    token_grid = jnp.broadcast_to(
        jnp.arange(tok_count, dtype=jnp.int32)[None, :], (local_count, tok_count)
    )
    slot_owner = (
        jnp.full((local_count, CAP), tok_count, jnp.int32)
        .at[expert_grid, target]
        .set(token_grid, mode="drop")
    )
    padded = jnp.concatenate([inputs, jnp.zeros((1, feature_width), inputs.dtype)], axis=0)
    dispatched = padded[slot_owner]
    logits_part = jnp.dot(inputs, gate_weight, preferred_element_type=jnp.float32)
    projected = jnp.einsum(
        "esd,edr->esr",
        dispatched,
        lax.all_gather(reduce_weight, "batch", axis=1, tiled=True),
        preferred_element_type=jnp.float32,
    )
    middle_full = lax.all_gather(middle_weight, "batch", axis=1, tiled=True)
    logits, summed = (
        lax.psum(logits_part.astype(jnp.bfloat16), "dim").astype(jnp.float32),
        lax.psum(projected.astype(jnp.bfloat16), "dim").astype(jnp.float32),
    )
    squashed = jnp.tanh(summed).astype(jnp.bfloat16)
    inner_mix = jnp.einsum(
        "esj,eij->esi", squashed, middle_full, preferred_element_type=jnp.float32
    )
    hidden = jnp.tanh(inner_mix).astype(jnp.bfloat16)
    expanded = jnp.einsum(
        "esr,edr->esd",
        hidden,
        lax.all_gather(expand_weight, "batch", axis=1, tiled=True),
        preferred_element_type=jnp.float32,
    )
    gate_values = jax.nn.sigmoid(
        lax.dynamic_slice_in_dim(logits, first_expert, local_count, 1)
    ) * chosen_here.astype(jnp.float32)
    slot_read = jnp.minimum(position_here, CAP - 1).T
    picked = jax.vmap(pick_rows)(expanded, slot_read)
    expert_mix = jnp.sum(gate_values.T[:, :, None] * (picked + bias[None, None, :]), axis=0)
    partial_term = inputs.astype(jnp.float32) * expert_mix
    summed_rows = lax.psum_scatter(
        partial_term.astype(jnp.bfloat16), "expert", scatter_dimension=0, tiled=True
    ).astype(jnp.float32)
    row_count = summed_rows.shape[0]
    own_rows = lax.dynamic_slice_in_dim(inputs, lax.axis_index("expert") * row_count, row_count, 0)
    return (own_rows.astype(jnp.float32) + summed_rows).astype(jnp.bfloat16)


def solution(mesh):
    in_specs = (
        P("batch", "dim"),
        P("batch", None),
        P("dim", None),
        P("expert", ("dim", "batch"), None),
        P("expert", "batch", None),
        P("expert", ("dim", "batch"), None),
        P("dim"),
    )
    out_specs = P(("batch", "expert"), "dim")
    return jax.shard_map(
        on_device, mesh=mesh, in_specs=in_specs, out_specs=out_specs, check_vma=False
    )
```

profile of v0, /device:TPU:0, one launch (start us, length us, event | category | flops | bytes accessed | tf_op | source)
XLA Modules:
  0.0 194.0 jit_solution(1393359733203876569)
XLA Ops:
  6.5 0.0 copy-start
  6.5 0.0 all-gather.3.cloned.1.call-start
  6.5 0.7 all-gather.3.cloned.1.call-update
  7.3 0.0 all-gather.5.cloned.1.call-start
  7.3 0.7 all-gather.5.cloned.1.call-update
  8.0 0.0 all-reduce.3.cloned.1.call-start
  8.1 0.7 convert_reduce_fusion
  8.8 2.3 %reduce-window.6 = s32[8,8,128]{2,1,0:T(8,128)S(1)} reduce-window(s32[8,8,128]{2,1,0:T(8,128)S(1)} %copy.12, s32[]{:T(128)} %constant.15.clone.1), window={size=1x1x128 pad=0_0x0_0x127_0}, to_apply=%region_2.3 | reduce-window | flops 1040384 | bytes 65540 | tf_op jit(solution)/shard_map/reduce-window
  11.1 0.3 slice_reduce_fusion
  11.4 0.2 reduce-window.9
  11.6 0.1 add_bitcast_fusion
  11.7 0.8 and_reduce_fusion
  12.4 0.7 multiply_reduce_fusion.1
  13.2 8.0 %scatter_custom_fusion = s32[2048]{0:T(1024)S(1)} fusion(s32[2048]{0:T(1024)S(1)} %get-tuple-element.6, s32[2048]{0:T(1024)S(1)} %get-tuple-element.5, s32[]{:T(128)} %constant.5.clone.1), kind=kCustom, calls=%fused_computation.40 | custom fusion | bytes 8196
  21.3 1.8 concatenate.6
  23.1 9.7 %gather_fusion = bf16[2048,1024]{1,0:T(8,128)(2,1)} fusion(bf16[1025,1024]{1,0:T(8,128)(2,1)S(1)} %concatenate.6, s32[2048]{0:T(1024)S(1)} %bitcast_clamp_fusion), kind=kCustom, calls=%fused_computation | custom fusion | bytes 8396800 | tf_op jit(solution)/shard_map/gather | solution.py:36
  32.8 0.0 copy-start.1
  32.8 0.0 all-gather.3.cloned.1.call-done
  32.8 0.0 copy-start.2
  32.8 4.9 %convolution_convert_fusion = bf16[2,1024,256]{2,1,0:T(8,128)(2,1)} fusion(bf16[2,1024,1024]{2,1,0:T(8,128)(2,1)} %bitcast.61, bf16[2,1024,256]{2,1,0:T(8,128)(2,1)} %all-gather.3.cloned.1.call-done), kind=kOutput, calls=%fused_computation.7 | convolution fusion | flops 1074266112 | bytes 6291456 | tf_op jit(solution)/shard_map/esd,edr->esr/dot_general | solution.py:38
  37.7 0.0 all-reduce.3.cloned.1.call-update
  37.7 0.0 reduce-scatter.2.cloned.1.call-start
  37.8 0.0 copy-done
  37.8 0.0 copy-done.1
  37.8 0.6 convolution_convert_fusion.1
  38.4 21.4 %psum.14 = bf16[1024,8]{0,1:T(8,128)(2,1)S(1)} all-reduce(bf16[1024,8]{0,1:T(8,128)(2,1)S(1)} %convolution_convert_fusion.1), channel_id=1, replica_groups=mesh['batch'=2,'expert'=4,'dim'=4] {'dim'}, use_global_device_ids=true, to_apply=%region_0.0 | all-reduce | flops 8192 | bytes 32768 | tf_op jit(solution)/shard_map/psum | solution.py:46
  59.9 0.0 copy-done.2
  59.9 2.0 %all_gather.10 = bf16[2,256,256]{2,1,0:T(8,128)(2,1)S(1)} all-gather(bf16[2,128,256]{2,1,0:T(8,128)(2,1)S(1)} %copy-done.2), channel_id=1, replica_groups=mesh['batch'=2,'expert'=4,'dim'=4] {'batch'}, dimensions={1}, use_global_device_ids=true | all-gather | bytes 393216 | tf_op jit(solution)/shard_map/all_gather | solution.py:44
  61.9 0.0 all-gather.5.cloned.1.call-done
  61.9 30.9 %all-reduce.3.cloned.1.call-done = bf16[2,1024,256]{2,1,0:T(8,128)(2,1)} async-done(((bf16[2,1024,256]{2,1,0:T(8,128)(2,1)}), bf16[2,1024,256]{2,1,0:T(8,128)(2,1)}) %all-reduce.3.cloned.1.call-update) | async-done | bytes 1048592 | tf_op jit(solution)/shard_map/psum | solution.py:47
  92.8 6.5 %fusion = f32[2,1024,1024]{2,1,0:T(8,128)} fusion(bf16[2,1024,256]{2,1,0:T(8,128)(2,1)} %all-gather.5.cloned.1.call-done, bf16[2,256,256]{2,1,0:T(8,128)(2,1)S(1)} %all_gather.10, bf16[2,1024,256]{2,1,0:T(8,128)(2,1)} %all-reduce.3.cloned.1.call-done), kind=kOutput, calls=%fused_computation.8 | convolution fusion | flops 1343750144 | bytes 10747904 | tf_op jit(solution)/shard_map/esr,edr->esd/dot_general | solution.py:54
  99.3 0.0 copy-start.3
  99.3 44.0 %gather_fusion.1 = f32[2048,1024]{1,0:T(8,128)} fusion(f32[2,1024,1024]{2,1,0:T(8,128)} %fusion, s32[2048]{0:T(1024)S(1)} %bitcast.59), kind=kCustom, calls=%fused_computation.1 | custom fusion | bytes 16793600 | tf_op jit(solution)/shard_map/vmap()/gather | solution.py:10
  143.3 0.0 copy-done.3
  143.3 4.3 %multiply_reduce_fusion = f32[1024,1024]{1,0:T(8,128)S(1)} fusion(f32[2,1024,1024]{2,1,0:T(8,128)} %bitcast.60, f32[1024]{0:T(1024)S(1)} %copy-done.3, f32[2,1024]{1,0:T(2,128)S(1)} %fusion.9), kind=kLoop, calls=%fused_computation.3 | loop fusion | flops 5242880 | bytes 12595200 | tf_op jit(solution)/shard_map/reduce_sum | solution.py:65
  147.5 2.2 %multiply_convert_fusion = bf16[1024,1024]{1,0:T(8,128)(2,1)} fusion(f32[1024,1024]{1,0:T(8,128)S(1)} %multiply_reduce_fusion, bf16[1024,1024]{1,0:T(8,128)(2,1)S(1)} %copy-done.1), kind=kLoop, calls=%fused_computation.4 | loop fusion | flops 3145728 | bytes 8388608 | tf_op jit(solution)/shard_map/convert_element_type | solution.py:68
  149.8 0.0 reduce-scatter.2.cloned.1.call-update
  149.8 35.6 %reduce-scatter.2.cloned.1.call-done = bf16[256,1024]{1,0:T(8,128)(2,1)} async-done(((bf16[1024,1024]{1,0:T(8,128)(2,1)}), bf16[256,1024]{1,0:T(8,128)(2,1)}) %reduce-scatter.2.cloned.1.call-update) | async-done | bytes 524304 | tf_op jit(solution)/shard_map/reduce_scatter | solution.py:67
  185.4 2.0 %add_convert_fusion = bf16[256,1024]{1,0:T(8,128)(2,1)} fusion(bf16[256,1024]{1,0:T(8,128)(2,1)} %reduce-scatter.2.cloned.1.call-done, bf16[1024,1024]{1,0:T(8,128)(2,1)S(1)} %copy-done.1, s32[]{:T(128)S(6)} %select_n.23), kind=kLoop, calls=%fused_computation.10 | loop fusion | flops 1048576 | bytes 1572868 | tf_op jit(solution)/shard_map/convert_element_type | solution.py:72
  (13 shorter events, 0.1 us)
Async XLA Ops:
  6.5 31.2 %copy-start = (bf16[1024,8]{0,1:T(8,128)(2,1)S(1)}, bf16[1024,8]{0,1:T(8,128)(2,1)}, u32[]{:S(2)}) copy-start(bf16[1024,8]{0,1:T(8,128)(2,1)} %param.9) | copy-start | bytes 49156
  6.5 26.2 %all-gather.3.cloned.1.call-start = ((), (), s32[]{:S(2)}) async-start(), calls=%async_computation.1 | async-start | bytes 1572864 | tf_op jit(solution)/shard_map/all_gather | solution.py:41
  7.3 54.7 %all-gather.5.cloned.1.call-start = ((), (), s32[]{:S(2)}) async-start(), calls=%async_computation.3 | async-start | bytes 1572864 | tf_op jit(solution)/shard_map/all_gather | solution.py:57
  8.0 84.8 %all-reduce.3.cloned.1.call-start = ((), (), s32[]{:S(2)}) async-start(), calls=%async_computation.2 | async-start | bytes 2097152 | tf_op jit(solution)/shard_map/psum | solution.py:47
  32.8 5.0 %copy-start.1 = (bf16[1024,1024]{1,0:T(8,128)(2,1)S(1)}, bf16[1024,1024]{1,0:T(8,128)(2,1)}, u32[]{:S(2)}) copy-start(bf16[1024,1024]{1,0:T(8,128)(2,1)} %param.7) | copy-start | bytes 6291460
  32.8 27.1 %copy-start.2 = (bf16[2,128,256]{2,1,0:T(8,128)(2,1)S(1)}, bf16[2,128,256]{2,1,0:T(8,128)(2,1)}, u32[]{:S(2)}) copy-start(bf16[2,128,256]{2,1,0:T(8,128)(2,1)} %param.11) | copy-start | bytes 393220
  37.7 147.7 %reduce-scatter.2.cloned.1.call-start = ((), (), s32[]{:S(2)}) async-start(), calls=%async_computation.4 | async-start | bytes 2621440 | tf_op jit(solution)/shard_map/reduce_scatter | solution.py:67
  99.3 44.0 %copy-start.3 = (f32[1024]{0:T(1024)S(1)}, f32[1024]{0:T(1024)}, u32[]{:S(2)}) copy-start(f32[1024]{0:T(1024)} %param.13) | copy-start | bytes 12292
Sparse Core Ops, SparseCore 0:
  8.9 11.7 all-gather.2
  22.2 10.1 all-gather.4
  37.8 54.9 all-reduce.2
  149.9 35.4 reduce-scatter.1
where the time goes:
time: 195 us; the launch traced here: 194 us
  waiting for transfers between devices  68 us (35%)
  local copies, waits for them, and re-layouts  63.8 us (33%)
  blocking collectives  23.4 us (12%)
  other arithmetic  13.4 us (7%)
  between operations  13.3 us (7%)
  matrix products  12 us (6%)
    gather x1, local copies, waits for them, and re-layouts, pick_rows(): return expert_rows[slot_pick]  44 us
    reduce_scatter x1, waiting for transfers between devices, on_device(): lax.psum_scatter(partial_term.astype(jnp.bfloat16), 'expert', scatter_dim...  35.6 us
    psum x1, waiting for transfers between devices, on_device(): lax.psum(projected.astype(jnp.bfloat16), 'dim').astype(jnp.float32)  30.9 us
    psum x1, blocking collectives, on_device(): lax.psum(logits_part.astype(jnp.bfloat16), 'dim').astype(jnp.float32)  21.4 us
    gather x1, local copies, waits for them, and re-layouts, on_device(): dispatched = padded[slot_owner]  9.67 us
    unnamed x12, local copies, waits for them, and re-layouts  8.09 us
    dot_general x1, matrix products, on_device(): jnp.einsum('esr,edr->esd', hidden, lax.all_gather(expand_weight, 'batch',...  6.48 us
    dot_general x1, matrix products, on_device(): jnp.einsum('esd,edr->esr', dispatched, lax.all_gather(reduce_weight, 'bat...  4.9 us
  transfers between devices with their start and end apart: 4, of which 2 were waited for; matrix products, arithmetic and copies ran while one was open for 16% of the time, Pallas kernels for 0%

commit v1 on v0

v1 whole, which is shorter than its diff:
```python
import jax
import jax.numpy as jnp
from jax import lax
from jax.experimental import pallas as pl
from jax.experimental.pallas import tpu as pltpu
from jax.sharding import PartitionSpec as P


F32 = jnp.float32
BF16 = jnp.bfloat16
LAST = (((1,), (1,)), ((), ()))
MIB = 1 << 20
SPLIT = 2


def peer_to(i, m, n):
    return i ^ m if n & (n - 1) == 0 else (i + m) % n


def peer_from(i, m, n):
    return i ^ m if n & (n - 1) == 0 else (i - m + n) % n


def send(x, axis, m, n):
    return lax.ppermute(x, axis, [(i, peer_to(i, m, n)) for i in range(n)])


def vmem():
    return pl.BlockSpec(memory_space=pltpu.VMEM)


def call(body, args, outs, scratch=(), limit=12, flops=None, held=(), alias=None):
    space = lambda k: pl.BlockSpec(memory_space=pl.ANY) if k in held else vmem()
    cost = None if flops is None else pl.CostEstimate(flops, 0, flops // 500)
    return pl.pallas_call(
        body,
        in_specs=[pl.BlockSpec(memory_space=pltpu.SMEM)] + [space(k) for k in range(1, len(args))],
        out_specs=[space("out") for _ in outs],
        out_shape=[jax.ShapeDtypeStruct(s, t) for s, t in outs],
        scratch_shapes=list(scratch),
        input_output_aliases={} if alias is None else {alias: 0},
        cost_estimate=cost,
        compiler_params=pltpu.CompilerParams(vmem_limit_bytes=limit * MIB),
    )(*args)


def rows_at(start, size):
    return pl.ds(pl.multiple_of(start, size), size)


def as_rows(cols_t):
    top, n = cols_t.shape
    pad = jnp.zeros((8 - top, n), cols_t.dtype)
    return jnp.concatenate([cols_t, pad], axis=0).T


def project(place, x, pieces, row_starts, n_row, pair, gate_t=None):
    n_loc, width, rank = pieces[0].shape
    n_piece = len(pieces)
    count = row_starts[1]

    def body(place_ref, x_ref, *refs):
        w_refs, outs = refs[:n_piece], refs[n_piece:]
        starts = row_starts[0](place_ref)
        first = [place_ref[0], 1 - place_ref[0]] if pair else [0]
        xs = []
        for p in range(n_piece):
            cols = rows_at(first[p] * width, width)
            xs.append(jnp.concatenate([x_ref[rows_at(s, n_row), cols] for s in starts], axis=0))
        if gate_t is not None:
            logit = None
            for p in range(n_piece):
                part = lax.dot_general(
                    outs[0][:, rows_at(first[p] * width, width)], xs[p], LAST,
                    preferred_element_type=F32,
                )
                logit = part if logit is None else logit + part
            outs[-1][...] = logit
            outs = outs[1:]
        for e in range(n_loc):
            acc = jnp.dot(xs[0], w_refs[0][e], preferred_element_type=F32)
            for p in range(1, n_piece):
                acc = acc + jnp.dot(xs[p], w_refs[p][e], preferred_element_type=F32)
            acc = acc.astype(BF16)
            for k in range(count):
                outs[k][:, e * rank : (e + 1) * rank] = acc[k * n_row : (k + 1) * n_row]

    args = [place, x, *pieces]
    outs = [((n_row, n_loc * rank), BF16)] * count
    if gate_t is not None:
        args.append(gate_t)
        outs = outs + [((gate_t.shape[0], n_row * count), F32)]
    return call(body, args, outs)


def widen(place, wide):
    n_loc, half, rank = wide.shape

    def body(place_ref, w_ref, out_ref, buf, sem):
        copy = pltpu.make_async_copy(w_ref, buf, sem)
        copy.start()
        copy.wait()
        for e in range(n_loc):
            out_ref[e] = buf[e].T

    return call(
        body, [place, wide], [((n_loc, rank, half), BF16)],
        [pltpu.VMEM(wide.shape, BF16), pltpu.SemaphoreType.DMA], flops=4_000_000_000, held=(1,),
    )[0]


def turn(place, mids):
    n_loc, half, rank = mids[0].shape

    def body(place_ref, *refs):
        for q in range(len(mids)):
            for e in range(n_loc):
                refs[-1][q * n_loc + e] = refs[q][e].T

    return call(body, [place, *mids], [((len(mids) * n_loc, rank, half), BF16)])[0]


def wide_ids(ids_ref, start, n, width):
    ids = as_rows(ids_ref[:, rows_at(start, n)].astype(F32))
    top = ids_ref.shape[0]
    return [jnp.broadcast_to(ids[:, j : j + 1], (n, width)).astype(BF16) for j in range(top)]


def pack(place, ids_t, parts, at, n_expert, n_dim, n_loc, logit=None):
    rows, wide = parts[0].shape
    rank = wide // n_loc
    per = rows // n_dim
    top = ids_t.shape[0]
    n_part = len(parts)
    more = 0 if logit is None else logit.shape[0]

    def body(place_ref, ids_ref, *refs):
        p_refs, scratch = refs[:n_part], refs[-1]
        outs = refs[n_part:-1] if logit is None else refs[n_part + 1 : -1]
        x_at, z_at = place_ref[1], place_ref[2]
        ids = wide_ids(ids_ref, x_at * (rows * SPLIT) + at * rows, rows, rank)
        for j in range(top):
            acc = jnp.zeros((rows, rank), BF16)
            for q in range(n_part):
                base = peer_from(x_at, q, n_expert) * n_loc
                for e in range(n_loc):
                    number = (base + e).astype(F32).astype(BF16)
                    acc = jnp.where(
                        ids[j] == number, p_refs[q][:, e * rank : (e + 1) * rank], acc
                    )
            scratch[:, j * rank : (j + 1) * rank] = acc
        for m in range(n_dim):
            outs[m][:per, :] = scratch[rows_at(peer_to(z_at, m, n_dim) * per, per), :]
        if logit is not None:
            full = refs[n_part][...]
            n = full.shape[1]
            high = full.astype(BF16)
            low = (full - high.astype(F32)).astype(BF16)
            for m in range(n_dim):
                outs[m][per:, :n] = high
                outs[m][per:, n : 2 * n] = low
                outs[m][per:, 2 * n :] = jnp.zeros((more, top * rank - 2 * n), BF16)

    return call(
        body,
        [place, ids_t, *parts] + ([] if logit is None else [logit]),
        [((per + more, top * rank), BF16)] * n_dim,
        [pltpu.VMEM((rows, top * rank), BF16)],
    )


def mix(place, ids_t, gates_t, parts, mids, at, block, n_expert, n_dim, pair):
    wide = parts[0].shape[1]
    top, _ = ids_t.shape
    rank = wide // top
    per = block // SPLIT // n_dim
    n_part = len(parts)
    n_piece = len(mids)
    n_all, _, half = mids[0].shape
    n_loc = n_all // n_expert
    make = gates_t is None

    def body(place_ref, ids_ref, *refs):
        if make:
            p_refs, refs = refs[:n_part], refs[n_part:]
        else:
            g_ref, p_refs, refs = refs[0], refs[1 : n_part + 1], refs[n_part + 1 :]
        m_refs, refs = refs[:n_piece], refs[n_piece:]
        if make:
            out_ref, g_out, squash, ids_s, gate_s = refs
            logit = jnp.zeros((n_all, block), F32)
            for p in range(n_part):
                logit = logit + p_refs[p][per:, :block].astype(F32)
                logit = logit + p_refs[p][per:, block : 2 * block].astype(F32)
            gates_t = jax.nn.sigmoid(logit)
            g_out[...] = gates_t
        else:
            out_ref, squash, ids_s, gate_s = refs
            gates_t = g_ref[...]
        x_at, z_at = place_ref[1], place_ref[2]
        first = [place_ref[0], 1 - place_ref[0]] if pair else [0]
        ids_s[...] = as_rows(ids_ref[:, rows_at(x_at * block, block)])
        gate_s[...] = gates_t.T
        mine = rows_at(at * per * n_dim + z_at * per, per)
        ids, gates = ids_s[mine, :], gate_s[mine, :]
        lane = lax.broadcasted_iota(jnp.int32, gates.shape, 1)
        chosen, gate = [], []
        for j in range(top):
            cols = slice(j * rank, (j + 1) * rank)
            acc = p_refs[0][:per, cols].astype(F32)
            for p in range(1, n_part):
                acc = acc + p_refs[p][:per, cols].astype(F32)
            squash[j * per : (j + 1) * per, :] = jnp.tanh(acc).astype(BF16)
            own = ids[:, j : j + 1]
            chosen.append(own)
            gate.append(jnp.sum(jnp.where(lane == own, gates, 0.0), axis=1, keepdims=True))
        chosen = jnp.broadcast_to(jnp.concatenate(chosen, axis=0), (top * per, half))
        sq = squash[...]
        for h in range(n_piece):
            acc = jnp.zeros((top * per, half), F32)
            for q in range(n_expert):
                base = peer_from(x_at, q, n_expert) * n_loc
                for e in range(n_loc):
                    got = jnp.dot(sq, m_refs[h][q * n_loc + e], preferred_element_type=F32)
                    acc = jnp.where(chosen == base + e, got, acc)
            hid = jnp.tanh(acc)
            for j in range(top):
                start = pl.multiple_of(j * rank + first[h] * half, half)
                gated = hid[j * per : (j + 1) * per, :] * gate[j]
                out_ref[:, pl.ds(start, half)] = gated.astype(BF16)

    return call(
        body,
        [place, ids_t] + ([] if make else [gates_t]) + [*parts, *mids],
        [((per, wide), BF16)] + ([((n_all, block), F32)] if make else []),
        [
            pltpu.VMEM((top * per, rank), BF16),
            pltpu.VMEM((block, 8), jnp.int32),
            pltpu.VMEM((block, n_all), F32),
        ],
    )


def expand(place, x, ids_t, bias, gates_t, hids, wides, at, so_far, n_expert, n_dim, n_loc, pair):
    per, wide = hids[0].shape
    top, _ = ids_t.shape
    rank = wide // top
    rows = per * n_dim
    block = rows * SPLIT
    feats = x.shape[1]
    n_src = len(wides)
    n_piece = len(wides[0])
    half = wides[0][0].shape[2]
    flat_w = [w for src in wides for w in src]
    n_h, n_w = len(hids), len(flat_w)
    n_first = 0 if so_far is None else 1

    def body(place_ref, *refs):
        refs = refs[n_first:]
        x_ref, ids_ref, bias_ref, g_ref, *refs = refs
        h_refs, w_refs = refs[:n_h], refs[n_h : n_h + n_w]
        out_ref, hid, left, buf, sems = refs[n_h + n_w :]
        x_at, z_at = place_ref[1], place_ref[2]
        first = [place_ref[0], 1 - place_ref[0]] if pair else [0]
        mine = rows_at(x_at * block + at * rows, rows)
        for m in range(n_dim):
            hid[rows_at(peer_from(z_at, m, n_dim) * per, per), :] = h_refs[m][...]
        ids = wide_ids(ids_ref, x_at * block + at * rows, rows, rank)
        for q in range(n_src):
            base = peer_from(x_at, q, n_expert) * n_loc
            for e in range(n_loc):
                number = (base + e).astype(F32).astype(BF16)
                acc = jnp.zeros((rows, rank), BF16)
                for j in range(top):
                    acc = jnp.where(ids[j] == number, hid[:, j * rank : (j + 1) * rank], acc)
                left[q * n_loc + e] = acc
        own = ids_ref[:, mine]
        gates = g_ref[:, at * rows : (at + 1) * rows]
        number = lax.broadcasted_iota(jnp.int32, gates.shape, 0)
        hit = own[0:1, :] == number
        for j in range(1, top):
            hit = hit | (own[j : j + 1, :] == number)
        total = jnp.sum(jnp.where(hit, gates, 0.0), axis=0, keepdims=True)
        total = jnp.broadcast_to(total, gates.shape).T[:, 0:1]
        copies = []
        for h in range(n_piece):
            acc = jnp.zeros((rows, half), F32)
            for q in range(n_src):
                for e in range(n_loc):
                    w = w_refs[q * n_piece + h][e]
                    acc = acc + jnp.dot(left[q * n_loc + e], w, preferred_element_type=F32)
            cols = rows_at(first[h] * half, half)
            xs = x_ref[mine, cols].astype(F32)
            buf[h] = (xs + xs * (acc + total * bias_ref[:, cols])).astype(BF16)
            there = out_ref.at[at * rows : (at + 1) * rows, cols]
            copies.append(pltpu.make_async_copy(buf.at[h], there, sems.at[h]))
            copies[-1].start()
        for c in copies:
            c.wait()

    args = [place] + ([] if so_far is None else [so_far])
    return call(
        body,
        args + [x, ids_t, bias, gates_t, *hids, *flat_w],
        [((block, feats), BF16)],
        [
            pltpu.VMEM((rows, wide), BF16),
            pltpu.VMEM((n_src * n_loc, rows, rank), BF16),
            pltpu.VMEM((n_piece, rows, half), BF16),
            pltpu.SemaphoreType.DMA((n_piece,)),
        ],
        held=("out",) if so_far is None else ("out", 1),
        alias=None if so_far is None else 1,
    )[0]


def on_device(
    nb, ne, nz, inputs, expert_ids, gate_weight, reduce_weight, middle_weight, expand_weight, bias
):
    tok, _ = inputs.shape
    n_loc = reduce_weight.shape[0]
    block = tok // ne
    n_row = block // SPLIT
    pair = nb == 2
    place = jnp.stack([lax.axis_index(a).astype(jnp.int32) for a in ("batch", "expert", "dim")])
    ids_t = expert_ids.T

    def swap(w):
        return lax.ppermute(w, "batch", [(0, 1), (1, 0)])

    def whole(w):
        return lax.all_gather(w, "batch", axis=1, tiled=True)

    if pair:
        pieces = [reduce_weight, swap(reduce_weight)]
    else:
        pieces = [whole(reduce_weight)]
        middle_weight, expand_weight = whole(middle_weight), whole(expand_weight)
    far = list(range(1, ne))
    wide = widen(place, expand_weight)
    mids = [middle_weight] + [send(middle_weight, "expert", m, ne) for m in far]

    parts = []
    for h in range(SPLIT):
        starts = lambda r, h=h: [peer_to(r[1], m, ne) * block + h * n_row for m in far]
        sent = project(place, inputs, pieces, (starts, len(far)), n_row, pair)
        parts.append([send(s, "expert", m, ne) for s, m in zip(sent, far)])
    starts = lambda r: [r[1] * block + h * n_row for h in range(SPLIT)]
    *own, logit = project(place, inputs, pieces, (starts, SPLIT), n_row, pair, gate_weight.T)
    wides = [wide] + [send(wide, "expert", m, ne) for m in far]
    mids = [turn(place, mids)]
    if pair:
        mids.append(swap(mids[0]))

    sums = []
    for h in range(SPLIT):
        packed = pack(
            place, ids_t, [own[h]] + parts[h], h, ne, nz, n_loc, logit if h == 0 else None
        )
        sums.append([packed[0]] + [send(packed[m], "dim", m, nz) for m in range(1, nz)])
    hids, gates_t = [], None
    for h in range(SPLIT):
        hid, *made = mix(place, ids_t, gates_t, sums[h], mids, h, block, ne, nz, pair)
        gates_t = made[0] if made else gates_t
        hids.append([hid] + [send(hid, "dim", m, nz) for m in range(1, nz)])
    wides = [[w] + ([swap(w)] if pair else []) for w in wides]
    out = None
    for h in range(SPLIT):
        out = expand(
            place, inputs, ids_t, bias[None, :], gates_t, hids[h], wides, h, out, ne, nz, n_loc,
            pair,
        )
    return out


def solution(mesh):
    sizes = dict(mesh.shape)
    in_specs = (
        P("batch", "dim"),
        P("batch", None),
        P("dim", None),
        P("expert", ("dim", "batch"), None),
        P("expert", "batch", None),
        P("expert", ("dim", "batch"), None),
        P("dim"),
    )
    out_specs = P(("batch", "expert"), "dim")
    nb, ne, nz = sizes["batch"], sizes["expert"], sizes["dim"]

    def body(*args):
        return on_device(nb, ne, nz, *args)

    return jax.shard_map(body, mesh=mesh, in_specs=in_specs, out_specs=out_specs, check_vma=False)
```

time: 195 us -> 87.4 us (0.45)
  local copies, waits for them, and re-layouts: 63.8 us -> 1.07 us
  starting transfers between devices: 0.12 us -> 40.9 us
  waiting for transfers between devices: 68 us -> 30.4 us
  blocking collectives: 23.4 us -> 0 us
  other arithmetic: 13.4 us -> 0.08 us
  between operations: 13.3 us -> 0.2 us
  Pallas kernels: 0 us -> 13.1 us
  matrix products: 12 us -> 0 us
    gather x2 -> x0, local copies, waits for them, and re-layouts: 53.6 us -> none  [the longest x1 44 us: pick_rows(): return expert_rows[slot_pick]]
    ppermute x0 -> x30, starting transfers between devices: none -> 40.9 us  [the longest x24 39.9 us: send(): return lax.ppermute(x, axis, [(i, peer_to(i, m, n)) for i in range(n)])]
    reduce_scatter x1 -> x0, waiting for transfers between devices: 35.6 us -> none  [on_device(): lax.psum_scatter(partial_term.astype(jnp.bfloat16), 'expert', scatter_dim...]
    psum x1 -> x0, waiting for transfers between devices: 30.9 us -> none  [on_device(): lax.psum(projected.astype(jnp.bfloat16), 'dim').astype(jnp.float32)]
    ppermute x0 -> x30, waiting for transfers between devices: none -> 30.4 us  [the longest x24 30.4 us: send(): return lax.ppermute(x, axis, [(i, peer_to(i, m, n)) for i in range(n)])]
    psum x1 -> x0, blocking collectives: 21.4 us -> none  [on_device(): lax.psum(logits_part.astype(jnp.bfloat16), 'dim').astype(jnp.float32)]
    pallas_call x0 -> x11, Pallas kernels: none -> 13.1 us  [call(): pl.pallas_call(body, in_specs=[pl.BlockSpec(memory_space=pltpu.SMEM)] + [...]
    dot_general x3 -> x0, matrix products: 12 us -> none  [the longest x1 6.48 us: on_device(): jnp.einsum('esr,edr->esd', hidden, lax.all_gather(expand_weight, 'batch',...]
  transfers between devices with their start and end apart: 4 -> 30, of which waited for: 2 -> 12; matrix products, arithmetic and copies ran while one was open for 16% -> 0% of each run, Pallas kernels for 0% -> 13%
where the time goes in v1:
time: 87.4 us; the launch traced here: 85.8 us
  starting transfers between devices  40.9 us (47%)
  waiting for transfers between devices  30.4 us (35%)
  Pallas kernels  13.1 us (15%)
  local copies, waits for them, and re-layouts  1.07 us (1%)
    ppermute x24, starting transfers between devices, send(): return lax.ppermute(x, axis, [(i, peer_to(i, m, n)) for i in range(n)])  39.9 us
    ppermute x24, waiting for transfers between devices, send(): return lax.ppermute(x, axis, [(i, peer_to(i, m, n)) for i in range(n)])  30.4 us
    pallas_call x11, Pallas kernels, call(): pl.pallas_call(body, in_specs=[pl.BlockSpec(memory_space=pltpu.SMEM)] + [...  13.1 us
  transfers between devices with their start and end apart: 30, of which 12 were waited for; matrix products, arithmetic and copies ran while one was open for 0% of the time, Pallas kernels for 13%

profile of v1, /device:TPU:0, one launch (start us, length us, event | category | flops | bytes accessed | tf_op | source)
XLA Modules:
  0.0 85.8 jit_solution(7246848563844988426)
XLA Ops:
  0.0 3.0 %collective-permute-start.7 = (bf16[2,128,256]{2,1,0:T(8,128)(2,1)}, bf16[2,128,256]{2,1,0:T(8,128)(2,1)S(1)}, u32[]{:S(2)}, u32[]{:S(2)}) collective-permute-start(bf16[2,128,256]{2,1,0:T(8,128)(2,1)} %refs_0_.7), channel_id=1, source_target_pairs={{0,4},{4,0},{8,12},{12,8},{1,5},{5,1},{9,13},{13,9},{2,6},{6,2},{1... | collective-permute-start | bytes 393224 | tf_op jit(solution)/shard_map/ppermute | solution.py:25
  3.0 1.5 %collective-permute-start.8 = (bf16[2,128,256]{2,1,0:T(8,128)(2,1)}, bf16[2,128,256]{2,1,0:T(8,128)(2,1)S(1)}, u32[]{:S(2)}, u32[]{:S(2)}) collective-permute-start(bf16[2,128,256]{2,1,0:T(8,128)(2,1)} %refs_0_.7), channel_id=1, source_target_pairs={{0,8},{4,12},{8,0},{12,4},{1,9},{5,13},{9,1},{13,5},{2,10},{6,14},... | collective-permute-start | bytes 393224 | tf_op jit(solution)/shard_map/ppermute | solution.py:25
  4.5 0.1 pad_add_fusion.place_ref
  4.6 1.0 %copy-done.6 = bf16[2,512,256]{2,1,0:T(8,128)(2,1)S(1)} copy-done((bf16[2,512,256]{2,1,0:T(8,128)(2,1)S(1)}, bf16[2,512,256]{2,1,0:T(8,128)(2,1)}, u32[]{:S(2)}) %copy-start.6) | copy-done | bytes 524312
  5.6 0.8 shard_map.78.refs_8_.refs_9_
  6.4 2.0 %collective-permute-start.15 = (bf16[2,256,512]{2,1,0:T(8,128)(2,1)S(1)}, bf16[2,256,512]{2,1,0:T(8,128)(2,1)S(1)}, u32[]{:S(2)}, u32[]{:S(2)}) collective-permute-start(bf16[2,256,512]{2,1,0:T(8,128)(2,1)S(1)} %shard_map.78.refs_8_.refs_9_), channel_id=1, source_target_pairs={{0,4},{4,0},{8,12},{12,8},{1,5},{5,1},{9,13},{13,9},{2,6},{6,2},{1... | collective-permute-start | bytes 1572872 | tf_op jit(solution)/shard_map/ppermute | solution.py:25
  8.4 1.5 %collective-permute-start.17 = (bf16[2,256,512]{2,1,0:T(8,128)(2,1)S(1)}, bf16[2,256,512]{2,1,0:T(8,128)(2,1)S(1)}, u32[]{:S(2)}, u32[]{:S(2)}) collective-permute-start(bf16[2,256,512]{2,1,0:T(8,128)(2,1)S(1)} %shard_map.78.refs_8_.refs_9_), channel_id=1, source_target_pairs={{0,8},{4,12},{8,0},{12,4},{1,9},{5,13},{9,1},{13,5},{2,10},{6,14},... | collective-permute-start | bytes 1572872 | tf_op jit(solution)/shard_map/ppermute | solution.py:25
  10.0 1.0 %collective-permute-done.8.refs_2_ = bf16[2,128,256]{2,1,0:T(8,128)(2,1)S(1)} collective-permute-done((bf16[2,128,256]{2,1,0:T(8,128)(2,1)}, bf16[2,128,256]{2,1,0:T(8,128)(2,1)S(1)}, u32[]{:S(2)}, u32[]{:S(2)}) %collective-permute-start.8) | collective-permute-done | bytes 131104 | tf_op jit(solution)/shard_map/ppermute | solution.py:25
  11.0 1.5 %collective-permute-start.19 = (bf16[2,256,512]{2,1,0:T(8,128)(2,1)S(1)}, bf16[2,256,512]{2,1,0:T(8,128)(2,1)S(1)}, u32[]{:S(2)}, u32[]{:S(2)}) collective-permute-start(bf16[2,256,512]{2,1,0:T(8,128)(2,1)S(1)} %shard_map.78.refs_8_.refs_9_), channel_id=1, source_target_pairs={{0,12},{4,8},{8,4},{12,0},{1,13},{5,9},{9,5},{13,1},{2,14},{6,10},... | collective-permute-start | bytes 1572872 | tf_op jit(solution)/shard_map/ppermute | solution.py:25
  12.4 0.7 shard_map.76.refs_4_.refs_5_
  13.2 0.6 collective-permute-start.10
  13.8 1.1 %shard_map.74 = (bf16[128,512]{1,0:T(8,128)(2,1)S(1)}, bf16[128,512]{1,0:T(8,128)(2,1)S(1)}, bf16[128,512]{1,0:T(8,128)(2,1)S(1)}) custom-call(s32[3]{0:T(128)S(1)} %pad_add_fusion.place_ref, bf16[1024,1024]{1,0:T(8,128)(2,1)S(1)} %copy-done, bf16[2,512,256]{2,1,0:T(8,128)(2,1)S(1)} %copy-done.1, bf16[2,512,256]{2,1,0:T(8,128)(2,1)S(1)} %collective-permute-done.refs_1_), custom_call_target="tpu_custom_call" | custom-call | tf_op jit(solution)/shard_map/pallas_call | solution.py:35
  14.9 6.4 %collective-permute-done.15.refs_10_.refs_11_ = bf16[2,256,512]{2,1,0:T(8,128)(2,1)S(1)} collective-permute-done((bf16[2,256,512]{2,1,0:T(8,128)(2,1)S(1)}, bf16[2,256,512]{2,1,0:T(8,128)(2,1)S(1)}, u32[]{:S(2)}, u32[]{:S(2)}) %collective-permute-start.15) | collective-permute-done | bytes 524320 | tf_op jit(solution)/shard_map/ppermute | solution.py:25
  21.3 2.0 %collective-permute-start.1 = (bf16[128,512]{1,0:T(8,128)(2,1)S(1)}, bf16[128,512]{1,0:T(8,128)(2,1)S(1)}, u32[]{:S(2)}, u32[]{:S(2)}) collective-permute-start(bf16[128,512]{1,0:T(8,128)(2,1)S(1)} %get-tuple-element.25), channel_id=1, source_target_pairs={{0,4},{4,0},{8,12},{12,8},{1,5},{5,1},{9,13},{13,9},{2,6},{6,2},{1... | collective-permute-start | bytes 393224 | tf_op jit(solution)/shard_map/ppermute | solution.py:25
  23.2 10.2 %collective-permute-done.17.refs_12_.refs_13_ = bf16[2,256,512]{2,1,0:T(8,128)(2,1)S(1)} collective-permute-done((bf16[2,256,512]{2,1,0:T(8,128)(2,1)S(1)}, bf16[2,256,512]{2,1,0:T(8,128)(2,1)S(1)}, u32[]{:S(2)}, u32[]{:S(2)}) %collective-permute-start.17) | collective-permute-done | bytes 524320 | tf_op jit(solution)/shard_map/ppermute | solution.py:25
  33.5 1.8 %collective-permute-start.2 = (bf16[128,512]{1,0:T(8,128)(2,1)S(1)}, bf16[128,512]{1,0:T(8,128)(2,1)S(1)}, u32[]{:S(2)}, u32[]{:S(2)}) collective-permute-start(bf16[128,512]{1,0:T(8,128)(2,1)S(1)} %get-tuple-element.26), channel_id=1, source_target_pairs={{0,8},{4,12},{8,0},{12,4},{1,9},{5,13},{9,1},{13,5},{2,10},{6,14},... | collective-permute-start | bytes 393224 | tf_op jit(solution)/shard_map/ppermute | solution.py:25
  35.3 0.2 collective-permute-start.3
  35.4 1.1 %shard_map.80 = (bf16[128,512]{1,0:T(8,128)(2,1)S(1)}, bf16[128,512]{1,0:T(8,128)(2,1)S(1)}, bf16[128,512]{1,0:T(8,128)(2,1)S(1)}) custom-call(s32[3]{0:T(128)S(1)} %pad_add_fusion.place_ref, bf16[1024,1024]{1,0:T(8,128)(2,1)S(1)} %copy-done, bf16[2,512,256]{2,1,0:T(8,128)(2,1)S(1)} %copy-done.1, bf16[2,512,256]{2,1,0:T(8,128)(2,1)S(1)} %collective-permute-done.refs_1_), custom_call_target="tpu_custom_call" | custom-call | tf_op jit(solution)/shard_map/pallas_call | solution.py:35
  36.6 1.6 %collective-permute-start.21 = (bf16[128,512]{1,0:T(8,128)(2,1)S(1)}, bf16[128,512]{1,0:T(8,128)(2,1)S(1)}, u32[]{:S(2)}, u32[]{:S(2)}) collective-permute-start(bf16[128,512]{1,0:T(8,128)(2,1)S(1)} %get-tuple-element.36), channel_id=1, source_target_pairs={{0,4},{4,0},{8,12},{12,8},{1,5},{5,1},{9,13},{13,9},{2,6},{6,2},{1... | collective-permute-start | bytes 393224 | tf_op jit(solution)/shard_map/ppermute | solution.py:25
  38.2 2.2 %collective-permute-done.2.refs_2_ = bf16[128,512]{1,0:T(8,128)(2,1)S(1)} collective-permute-done((bf16[128,512]{1,0:T(8,128)(2,1)S(1)}, bf16[128,512]{1,0:T(8,128)(2,1)S(1)}, u32[]{:S(2)}, u32[]{:S(2)}) %collective-permute-start.2) | collective-permute-done | bytes 131104 | tf_op jit(solution)/shard_map/ppermute | solution.py:25
  40.4 2.4 %collective-permute-start.22 = (bf16[128,512]{1,0:T(8,128)(2,1)S(1)}, bf16[128,512]{1,0:T(8,128)(2,1)S(1)}, u32[]{:S(2)}, u32[]{:S(2)}) collective-permute-start(bf16[128,512]{1,0:T(8,128)(2,1)S(1)} %get-tuple-element.37), channel_id=1, source_target_pairs={{0,8},{4,12},{8,0},{12,4},{1,9},{5,13},{9,1},{13,5},{2,10},{6,14},... | collective-permute-start | bytes 393224 | tf_op jit(solution)/shard_map/ppermute | solution.py:25
  42.8 0.5 collective-permute-start.20
  43.4 1.3 %collective-permute-start.23 = (bf16[128,512]{1,0:T(8,128)(2,1)S(1)}, bf16[128,512]{1,0:T(8,128)(2,1)S(1)}, u32[]{:S(2)}, u32[]{:S(2)}) collective-permute-start(bf16[128,512]{1,0:T(8,128)(2,1)S(1)} %get-tuple-element.38), channel_id=1, source_target_pairs={{0,12},{4,8},{8,4},{12,0},{1,13},{5,9},{9,5},{13,1},{2,14},{6,10},... | collective-permute-start | bytes 393224 | tf_op jit(solution)/shard_map/ppermute | solution.py:25
  44.7 1.1 %shard_map.73 = (bf16[128,512]{1,0:T(8,128)(2,1)S(1)}, bf16[128,512]{1,0:T(8,128)(2,1)S(1)}, f32[8,256]{1,0:T(8,128)S(1)}) custom-call(s32[3]{0:T(128)S(1)} %pad_add_fusion.place_ref, bf16[1024,1024]{1,0:T(8,128)(2,1)S(1)} %copy-done, bf16[2,512,256]{2,1,0:T(8,128)(2,1)S(1)} %copy-done.1, bf16[2,512,256]{2,1,0:T(8,128)(2,1)S(1)} %collective-permute-done.refs_1_, ...), custom_call_target="tpu_custom_call" | custom-call | tf_op jit(solution)/shard_map/pallas_call | solution.py:35
  45.8 0.8 shard_map.75
  46.7 1.5 %collective-permute-done.22.refs_2_ = bf16[128,512]{1,0:T(8,128)(2,1)S(1)} collective-permute-done((bf16[128,512]{1,0:T(8,128)(2,1)S(1)}, bf16[128,512]{1,0:T(8,128)(2,1)S(1)}, u32[]{:S(2)}, u32[]{:S(2)}) %collective-permute-start.22) | collective-permute-done | bytes 131104 | tf_op jit(solution)/shard_map/ppermute | solution.py:25
  48.1 1.6 %collective-permute-start.4 = (bf16[40,1024]{1,0:T(8,128)(2,1)S(1)}, bf16[40,1024]{1,0:T(8,128)(2,1)S(1)}, u32[]{:S(2)}, u32[]{:S(2)}) collective-permute-start(bf16[40,1024]{1,0:T(8,128)(2,1)S(1)} %get-tuple-element.30), channel_id=1, source_target_pairs={{0,1},{1,0},{2,3},{3,2},{4,5},{5,4},{6,7},{7,6},{8,9},{9,8},{10,11... | collective-permute-start | bytes 245768 | tf_op jit(solution)/shard_map/ppermute | solution.py:25
  49.7 2.6 %collective-permute-start.5 = (bf16[40,1024]{1,0:T(8,128)(2,1)S(1)}, bf16[40,1024]{1,0:T(8,128)(2,1)S(1)}, u32[]{:S(2)}, u32[]{:S(2)}) collective-permute-start(bf16[40,1024]{1,0:T(8,128)(2,1)S(1)} %get-tuple-element.31), channel_id=1, source_target_pairs={{0,2},{1,3},{2,0},{3,1},{4,6},{5,7},{6,4},{7,5},{8,10},{9,11},{10,... | collective-permute-start | bytes 245768 | tf_op jit(solution)/shard_map/ppermute | solution.py:25
  52.3 1.1 %collective-permute-done.4.refs_1_ = bf16[40,1024]{1,0:T(8,128)(2,1)S(1)} collective-permute-done((bf16[40,1024]{1,0:T(8,128)(2,1)S(1)}, bf16[40,1024]{1,0:T(8,128)(2,1)S(1)}, u32[]{:S(2)}, u32[]{:S(2)}) %collective-permute-start.4) | collective-permute-done | bytes 81952 | tf_op jit(solution)/shard_map/ppermute | solution.py:25
  53.4 2.7 %collective-permute-start.6 = (bf16[40,1024]{1,0:T(8,128)(2,1)S(1)}, bf16[40,1024]{1,0:T(8,128)(2,1)S(1)}, u32[]{:S(2)}, u32[]{:S(2)}) collective-permute-start(bf16[40,1024]{1,0:T(8,128)(2,1)S(1)} %get-tuple-element.32), channel_id=1, source_target_pairs={{0,3},{1,2},{2,1},{3,0},{4,7},{5,6},{6,5},{7,4},{8,11},{9,10},{10,... | collective-permute-start | bytes 245768 | tf_op jit(solution)/shard_map/ppermute | solution.py:25
  56.2 0.8 shard_map.81
  57.0 0.7 collective-permute-done.5.refs_2_
  57.8 2.0 %collective-permute-done.6.refs_3_ = bf16[40,1024]{1,0:T(8,128)(2,1)S(1)} collective-permute-done((bf16[40,1024]{1,0:T(8,128)(2,1)S(1)}, bf16[40,1024]{1,0:T(8,128)(2,1)S(1)}, u32[]{:S(2)}, u32[]{:S(2)}) %collective-permute-start.6) | collective-permute-done | bytes 81952 | tf_op jit(solution)/shard_map/ppermute | solution.py:25
  59.8 2.1 %collective-permute-start.25 = (bf16[32,1024]{1,0:T(8,128)(2,1)S(1)}, bf16[32,1024]{1,0:T(8,128)(2,1)S(1)}, u32[]{:S(2)}, u32[]{:S(2)}) collective-permute-start(bf16[32,1024]{1,0:T(8,128)(2,1)S(1)} %get-tuple-element.41), channel_id=1, source_target_pairs={{0,2},{1,3},{2,0},{3,1},{4,6},{5,7},{6,4},{7,5},{8,10},{9,11},{10,... | collective-permute-start | bytes 196616 | tf_op jit(solution)/shard_map/ppermute | solution.py:25
  61.9 1.1 %shard_map.77 = (bf16[32,1024]{1,0:T(8,128)(2,1)S(1)}, f32[8,256]{1,0:T(8,128)S(1)}) custom-call(s32[3]{0:T(128)S(1)} %pad_add_fusion.place_ref, s32[4,1024]{1,0:T(4,128)S(1)} %bitcast.8, bf16[40,1024]{1,0:T(8,128)(2,1)S(1)} %get-tuple-element.29.refs_0_, bf16[40,1024]{1,0:T(8,128)(2,1)S(1)} %collective-permute-done.4.refs_1_, ...), custom_call_target="tpu_custom_call" | custom-call | tf_op jit(solution)/shard_map/pallas_call | solution.py:35
  63.0 2.1 %collective-permute-start.26 = (bf16[32,1024]{1,0:T(8,128)(2,1)S(1)}, bf16[32,1024]{1,0:T(8,128)(2,1)S(1)}, u32[]{:S(2)}, u32[]{:S(2)}) collective-permute-start(bf16[32,1024]{1,0:T(8,128)(2,1)S(1)} %get-tuple-element.42), channel_id=1, source_target_pairs={{0,3},{1,2},{2,1},{3,0},{4,7},{5,6},{6,5},{7,4},{8,11},{9,10},{10,... | collective-permute-start | bytes 196616 | tf_op jit(solution)/shard_map/ppermute | solution.py:25
  65.1 0.7 collective-permute-done.25.refs_3_
  65.7 0.9 %collective-permute-start.11 = (bf16[32,1024]{1,0:T(8,128)(2,1)S(1)}, bf16[32,1024]{1,0:T(8,128)(2,1)S(1)}, u32[]{:S(2)}, u32[]{:S(2)}) collective-permute-start(bf16[32,1024]{1,0:T(8,128)(2,1)S(1)} %get-tuple-element.34.refs_4_), channel_id=1, source_target_pairs={{0,1},{1,0},{2,3},{3,2},{4,5},{5,4},{6,7},{7,6},{8,9},{9,8},{10,11... | collective-permute-start | bytes 196616 | tf_op jit(solution)/shard_map/ppermute | solution.py:25
  66.6 2.6 %collective-permute-done.26.refs_4_ = bf16[32,1024]{1,0:T(8,128)(2,1)S(1)} collective-permute-done((bf16[32,1024]{1,0:T(8,128)(2,1)S(1)}, bf16[32,1024]{1,0:T(8,128)(2,1)S(1)}, u32[]{:S(2)}, u32[]{:S(2)}) %collective-permute-start.26) | collective-permute-done | bytes 65568 | tf_op jit(solution)/shard_map/ppermute | solution.py:25
  69.2 0.9 collective-permute-start.12
  70.1 3.9 %collective-permute-start.13 = (bf16[32,1024]{1,0:T(8,128)(2,1)S(1)}, bf16[32,1024]{1,0:T(8,128)(2,1)S(1)}, u32[]{:S(2)}, u32[]{:S(2)}) collective-permute-start(bf16[32,1024]{1,0:T(8,128)(2,1)S(1)} %get-tuple-element.34.refs_4_), channel_id=1, source_target_pairs={{0,3},{1,2},{2,1},{3,0},{4,7},{5,6},{6,5},{7,4},{8,11},{9,10},{10,... | collective-permute-start | bytes 196616 | tf_op jit(solution)/shard_map/ppermute | solution.py:25
  74.0 1.1 %shard_map.82.refs_5_ = bf16[32,1024]{1,0:T(8,128)(2,1)S(1)} custom-call(s32[3]{0:T(128)S(1)} %pad_add_fusion.place_ref, s32[4,1024]{1,0:T(4,128)S(1)} %bitcast.9, f32[8,256]{1,0:T(8,128)S(1)} %get-tuple-element.33.refs_3_.refs_0_.refs_4_, bf16[32,1024]{1,0:T(8,128)(2,1)S(1)} %get-tuple-element.39.refs_1_, ...), custom_call_target="tpu_custom_call" | custom-call | tf_op jit(solution)/shard_map/pallas_call | solution.py:35
  75.2 1.2 %collective-permute-done.13.refs_7_ = bf16[32,1024]{1,0:T(8,128)(2,1)S(1)} collective-permute-done((bf16[32,1024]{1,0:T(8,128)(2,1)S(1)}, bf16[32,1024]{1,0:T(8,128)(2,1)S(1)}, u32[]{:S(2)}, u32[]{:S(2)}) %collective-permute-start.13) | collective-permute-done | bytes 65568 | tf_op jit(solution)/shard_map/ppermute | solution.py:25
  76.3 1.2 %collective-permute-start.28 = (bf16[32,1024]{1,0:T(8,128)(2,1)S(1)}, bf16[32,1024]{1,0:T(8,128)(2,1)S(1)}, u32[]{:S(2)}, u32[]{:S(2)}) collective-permute-start(bf16[32,1024]{1,0:T(8,128)(2,1)S(1)} %shard_map.82.refs_5_), channel_id=1, source_target_pairs={{0,2},{1,3},{2,0},{3,1},{4,6},{5,7},{6,4},{7,5},{8,10},{9,11},{10,... | collective-permute-start | bytes 196616 | tf_op jit(solution)/shard_map/ppermute | solution.py:25
  77.5 3.0 %collective-permute-start.29 = (bf16[32,1024]{1,0:T(8,128)(2,1)S(1)}, bf16[32,1024]{1,0:T(8,128)(2,1)S(1)}, u32[]{:S(2)}, u32[]{:S(2)}) collective-permute-start(bf16[32,1024]{1,0:T(8,128)(2,1)S(1)} %shard_map.82.refs_5_), channel_id=1, source_target_pairs={{0,3},{1,2},{2,1},{3,0},{4,7},{5,6},{6,5},{7,4},{8,11},{9,10},{10,... | collective-permute-start | bytes 196616 | tf_op jit(solution)/shard_map/ppermute | solution.py:25
  80.5 2.2 %shard_map.79.refs_0_ = bf16[256,1024]{1,0:T(8,128)(2,1)} custom-call(s32[3]{0:T(128)S(1)} %pad_add_fusion.place_ref, bf16[1024,1024]{1,0:T(8,128)(2,1)S(1)} %copy-done, s32[4,1024]{1,0:T(4,128)S(1)} %bitcast.10, f32[1,1024]{1,0:T(1,128)S(1)} %bitcast.13, f32[8,256]{1,0:T(8,128)S(1)} %get-tuple-element.33.refs_3_.refs_0_.refs_4_, ...), custom_call_target="tpu_custom_call" | custom-call | tf_op jit(solution)/shard_map/pallas_call | solution.py:35
  82.8 0.8 collective-permute-done.29.refs_8_
  83.6 2.2 %shard_map.83 = bf16[256,1024]{1,0:T(8,128)(2,1)} custom-call(s32[3]{0:T(128)S(1)} %pad_add_fusion.place_ref, bf16[256,1024]{1,0:T(8,128)(2,1)} %shard_map.79.refs_0_, bf16[1024,1024]{1,0:T(8,128)(2,1)S(1)} %copy-done, s32[4,1024]{1,0:T(4,128)S(1)} %bitcast.11, f32[1,1024]{1,0:T(1,128)S(1)} %bitcast.14, ...), custom_call_target="tpu_custom_call", output_to_operand_aliasing={{}: (1, {})} | custom-call | tf_op jit(solution)/shard_map/pallas_call | solution.py:35
  (38 shorter events, 0.2 us)
Async XLA Ops:
  0.0 8.4 %collective-permute-start.7 = (bf16[2,128,256]{2,1,0:T(8,128)(2,1)}, bf16[2,128,256]{2,1,0:T(8,128)(2,1)S(1)}, u32[]{:S(2)}, u32[]{:S(2)}) collective-permute-start(bf16[2,128,256]{2,1,0:T(8,128)(2,1)} %refs_0_.7), channel_id=1, source_target_pairs={{0,4},{4,0},{8,12},{12,8},{1,5},{5,1},{9,13},{13,9},{2,6},{6,2},{1... | collective-permute-start | bytes 393224 | tf_op jit(solution)/shard_map/ppermute | solution.py:25
  3.0 8.0 %collective-permute-start.8 = (bf16[2,128,256]{2,1,0:T(8,128)(2,1)}, bf16[2,128,256]{2,1,0:T(8,128)(2,1)S(1)}, u32[]{:S(2)}, u32[]{:S(2)}) collective-permute-start(bf16[2,128,256]{2,1,0:T(8,128)(2,1)} %refs_0_.7), channel_id=1, source_target_pairs={{0,8},{4,12},{8,0},{12,4},{1,9},{5,13},{9,1},{13,5},{2,10},{6,14},... | collective-permute-start | bytes 393224 | tf_op jit(solution)/shard_map/ppermute | solution.py:25
  4.5 8.0 %collective-permute-start.9 = (bf16[2,128,256]{2,1,0:T(8,128)(2,1)}, bf16[2,128,256]{2,1,0:T(8,128)(2,1)S(1)}, u32[]{:S(2)}, u32[]{:S(2)}) collective-permute-start(bf16[2,128,256]{2,1,0:T(8,128)(2,1)} %refs_0_.7), channel_id=1, source_target_pairs={{0,12},{4,8},{8,4},{12,0},{1,13},{5,9},{9,5},{13,1},{2,14},{6,10},... | collective-permute-start | bytes 393224 | tf_op jit(solution)/shard_map/ppermute | solution.py:25
  4.5 8.7 %collective-permute-start = (bf16[2,512,256]{2,1,0:T(8,128)(2,1)}, bf16[2,512,256]{2,1,0:T(8,128)(2,1)S(1)}, u32[]{:S(2)}, u32[]{:S(2)}) collective-permute-start(bf16[2,512,256]{2,1,0:T(8,128)(2,1)} %refs_0_.9), channel_id=1, source_target_pairs={{0,16},{16,0},{1,17},{17,1},{2,18},{18,2},{3,19},{19,3},{4,20},{20... | collective-permute-start | bytes 1572872 | tf_op jit(solution)/shard_map/ppermute | solution.py:329
  4.6 1.0 %copy-start.6 = (bf16[2,512,256]{2,1,0:T(8,128)(2,1)S(1)}, bf16[2,512,256]{2,1,0:T(8,128)(2,1)}, u32[]{:S(2)}) copy-start(bf16[2,512,256]{2,1,0:T(8,128)(2,1)} %w_ref.1) | copy-start | bytes 1572868
  5.6 6.8 %copy-start.3 = (bf16[2,128,256]{2,1,0:T(8,128)(2,1)S(1)}, bf16[2,128,256]{2,1,0:T(8,128)(2,1)}, u32[]{:S(2)}) copy-start(bf16[2,128,256]{2,1,0:T(8,128)(2,1)} %refs_0_.7) | copy-start | bytes 393220
  5.6 8.1 %copy-start = (bf16[1024,1024]{1,0:T(8,128)(2,1)S(1)}, bf16[1024,1024]{1,0:T(8,128)(2,1)}, u32[]{:S(2)}) copy-start(bf16[1024,1024]{1,0:T(8,128)(2,1)} %refs_1_.1) | copy-start | bytes 6291460
  5.6 8.1 %copy-start.1 = (bf16[2,512,256]{2,1,0:T(8,128)(2,1)S(1)}, bf16[2,512,256]{2,1,0:T(8,128)(2,1)}, u32[]{:S(2)}) copy-start(bf16[2,512,256]{2,1,0:T(8,128)(2,1)} %refs_0_.9) | copy-start | bytes 1572868
  6.4 14.9 %collective-permute-start.15 = (bf16[2,256,512]{2,1,0:T(8,128)(2,1)S(1)}, bf16[2,256,512]{2,1,0:T(8,128)(2,1)S(1)}, u32[]{:S(2)}, u32[]{:S(2)}) collective-permute-start(bf16[2,256,512]{2,1,0:T(8,128)(2,1)S(1)} %shard_map.78.refs_8_.refs_9_), channel_id=1, source_target_pairs={{0,4},{4,0},{8,12},{12,8},{1,5},{5,1},{9,13},{13,9},{2,6},{6,2},{1... | collective-permute-start | bytes 1572872 | tf_op jit(solution)/shard_map/ppermute | solution.py:25
  8.4 25.0 %collective-permute-start.17 = (bf16[2,256,512]{2,1,0:T(8,128)(2,1)S(1)}, bf16[2,256,512]{2,1,0:T(8,128)(2,1)S(1)}, u32[]{:S(2)}, u32[]{:S(2)}) collective-permute-start(bf16[2,256,512]{2,1,0:T(8,128)(2,1)S(1)} %shard_map.78.refs_8_.refs_9_), channel_id=1, source_target_pairs={{0,8},{4,12},{8,0},{12,4},{1,9},{5,13},{9,1},{13,5},{2,10},{6,14},... | collective-permute-start | bytes 1572872 | tf_op jit(solution)/shard_map/ppermute | solution.py:25
  11.0 24.3 %collective-permute-start.19 = (bf16[2,256,512]{2,1,0:T(8,128)(2,1)S(1)}, bf16[2,256,512]{2,1,0:T(8,128)(2,1)S(1)}, u32[]{:S(2)}, u32[]{:S(2)}) collective-permute-start(bf16[2,256,512]{2,1,0:T(8,128)(2,1)S(1)} %shard_map.78.refs_8_.refs_9_), channel_id=1, source_target_pairs={{0,12},{4,8},{8,4},{12,0},{1,13},{5,9},{9,5},{13,1},{2,14},{6,10},... | collective-permute-start | bytes 1572872 | tf_op jit(solution)/shard_map/ppermute | solution.py:25
  12.4 24.1 %collective-permute-start.14 = (bf16[2,256,512]{2,1,0:T(8,128)(2,1)S(1)}, bf16[2,256,512]{2,1,0:T(8,128)(2,1)S(1)}, u32[]{:S(2)}, u32[]{:S(2)}) collective-permute-start(bf16[2,256,512]{2,1,0:T(8,128)(2,1)S(1)} %shard_map.78.refs_8_.refs_9_), channel_id=1, source_target_pairs={{0,16},{16,0},{1,17},{17,1},{2,18},{18,2},{3,19},{19,3},{4,20},{20... | collective-permute-start | bytes 1572872 | tf_op jit(solution)/shard_map/ppermute | solution.py:329
  13.2 29.7 %collective-permute-start.10 = (bf16[8,256,128]{2,1,0:T(8,128)(2,1)S(1)}, bf16[8,256,128]{2,1,0:T(8,128)(2,1)S(1)}, u32[]{:S(2)}, u32[]{:S(2)}) collective-permute-start(bf16[8,256,128]{2,1,0:T(8,128)(2,1)S(1)} %shard_map.76.refs_4_.refs_5_), channel_id=1, source_target_pairs={{0,16},{16,0},{1,17},{17,1},{2,18},{18,2},{3,19},{19,3},{4,20},{20... | collective-permute-start | bytes 1572872 | tf_op jit(solution)/shard_map/ppermute | solution.py:329
  14.9 29.8 %copy-start.4 = (bf16[1024,8]{0,1:T(8,128)(2,1)S(1)}, bf16[1024,8]{0,1:T(8,128)(2,1)}, u32[]{:S(2)}) copy-start(bf16[1024,8]{0,1:T(8,128)(2,1)} %param.9) | copy-start | bytes 49156
  21.3 16.9 %collective-permute-start.1 = (bf16[128,512]{1,0:T(8,128)(2,1)S(1)}, bf16[128,512]{1,0:T(8,128)(2,1)S(1)}, u32[]{:S(2)}, u32[]{:S(2)}) collective-permute-start(bf16[128,512]{1,0:T(8,128)(2,1)S(1)} %get-tuple-element.25), channel_id=1, source_target_pairs={{0,4},{4,0},{8,12},{12,8},{1,5},{5,1},{9,13},{13,9},{2,6},{6,2},{1... | collective-permute-start | bytes 393224 | tf_op jit(solution)/shard_map/ppermute | solution.py:25
  33.5 6.9 %collective-permute-start.2 = (bf16[128,512]{1,0:T(8,128)(2,1)S(1)}, bf16[128,512]{1,0:T(8,128)(2,1)S(1)}, u32[]{:S(2)}, u32[]{:S(2)}) collective-permute-start(bf16[128,512]{1,0:T(8,128)(2,1)S(1)} %get-tuple-element.26), channel_id=1, source_target_pairs={{0,8},{4,12},{8,0},{12,4},{1,9},{5,13},{9,1},{13,5},{2,10},{6,14},... | collective-permute-start | bytes 393224 | tf_op jit(solution)/shard_map/ppermute | solution.py:25
  35.3 7.6 %collective-permute-start.3 = (bf16[128,512]{1,0:T(8,128)(2,1)S(1)}, bf16[128,512]{1,0:T(8,128)(2,1)S(1)}, u32[]{:S(2)}, u32[]{:S(2)}) collective-permute-start(bf16[128,512]{1,0:T(8,128)(2,1)S(1)} %get-tuple-element.27), channel_id=1, source_target_pairs={{0,12},{4,8},{8,4},{12,0},{1,13},{5,9},{9,5},{13,1},{2,14},{6,10},... | collective-permute-start | bytes 393224 | tf_op jit(solution)/shard_map/ppermute | solution.py:25
  36.6 9.2 %copy-start.2 = (s32[1024,4]{0,1:T(4,128)S(1)}, s32[1024,4]{0,1:T(4,128)}, u32[]{:S(2)}) copy-start(s32[1024,4]{0,1:T(4,128)} %param.8) | copy-start | bytes 49156
  36.6 6.8 %collective-permute-start.21 = (bf16[128,512]{1,0:T(8,128)(2,1)S(1)}, bf16[128,512]{1,0:T(8,128)(2,1)S(1)}, u32[]{:S(2)}, u32[]{:S(2)}) collective-permute-start(bf16[128,512]{1,0:T(8,128)(2,1)S(1)} %get-tuple-element.36), channel_id=1, source_target_pairs={{0,4},{4,0},{8,12},{12,8},{1,5},{5,1},{9,13},{13,9},{2,6},{6,2},{1... | collective-permute-start | bytes 393224 | tf_op jit(solution)/shard_map/ppermute | solution.py:25
  38.2 39.3 %collective-permute-start.16 = (bf16[2,256,512]{2,1,0:T(8,128)(2,1)S(1)}, bf16[2,256,512]{2,1,0:T(8,128)(2,1)S(1)}, u32[]{:S(2)}, u32[]{:S(2)}) collective-permute-start(bf16[2,256,512]{2,1,0:T(8,128)(2,1)S(1)} %collective-permute-done.15.refs_10_.refs_11_), channel_id=1, source_target_pairs={{0,16},{16,0},{1,17},{17,1},{2,18},{18,2},{3,19},{19,3},{4,20},{20... | collective-permute-start | bytes 1572872 | tf_op jit(solution)/shard_map/ppermute | solution.py:329
  40.4 7.7 %collective-permute-start.22 = (bf16[128,512]{1,0:T(8,128)(2,1)S(1)}, bf16[128,512]{1,0:T(8,128)(2,1)S(1)}, u32[]{:S(2)}, u32[]{:S(2)}) collective-permute-start(bf16[128,512]{1,0:T(8,128)(2,1)S(1)} %get-tuple-element.37), channel_id=1, source_target_pairs={{0,8},{4,12},{8,0},{12,4},{1,9},{5,13},{9,1},{13,5},{2,10},{6,14},... | collective-permute-start | bytes 393224 | tf_op jit(solution)/shard_map/ppermute | solution.py:25
  42.8 37.7 %collective-permute-start.18 = (bf16[2,256,512]{2,1,0:T(8,128)(2,1)S(1)}, bf16[2,256,512]{2,1,0:T(8,128)(2,1)S(1)}, u32[]{:S(2)}, u32[]{:S(2)}) collective-permute-start(bf16[2,256,512]{2,1,0:T(8,128)(2,1)S(1)} %collective-permute-done.17.refs_12_.refs_13_), channel_id=1, source_target_pairs={{0,16},{16,0},{1,17},{17,1},{2,18},{18,2},{3,19},{19,3},{4,20},{20... | collective-permute-start | bytes 1572872 | tf_op jit(solution)/shard_map/ppermute | solution.py:329
  42.8 37.7 %collective-permute-start.20 = (bf16[2,256,512]{2,1,0:T(8,128)(2,1)S(1)}, bf16[2,256,512]{2,1,0:T(8,128)(2,1)S(1)}, u32[]{:S(2)}, u32[]{:S(2)}) collective-permute-start(bf16[2,256,512]{2,1,0:T(8,128)(2,1)S(1)} %collective-permute-done.19.refs_14_.refs_15_), channel_id=1, source_target_pairs={{0,16},{16,0},{1,17},{17,1},{2,18},{18,2},{3,19},{19,3},{4,20},{20... | collective-permute-start | bytes 1572872 | tf_op jit(solution)/shard_map/ppermute | solution.py:329
  43.4 6.4 %collective-permute-start.23 = (bf16[128,512]{1,0:T(8,128)(2,1)S(1)}, bf16[128,512]{1,0:T(8,128)(2,1)S(1)}, u32[]{:S(2)}, u32[]{:S(2)}) collective-permute-start(bf16[128,512]{1,0:T(8,128)(2,1)S(1)} %get-tuple-element.38), channel_id=1, source_target_pairs={{0,12},{4,8},{8,4},{12,0},{1,13},{5,9},{9,5},{13,1},{2,14},{6,10},... | collective-permute-start | bytes 393224 | tf_op jit(solution)/shard_map/ppermute | solution.py:25
  45.8 34.7 %copy-start.5 = (f32[1024]{0:T(1024)S(1)}, f32[1024]{0:T(1024)}, u32[]{:S(2)}) copy-start(f32[1024]{0:T(1024)} %param.13) | copy-start | bytes 12292
  48.1 5.3 %collective-permute-start.4 = (bf16[40,1024]{1,0:T(8,128)(2,1)S(1)}, bf16[40,1024]{1,0:T(8,128)(2,1)S(1)}, u32[]{:S(2)}, u32[]{:S(2)}) collective-permute-start(bf16[40,1024]{1,0:T(8,128)(2,1)S(1)} %get-tuple-element.30), channel_id=1, source_target_pairs={{0,1},{1,0},{2,3},{3,2},{4,5},{5,4},{6,7},{7,6},{8,9},{9,8},{10,11... | collective-permute-start | bytes 245768 | tf_op jit(solution)/shard_map/ppermute | solution.py:25
  49.7 8.0 %collective-permute-start.5 = (bf16[40,1024]{1,0:T(8,128)(2,1)S(1)}, bf16[40,1024]{1,0:T(8,128)(2,1)S(1)}, u32[]{:S(2)}, u32[]{:S(2)}) collective-permute-start(bf16[40,1024]{1,0:T(8,128)(2,1)S(1)} %get-tuple-element.31), channel_id=1, source_target_pairs={{0,2},{1,3},{2,0},{3,1},{4,6},{5,7},{6,4},{7,5},{8,10},{9,11},{10,... | collective-permute-start | bytes 245768 | tf_op jit(solution)/shard_map/ppermute | solution.py:25
  53.4 6.3 %collective-permute-start.6 = (bf16[40,1024]{1,0:T(8,128)(2,1)S(1)}, bf16[40,1024]{1,0:T(8,128)(2,1)S(1)}, u32[]{:S(2)}, u32[]{:S(2)}) collective-permute-start(bf16[40,1024]{1,0:T(8,128)(2,1)S(1)} %get-tuple-element.32), channel_id=1, source_target_pairs={{0,3},{1,2},{2,1},{3,0},{4,7},{5,6},{6,5},{7,4},{8,11},{9,10},{10,... | collective-permute-start | bytes 245768 | tf_op jit(solution)/shard_map/ppermute | solution.py:25
  57.7 5.3 %collective-permute-start.24 = (bf16[32,1024]{1,0:T(8,128)(2,1)S(1)}, bf16[32,1024]{1,0:T(8,128)(2,1)S(1)}, u32[]{:S(2)}, u32[]{:S(2)}) collective-permute-start(bf16[32,1024]{1,0:T(8,128)(2,1)S(1)} %get-tuple-element.40), channel_id=1, source_target_pairs={{0,1},{1,0},{2,3},{3,2},{4,5},{5,4},{6,7},{7,6},{8,9},{9,8},{10,11... | collective-permute-start | bytes 196616 | tf_op jit(solution)/shard_map/ppermute | solution.py:25
  59.8 6.0 %collective-permute-start.25 = (bf16[32,1024]{1,0:T(8,128)(2,1)S(1)}, bf16[32,1024]{1,0:T(8,128)(2,1)S(1)}, u32[]{:S(2)}, u32[]{:S(2)}) collective-permute-start(bf16[32,1024]{1,0:T(8,128)(2,1)S(1)} %get-tuple-element.41), channel_id=1, source_target_pairs={{0,2},{1,3},{2,0},{3,1},{4,6},{5,7},{6,4},{7,5},{8,10},{9,11},{10,... | collective-permute-start | bytes 196616 | tf_op jit(solution)/shard_map/ppermute | solution.py:25
  63.0 6.2 %collective-permute-start.26 = (bf16[32,1024]{1,0:T(8,128)(2,1)S(1)}, bf16[32,1024]{1,0:T(8,128)(2,1)S(1)}, u32[]{:S(2)}, u32[]{:S(2)}) collective-permute-start(bf16[32,1024]{1,0:T(8,128)(2,1)S(1)} %get-tuple-element.42), channel_id=1, source_target_pairs={{0,3},{1,2},{2,1},{3,0},{4,7},{5,6},{6,5},{7,4},{8,11},{9,10},{10,... | collective-permute-start | bytes 196616 | tf_op jit(solution)/shard_map/ppermute | solution.py:25
  65.7 4.3 %collective-permute-start.11 = (bf16[32,1024]{1,0:T(8,128)(2,1)S(1)}, bf16[32,1024]{1,0:T(8,128)(2,1)S(1)}, u32[]{:S(2)}, u32[]{:S(2)}) collective-permute-start(bf16[32,1024]{1,0:T(8,128)(2,1)S(1)} %get-tuple-element.34.refs_4_), channel_id=1, source_target_pairs={{0,1},{1,0},{2,3},{3,2},{4,5},{5,4},{6,7},{7,6},{8,9},{9,8},{10,11... | collective-permute-start | bytes 196616 | tf_op jit(solution)/shard_map/ppermute | solution.py:25
  69.2 5.9 %collective-permute-start.12 = (bf16[32,1024]{1,0:T(8,128)(2,1)S(1)}, bf16[32,1024]{1,0:T(8,128)(2,1)S(1)}, u32[]{:S(2)}, u32[]{:S(2)}) collective-permute-start(bf16[32,1024]{1,0:T(8,128)(2,1)S(1)} %get-tuple-element.34.refs_4_), channel_id=1, source_target_pairs={{0,2},{1,3},{2,0},{3,1},{4,6},{5,7},{6,4},{7,5},{8,10},{9,11},{10,... | collective-permute-start | bytes 196616 | tf_op jit(solution)/shard_map/ppermute | solution.py:25
  70.1 6.3 %collective-permute-start.13 = (bf16[32,1024]{1,0:T(8,128)(2,1)S(1)}, bf16[32,1024]{1,0:T(8,128)(2,1)S(1)}, u32[]{:S(2)}, u32[]{:S(2)}) collective-permute-start(bf16[32,1024]{1,0:T(8,128)(2,1)S(1)} %get-tuple-element.34.refs_4_), channel_id=1, source_target_pairs={{0,3},{1,2},{2,1},{3,0},{4,7},{5,6},{6,5},{7,4},{8,11},{9,10},{10,... | collective-permute-start | bytes 196616 | tf_op jit(solution)/shard_map/ppermute | solution.py:25
  75.1 7.7 %collective-permute-start.27 = (bf16[32,1024]{1,0:T(8,128)(2,1)S(1)}, bf16[32,1024]{1,0:T(8,128)(2,1)S(1)}, u32[]{:S(2)}, u32[]{:S(2)}) collective-permute-start(bf16[32,1024]{1,0:T(8,128)(2,1)S(1)} %shard_map.82.refs_5_), channel_id=1, source_target_pairs={{0,1},{1,0},{2,3},{3,2},{4,5},{5,4},{6,7},{7,6},{8,9},{9,8},{10,11... | collective-permute-start | bytes 196616 | tf_op jit(solution)/shard_map/ppermute | solution.py:25
  76.3 6.4 %collective-permute-start.28 = (bf16[32,1024]{1,0:T(8,128)(2,1)S(1)}, bf16[32,1024]{1,0:T(8,128)(2,1)S(1)}, u32[]{:S(2)}, u32[]{:S(2)}) collective-permute-start(bf16[32,1024]{1,0:T(8,128)(2,1)S(1)} %shard_map.82.refs_5_), channel_id=1, source_target_pairs={{0,2},{1,3},{2,0},{3,1},{4,6},{5,7},{6,4},{7,5},{8,10},{9,11},{10,... | collective-permute-start | bytes 196616 | tf_op jit(solution)/shard_map/ppermute | solution.py:25
  77.5 6.1 %collective-permute-start.29 = (bf16[32,1024]{1,0:T(8,128)(2,1)S(1)}, bf16[32,1024]{1,0:T(8,128)(2,1)S(1)}, u32[]{:S(2)}, u32[]{:S(2)}) collective-permute-start(bf16[32,1024]{1,0:T(8,128)(2,1)S(1)} %shard_map.82.refs_5_), channel_id=1, source_target_pairs={{0,3},{1,2},{2,1},{3,0},{4,7},{5,6},{6,5},{7,4},{8,11},{9,10},{10,... | collective-permute-start | bytes 196616 | tf_op jit(solution)/shard_map/ppermute | solution.py:25

commit v2 on v1

--- a/solution.py
+++ b/solution.py
@@ -32,9 +32,13 @@
 def call(body, args, outs, scratch=(), limit=12, flops=None, held=(), alias=None):
     space = lambda k: pl.BlockSpec(memory_space=pl.ANY) if k in held else vmem()
     cost = None if flops is None else pl.CostEstimate(flops, 0, flops // 500)
+
+    def placed(*refs):
+        body([lax.axis_index(a) for a in ("batch", "expert", "dim")], *refs)
+
     return pl.pallas_call(
-        body,
-        in_specs=[pl.BlockSpec(memory_space=pltpu.SMEM)] + [space(k) for k in range(1, len(args))],
+        placed,
+        in_specs=[space(k) for k in range(len(args))],
         out_specs=[space("out") for _ in outs],
         out_shape=[jax.ShapeDtypeStruct(s, t) for s, t in outs],
         scratch_shapes=list(scratch),
@@ -54,62 +58,62 @@
     return jnp.concatenate([cols_t, pad], axis=0).T
 
 
-def project(place, x, pieces, row_starts, n_row, pair, gate_t=None):
+def begin():
+    def body(place_ref, out_ref):
+        out_ref[...] = jnp.zeros(out_ref.shape, jnp.int32)
+
+    return call(body, [], [((8, 128), jnp.int32)], flops=6_000_000_000)[0]
+
+
+def project(x, pieces, gate_t, begun, h, n_row, n_expert, pair):
     n_loc, width, rank = pieces[0].shape
     n_piece = len(pieces)
-    count = row_starts[1]
+    block = n_row * SPLIT
 
     def body(place_ref, x_ref, *refs):
-        w_refs, outs = refs[:n_piece], refs[n_piece:]
-        starts = row_starts[0](place_ref)
+        w_refs, g_ref = refs[:n_piece], refs[n_piece]
+        logit_ref, *outs = refs[n_piece + 2 :]
         first = [place_ref[0], 1 - place_ref[0]] if pair else [0]
+        starts = [
+            peer_to(place_ref[1], m, n_expert) * block + h * n_row for m in range(n_expert)
+        ]
         xs = []
         for p in range(n_piece):
             cols = rows_at(first[p] * width, width)
             xs.append(jnp.concatenate([x_ref[rows_at(s, n_row), cols] for s in starts], axis=0))
-        if gate_t is not None:
-            logit = None
-            for p in range(n_piece):
-                part = lax.dot_general(
-                    outs[0][:, rows_at(first[p] * width, width)], xs[p], LAST,
-                    preferred_element_type=F32,
-                )
-                logit = part if logit is None else logit + part
-            outs[-1][...] = logit
-            outs = outs[1:]
         for e in range(n_loc):
             acc = jnp.dot(xs[0], w_refs[0][e], preferred_element_type=F32)
             for p in range(1, n_piece):
                 acc = acc + jnp.dot(xs[p], w_refs[p][e], preferred_element_type=F32)
             acc = acc.astype(BF16)
-            for k in range(count):
-                outs[k][:, e * rank : (e + 1) * rank] = acc[k * n_row : (k + 1) * n_row]
-
-    args = [place, x, *pieces]
-    outs = [((n_row, n_loc * rank), BF16)] * count
-    if gate_t is not None:
-        args.append(gate_t)
-        outs = outs + [((gate_t.shape[0], n_row * count), F32)]
-    return call(body, args, outs)
-
-
-def widen(place, wide):
+            for m in range(n_expert):
+                outs[m][:, e * rank : (e + 1) * rank] = acc[m * n_row : (m + 1) * n_row]
+        logit = None
+        for p in range(n_piece):
+            gate = g_ref[:, rows_at(first[p] * width, width)]
+            part = lax.dot_general(gate, xs[p][:n_row], LAST, preferred_element_type=F32)
+            logit = part if logit is None else logit + part
+        logit_ref[...] = logit
+
+    return call(
+        body,
+        [x, *pieces, gate_t, begun],
+        [((gate_t.shape[0], n_row), F32)] + [((n_row, n_loc * rank), BF16)] * n_expert,
+        flops=3_000_000_000,
+    )
+
+
+def widen(wide):
     n_loc, half, rank = wide.shape
 
-    def body(place_ref, w_ref, out_ref, buf, sem):
-        copy = pltpu.make_async_copy(w_ref, buf, sem)
-        copy.start()
-        copy.wait()
+    def body(place_ref, w_ref, out_ref):
         for e in range(n_loc):
-            out_ref[e] = buf[e].T
-
-    return call(
-        body, [place, wide], [((n_loc, rank, half), BF16)],
-        [pltpu.VMEM(wide.shape, BF16), pltpu.SemaphoreType.DMA], flops=4_000_000_000, held=(1,),
-    )[0]
-
-
-def turn(place, mids):
+            out_ref[e] = w_ref[e].T
+
+    return call(body, [wide], [((n_loc, rank, half), BF16)])[0]
+
+
+def turn(mids):
     n_loc, half, rank = mids[0].shape
 
     def body(place_ref, *refs):
@@ -117,7 +121,7 @@
             for e in range(n_loc):
                 refs[-1][q * n_loc + e] = refs[q][e].T
 
-    return call(body, [place, *mids], [((len(mids) * n_loc, rank, half), BF16)])[0]
+    return call(body, [*mids], [((len(mids) * n_loc, rank, half), BF16)])[0]
 
 
 def wide_ids(ids_ref, start, n, width):
@@ -126,17 +130,18 @@
     return [jnp.broadcast_to(ids[:, j : j + 1], (n, width)).astype(BF16) for j in range(top)]
 
 
-def pack(place, ids_t, parts, at, n_expert, n_dim, n_loc, logit=None):
+def pack(ids_t, parts, at, n_expert, n_dim, n_loc, logits=()):
     rows, wide = parts[0].shape
     rank = wide // n_loc
     per = rows // n_dim
     top = ids_t.shape[0]
     n_part = len(parts)
-    more = 0 if logit is None else logit.shape[0]
+    n_log = len(logits)
+    more = logits[0].shape[0] if logits else 0
 
     def body(place_ref, ids_ref, *refs):
         p_refs, scratch = refs[:n_part], refs[-1]
-        outs = refs[n_part:-1] if logit is None else refs[n_part + 1 : -1]
+        l_refs, outs = refs[n_part : n_part + n_log], refs[n_part + n_log : -1]
         x_at, z_at = place_ref[1], place_ref[2]
         ids = wide_ids(ids_ref, x_at * (rows * SPLIT) + at * rows, rows, rank)
         for j in range(top):
@@ -151,8 +156,8 @@
             scratch[:, j * rank : (j + 1) * rank] = acc
         for m in range(n_dim):
             outs[m][:per, :] = scratch[rows_at(peer_to(z_at, m, n_dim) * per, per), :]
-        if logit is not None:
-            full = refs[n_part][...]
+        if logits:
+            full = jnp.concatenate([r[...] for r in l_refs], axis=1)
             n = full.shape[1]
             high = full.astype(BF16)
             low = (full - high.astype(F32)).astype(BF16)
@@ -163,13 +168,13 @@
 
     return call(
         body,
-        [place, ids_t, *parts] + ([] if logit is None else [logit]),
+        [ids_t, *parts, *logits],
         [((per + more, top * rank), BF16)] * n_dim,
         [pltpu.VMEM((rows, top * rank), BF16)],
     )
 
 
-def mix(place, ids_t, gates_t, parts, mids, at, block, n_expert, n_dim, pair):
+def mix(ids_t, gates_t, parts, mids, at, block, n_expert, n_dim, pair):
     wide = parts[0].shape[1]
     top, _ = ids_t.shape
     rank = wide // top
@@ -231,7 +236,7 @@
 
     return call(
         body,
-        [place, ids_t] + ([] if make else [gates_t]) + [*parts, *mids],
+        [ids_t] + ([] if make else [gates_t]) + [*parts, *mids],
         [((per, wide), BF16)] + ([((n_all, block), F32)] if make else []),
         [
             pltpu.VMEM((top * per, rank), BF16),
@@ -241,7 +246,7 @@
     )
 
 
-def expand(place, x, ids_t, bias, gates_t, hids, wides, at, so_far, n_expert, n_dim, n_loc, pair):
+def expand(x, ids_t, bias, gates_t, hids, wides, at, n_expert, n_dim, n_loc, pair):
     per, wide = hids[0].shape
     top, _ = ids_t.shape
     rank = wide // top
@@ -253,28 +258,28 @@
     half = wides[0][0].shape[2]
     flat_w = [w for src in wides for w in src]
     n_h, n_w = len(hids), len(flat_w)
-    n_first = 0 if so_far is None else 1
-
-    def body(place_ref, *refs):
-        refs = refs[n_first:]
-        x_ref, ids_ref, bias_ref, g_ref, *refs = refs
+    later = n_expert - n_src
+
+    def body(place_ref, ids_ref, bias_ref, g_ref, *refs):
         h_refs, w_refs = refs[:n_h], refs[n_h : n_h + n_w]
-        out_ref, hid, left, buf, sems = refs[n_h + n_w :]
+        out_ref, later_ref, hid, left = refs[n_h + n_w :]
         x_at, z_at = place_ref[1], place_ref[2]
         first = [place_ref[0], 1 - place_ref[0]] if pair else [0]
-        mine = rows_at(x_at * block + at * rows, rows)
         for m in range(n_dim):
             hid[rows_at(peer_from(z_at, m, n_dim) * per, per), :] = h_refs[m][...]
         ids = wide_ids(ids_ref, x_at * block + at * rows, rows, rank)
-        for q in range(n_src):
+        for q in range(n_expert):
             base = peer_from(x_at, q, n_expert) * n_loc
             for e in range(n_loc):
                 number = (base + e).astype(F32).astype(BF16)
                 acc = jnp.zeros((rows, rank), BF16)
                 for j in range(top):
                     acc = jnp.where(ids[j] == number, hid[:, j * rank : (j + 1) * rank], acc)
-                left[q * n_loc + e] = acc
-        own = ids_ref[:, mine]
+                if q < n_src:
+                    left[q * n_loc + e] = acc
+                else:
+                    later_ref[(q - n_src) * n_loc + e] = acc
+        own = ids_ref[:, rows_at(x_at * block + at * rows, rows)]
         gates = g_ref[:, at * rows : (at + 1) * rows]
         number = lax.broadcasted_iota(jnp.int32, gates.shape, 0)
         hit = own[0:1, :] == number
@@ -282,36 +287,49 @@
             hit = hit | (own[j : j + 1, :] == number)
         total = jnp.sum(jnp.where(hit, gates, 0.0), axis=0, keepdims=True)
         total = jnp.broadcast_to(total, gates.shape).T[:, 0:1]
-        copies = []
         for h in range(n_piece):
-            acc = jnp.zeros((rows, half), F32)
+            cols = rows_at(first[h] * half, half)
+            acc = total * bias_ref[:, cols]
             for q in range(n_src):
                 for e in range(n_loc):
                     w = w_refs[q * n_piece + h][e]
                     acc = acc + jnp.dot(left[q * n_loc + e], w, preferred_element_type=F32)
-            cols = rows_at(first[h] * half, half)
-            xs = x_ref[mine, cols].astype(F32)
-            buf[h] = (xs + xs * (acc + total * bias_ref[:, cols])).astype(BF16)
-            there = out_ref.at[at * rows : (at + 1) * rows, cols]
-            copies.append(pltpu.make_async_copy(buf.at[h], there, sems.at[h]))
-            copies[-1].start()
-        for c in copies:
-            c.wait()
-
-    args = [place] + ([] if so_far is None else [so_far])
+            out_ref[:, cols] = acc
+
     return call(
         body,
-        args + [x, ids_t, bias, gates_t, *hids, *flat_w],
-        [((block, feats), BF16)],
-        [
-            pltpu.VMEM((rows, wide), BF16),
-            pltpu.VMEM((n_src * n_loc, rows, rank), BF16),
-            pltpu.VMEM((n_piece, rows, half), BF16),
-            pltpu.SemaphoreType.DMA((n_piece,)),
-        ],
-        held=("out",) if so_far is None else ("out", 1),
-        alias=None if so_far is None else 1,
-    )[0]
+        [ids_t, bias, gates_t, *hids, *flat_w],
+        [((rows, feats), F32), ((later * n_loc, rows, rank), BF16)],
+        [pltpu.VMEM((rows, wide), BF16), pltpu.VMEM((n_src * n_loc, rows, rank), BF16)],
+    )
+
+
+def close(x, sums, lefts, wides, pair):
+    rows, feats = sums[0].shape
+    block = rows * len(sums)
+    n_loc = wides[0][0].shape[0]
+    n_piece = len(wides[0])
+    half = wides[0][0].shape[2]
+    flat_w = [w for src in wides for w in src]
+    n = len(sums)
+
+    def body(place_ref, x_ref, *refs):
+        s_refs, l_refs, w_refs, out_ref = refs[:n], refs[n : 2 * n], refs[2 * n : -1], refs[-1]
+        first = [place_ref[0], 1 - place_ref[0]] if pair else [0]
+        mine = rows_at(place_ref[1] * block, block)
+        for h in range(n_piece):
+            cols = rows_at(first[h] * half, half)
+            acc = jnp.concatenate([s[:, cols] for s in s_refs], axis=0)
+            for q in range(len(wides)):
+                for e in range(n_loc):
+                    left = jnp.concatenate([r[q * n_loc + e] for r in l_refs], axis=0)
+                    w = w_refs[q * n_piece + h][e]
+                    acc = acc + jnp.dot(left, w, preferred_element_type=F32)
+            xs = x_ref[mine, cols].astype(F32)
+            out_ref[:, cols] = (xs + xs * acc).astype(BF16)
+
+    args = [x, *sums, *lefts, *flat_w]
+    return call(body, args, [((block, feats), BF16)])[0]
 
 
 def on_device(
@@ -322,7 +340,6 @@
     block = tok // ne
     n_row = block // SPLIT
     pair = nb == 2
-    place = jnp.stack([lax.axis_index(a).astype(jnp.int32) for a in ("batch", "expert", "dim")])
     ids_t = expert_ids.T
 
     def swap(w):
@@ -337,40 +354,42 @@
         pieces = [whole(reduce_weight)]
         middle_weight, expand_weight = whole(middle_weight), whole(expand_weight)
     far = list(range(1, ne))
-    wide = widen(place, expand_weight)
+    begun = begin()
+    gate_t = gate_weight.T
     mids = [middle_weight] + [send(middle_weight, "expert", m, ne) for m in far]
-
-    parts = []
+    own, parts, logits = [], [], []
     for h in range(SPLIT):
-        starts = lambda r, h=h: [peer_to(r[1], m, ne) * block + h * n_row for m in far]
-        sent = project(place, inputs, pieces, (starts, len(far)), n_row, pair)
+        logit, mine, *sent = project(inputs, pieces, gate_t, begun, h, n_row, ne, pair)
+        own.append(mine)
+        logits.append(logit)
         parts.append([send(s, "expert", m, ne) for s, m in zip(sent, far)])
-    starts = lambda r: [r[1] * block + h * n_row for h in range(SPLIT)]
-    *own, logit = project(place, inputs, pieces, (starts, SPLIT), n_row, pair, gate_weight.T)
+    wide = widen(expand_weight)
     wides = [wide] + [send(wide, "expert", m, ne) for m in far]
-    mids = [turn(place, mids)]
+    mids = [turn(mids)]
     if pair:
         mids.append(swap(mids[0]))
 
     sums = []
     for h in range(SPLIT):
         packed = pack(
-            place, ids_t, [own[h]] + parts[h], h, ne, nz, n_loc, logit if h == 0 else None
+            ids_t, [own[h]] + parts[h], h, ne, nz, n_loc, logits if h == 0 else ()
         )
         sums.append([packed[0]] + [send(packed[m], "dim", m, nz) for m in range(1, nz)])
     hids, gates_t = [], None
     for h in range(SPLIT):
-        hid, *made = mix(place, ids_t, gates_t, sums[h], mids, h, block, ne, nz, pair)
+        hid, *made = mix(ids_t, gates_t, sums[h], mids, h, block, ne, nz, pair)
         gates_t = made[0] if made else gates_t
         hids.append([hid] + [send(hid, "dim", m, nz) for m in range(1, nz)])
     wides = [[w] + ([swap(w)] if pair else []) for w in wides]
-    out = None
+    n_src = (ne + 1) // 2
+    sums, lefts = [], []
     for h in range(SPLIT):
-        out = expand(
-            place, inputs, ids_t, bias[None, :], gates_t, hids[h], wides, h, out, ne, nz, n_loc,
-            pair,
+        total, left = expand(
+            inputs, ids_t, bias[None, :], gates_t, hids[h], wides[:n_src], h, ne, nz, n_loc, pair
         )
-    return out
+        sums.append(total)
+        lefts.append(left)
+    return close(inputs, sums, lefts, wides[n_src:], pair)
 
 
 def solution(mesh):

time: 87.4 us -> 97 us (1.11); the launches traced: 85.8 us -> 96.9 us
  waiting for transfers between devices: 30.4 us -> 62 us
  starting transfers between devices: 40.9 us -> 27.1 us
  Pallas kernels: 13.1 us -> 6.45 us
    ppermute x24, waiting for transfers between devices: 30.4 us -> 62 us  [send(): return lax.ppermute(x, axis, [(i, peer_to(i, m, n)) for i in range(n)])]
    ppermute x24, starting transfers between devices: 39.9 us -> 26.8 us  [send(): return lax.ppermute(x, axis, [(i, peer_to(i, m, n)) for i in range(n)])]
    pallas_call x11 -> x12, Pallas kernels: 13.1 us -> 6.45 us  [call(): pl.pallas_call(placed, in_specs=[space(k) for k in range(len(args))], out...]
  transfers between devices with their start and end apart: 30 -> 30, of which waited for: 12 -> 17; matrix products, arithmetic and copies ran while one was open for 0% -> 0% of each run, Pallas kernels for 13% -> 5%
where the time goes in v2:
time: 97 us; the launch traced here: 96.9 us
  waiting for transfers between devices  62 us (64%)
  starting transfers between devices  27.1 us (28%)
  Pallas kernels  6.45 us (7%)
  local copies, waits for them, and re-layouts  1.08 us (1%)
    ppermute x24, waiting for transfers between devices, send(): return lax.ppermute(x, axis, [(i, peer_to(i, m, n)) for i in range(n)])  62 us
    ppermute x24, starting transfers between devices, send(): return lax.ppermute(x, axis, [(i, peer_to(i, m, n)) for i in range(n)])  26.8 us
    pallas_call x12, Pallas kernels, call(): pl.pallas_call(placed, in_specs=[space(k) for k in range(len(args))], out...  6.45 us
  transfers between devices with their start and end apart: 30, of which 17 were waited for; matrix products, arithmetic and copies ran while one was open for 0% of the time, Pallas kernels for 5%

profile of v2, /device:TPU:0, one launch (start us, length us, event | category | flops | bytes accessed | tf_op | source)
XLA Modules:
  0.0 96.9 jit_solution(8532836885228245799)
XLA Ops:
  0.0 3.0 %collective-permute-start.7 = (bf16[2,128,256]{2,1,0:T(8,128)(2,1)}, bf16[2,128,256]{2,1,0:T(8,128)(2,1)S(1)}, u32[]{:S(2)}, u32[]{:S(2)}) collective-permute-start(bf16[2,128,256]{2,1,0:T(8,128)(2,1)} %refs_0_.7), channel_id=1, source_target_pairs={{0,4},{4,0},{8,12},{12,8},{1,5},{5,1},{9,13},{13,9},{2,6},{6,2},{1... | collective-permute-start | bytes 393224 | tf_op jit(solution)/shard_map/ppermute | solution.py:25
  3.0 1.5 %collective-permute-start.8 = (bf16[2,128,256]{2,1,0:T(8,128)(2,1)}, bf16[2,128,256]{2,1,0:T(8,128)(2,1)S(1)}, u32[]{:S(2)}, u32[]{:S(2)}) collective-permute-start(bf16[2,128,256]{2,1,0:T(8,128)(2,1)} %refs_0_.7), channel_id=1, source_target_pairs={{0,8},{4,12},{8,0},{12,4},{1,9},{5,13},{9,1},{13,5},{2,10},{6,14},... | collective-permute-start | bytes 393224 | tf_op jit(solution)/shard_map/ppermute | solution.py:25
  4.5 1.0 %copy-done.2 = bf16[2,512,256]{2,1,0:T(8,128)(2,1)S(1)} copy-done((bf16[2,512,256]{2,1,0:T(8,128)(2,1)S(1)}, bf16[2,512,256]{2,1,0:T(8,128)(2,1)}, u32[]{:S(2)}) %copy-start.2) | copy-done | bytes 524312
  5.5 0.2 shard_map.79.refs_7_
  5.8 2.0 %collective-permute-start.15 = (bf16[2,256,512]{2,1,0:T(8,128)(2,1)S(1)}, bf16[2,256,512]{2,1,0:T(8,128)(2,1)S(1)}, u32[]{:S(2)}, u32[]{:S(2)}) collective-permute-start(bf16[2,256,512]{2,1,0:T(8,128)(2,1)S(1)} %shard_map.79.refs_7_), channel_id=1, source_target_pairs={{0,4},{4,0},{8,12},{12,8},{1,5},{5,1},{9,13},{13,9},{2,6},{6,2},{1... | collective-permute-start | bytes 1572872 | tf_op jit(solution)/shard_map/ppermute | solution.py:25
  7.8 1.5 %collective-permute-start.26 = (bf16[2,256,512]{2,1,0:T(8,128)(2,1)S(1)}, bf16[2,256,512]{2,1,0:T(8,128)(2,1)S(1)}, u32[]{:S(2)}, u32[]{:S(2)}) collective-permute-start(bf16[2,256,512]{2,1,0:T(8,128)(2,1)S(1)} %shard_map.79.refs_7_), channel_id=1, source_target_pairs={{0,8},{4,12},{8,0},{12,4},{1,9},{5,13},{9,1},{13,5},{2,10},{6,14},... | collective-permute-start | bytes 1572872 | tf_op jit(solution)/shard_map/ppermute | solution.py:25
  9.3 1.7 %collective-permute-done.8.refs_2_ = bf16[2,128,256]{2,1,0:T(8,128)(2,1)S(1)} collective-permute-done((bf16[2,128,256]{2,1,0:T(8,128)(2,1)}, bf16[2,128,256]{2,1,0:T(8,128)(2,1)S(1)}, u32[]{:S(2)}, u32[]{:S(2)}) %collective-permute-start.8) | collective-permute-done | bytes 131104 | tf_op jit(solution)/shard_map/ppermute | solution.py:25
  11.0 1.0 %collective-permute-start.28 = (bf16[2,256,512]{2,1,0:T(8,128)(2,1)S(1)}, bf16[2,256,512]{2,1,0:T(8,128)(2,1)S(1)}, u32[]{:S(2)}, u32[]{:S(2)}) collective-permute-start(bf16[2,256,512]{2,1,0:T(8,128)(2,1)S(1)} %shard_map.79.refs_7_), channel_id=1, source_target_pairs={{0,12},{4,8},{8,4},{12,0},{1,13},{5,9},{9,5},{13,1},{2,14},{6,10},... | collective-permute-start | bytes 1572872 | tf_op jit(solution)/shard_map/ppermute | solution.py:25
  12.0 0.2 shard_map.77.refs_5_.refs_6_
  12.2 0.1 collective-permute-start.10
  12.3 0.8 shard_map.75
  13.1 2.9 %collective-permute-start.17 = (bf16[128,512]{1,0:T(8,128)(2,1)S(1)}, bf16[128,512]{1,0:T(8,128)(2,1)S(1)}, u32[]{:S(2)}, u32[]{:S(2)}) collective-permute-start(bf16[128,512]{1,0:T(8,128)(2,1)S(1)} %get-tuple-element.43), channel_id=1, source_target_pairs={{0,4},{4,0},{8,12},{12,8},{1,5},{5,1},{9,13},{13,9},{2,6},{6,2},{1... | collective-permute-start | bytes 393224 | tf_op jit(solution)/shard_map/ppermute | solution.py:25
  16.0 6.3 %collective-permute-done.15.refs_9_ = bf16[2,256,512]{2,1,0:T(8,128)(2,1)S(1)} collective-permute-done((bf16[2,256,512]{2,1,0:T(8,128)(2,1)S(1)}, bf16[2,256,512]{2,1,0:T(8,128)(2,1)S(1)}, u32[]{:S(2)}, u32[]{:S(2)}) %collective-permute-start.15) | collective-permute-done | bytes 524320 | tf_op jit(solution)/shard_map/ppermute | solution.py:25
  22.2 1.6 %collective-permute-start.18 = (bf16[128,512]{1,0:T(8,128)(2,1)S(1)}, bf16[128,512]{1,0:T(8,128)(2,1)S(1)}, u32[]{:S(2)}, u32[]{:S(2)}) collective-permute-start(bf16[128,512]{1,0:T(8,128)(2,1)S(1)} %get-tuple-element.44), channel_id=1, source_target_pairs={{0,8},{4,12},{8,0},{12,4},{1,9},{5,13},{9,1},{13,5},{2,10},{6,14},... | collective-permute-start | bytes 393224 | tf_op jit(solution)/shard_map/ppermute | solution.py:25
  23.8 10.0 %collective-permute-done.26.refs_5_ = bf16[2,256,512]{2,1,0:T(8,128)(2,1)S(1)} collective-permute-done((bf16[2,256,512]{2,1,0:T(8,128)(2,1)S(1)}, bf16[2,256,512]{2,1,0:T(8,128)(2,1)S(1)}, u32[]{:S(2)}, u32[]{:S(2)}) %collective-permute-start.26) | collective-permute-done | bytes 524320 | tf_op jit(solution)/shard_map/ppermute | solution.py:25
  33.8 0.7 collective-permute-start.19
  34.5 0.8 shard_map.74
  35.2 2.9 %collective-permute-start.1 = (bf16[128,512]{1,0:T(8,128)(2,1)S(1)}, bf16[128,512]{1,0:T(8,128)(2,1)S(1)}, u32[]{:S(2)}, u32[]{:S(2)}) collective-permute-start(bf16[128,512]{1,0:T(8,128)(2,1)S(1)} %get-tuple-element.30), channel_id=1, source_target_pairs={{0,4},{4,0},{8,12},{12,8},{1,5},{5,1},{9,13},{13,9},{2,6},{6,2},{1... | collective-permute-start | bytes 393224 | tf_op jit(solution)/shard_map/ppermute | solution.py:25
  38.2 1.5 %collective-permute-start.3 = (bf16[128,512]{1,0:T(8,128)(2,1)S(1)}, bf16[128,512]{1,0:T(8,128)(2,1)S(1)}, u32[]{:S(2)}, u32[]{:S(2)}) collective-permute-start(bf16[128,512]{1,0:T(8,128)(2,1)S(1)} %get-tuple-element.32), channel_id=1, source_target_pairs={{0,12},{4,8},{8,4},{12,0},{1,13},{5,9},{9,5},{13,1},{2,14},{6,10},... | collective-permute-start | bytes 393224 | tf_op jit(solution)/shard_map/ppermute | solution.py:25
  39.7 1.1 %collective-permute-done.19.refs_4_ = bf16[128,512]{1,0:T(8,128)(2,1)S(1)} collective-permute-done((bf16[128,512]{1,0:T(8,128)(2,1)S(1)}, bf16[128,512]{1,0:T(8,128)(2,1)S(1)}, u32[]{:S(2)}, u32[]{:S(2)}) %collective-permute-start.19) | collective-permute-done | bytes 131104 | tf_op jit(solution)/shard_map/ppermute | solution.py:25
  40.8 0.3 shard_map.81
  41.1 1.9 %collective-permute-done.1.refs_2_ = bf16[128,512]{1,0:T(8,128)(2,1)S(1)} collective-permute-done((bf16[128,512]{1,0:T(8,128)(2,1)S(1)}, bf16[128,512]{1,0:T(8,128)(2,1)S(1)}, u32[]{:S(2)}, u32[]{:S(2)}) %collective-permute-start.1) | collective-permute-done | bytes 131104 | tf_op jit(solution)/shard_map/ppermute | solution.py:25
  43.0 2.0 %collective-permute-done.2.refs_3_ = bf16[128,512]{1,0:T(8,128)(2,1)S(1)} collective-permute-done((bf16[128,512]{1,0:T(8,128)(2,1)S(1)}, bf16[128,512]{1,0:T(8,128)(2,1)S(1)}, u32[]{:S(2)}, u32[]{:S(2)}) %collective-permute-start.2) | collective-permute-done | bytes 131104 | tf_op jit(solution)/shard_map/ppermute | solution.py:25
  45.0 1.7 %collective-permute-start.20 = (bf16[32,1024]{1,0:T(8,128)(2,1)S(1)}, bf16[32,1024]{1,0:T(8,128)(2,1)S(1)}, u32[]{:S(2)}, u32[]{:S(2)}) collective-permute-start(bf16[32,1024]{1,0:T(8,128)(2,1)S(1)} %get-tuple-element.47), channel_id=1, source_target_pairs={{0,1},{1,0},{2,3},{3,2},{4,5},{5,4},{6,7},{7,6},{8,9},{9,8},{10,11... | collective-permute-start | bytes 196616 | tf_op jit(solution)/shard_map/ppermute | solution.py:25
  46.7 2.6 %collective-permute-start.21 = (bf16[32,1024]{1,0:T(8,128)(2,1)S(1)}, bf16[32,1024]{1,0:T(8,128)(2,1)S(1)}, u32[]{:S(2)}, u32[]{:S(2)}) collective-permute-start(bf16[32,1024]{1,0:T(8,128)(2,1)S(1)} %get-tuple-element.48), channel_id=1, source_target_pairs={{0,2},{1,3},{2,0},{3,1},{4,6},{5,7},{6,4},{7,5},{8,10},{9,11},{10,... | collective-permute-start | bytes 196616 | tf_op jit(solution)/shard_map/ppermute | solution.py:25
  49.3 0.3 collective-permute-done.20.refs_3_
  49.6 0.2 collective-permute-start.29
  49.8 0.3 shard_map.76
  50.1 2.5 %collective-permute-done.21.refs_4_ = bf16[32,1024]{1,0:T(8,128)(2,1)S(1)} collective-permute-done((bf16[32,1024]{1,0:T(8,128)(2,1)S(1)}, bf16[32,1024]{1,0:T(8,128)(2,1)S(1)}, u32[]{:S(2)}, u32[]{:S(2)}) %collective-permute-start.21) | collective-permute-done | bytes 65568 | tf_op jit(solution)/shard_map/ppermute | solution.py:25
  52.5 0.2 collective-permute-start.4
  52.8 4.2 %collective-permute-done.4.refs_2_ = bf16[40,1024]{1,0:T(8,128)(2,1)S(1)} collective-permute-done((bf16[40,1024]{1,0:T(8,128)(2,1)S(1)}, bf16[40,1024]{1,0:T(8,128)(2,1)S(1)}, u32[]{:S(2)}, u32[]{:S(2)}) %collective-permute-start.4) | collective-permute-done | bytes 81952 | tf_op jit(solution)/shard_map/ppermute | solution.py:25
  57.0 1.9 %collective-permute-start.5 = (bf16[40,1024]{1,0:T(8,128)(2,1)S(1)}, bf16[40,1024]{1,0:T(8,128)(2,1)S(1)}, u32[]{:S(2)}, u32[]{:S(2)}) collective-permute-start(bf16[40,1024]{1,0:T(8,128)(2,1)S(1)} %get-tuple-element.37), channel_id=1, source_target_pairs={{0,2},{1,3},{2,0},{3,1},{4,6},{5,7},{6,4},{7,5},{8,10},{9,11},{10,... | collective-permute-start | bytes 245768 | tf_op jit(solution)/shard_map/ppermute | solution.py:25
  58.9 5.7 %collective-permute-done.5.refs_3_ = bf16[40,1024]{1,0:T(8,128)(2,1)S(1)} collective-permute-done((bf16[40,1024]{1,0:T(8,128)(2,1)S(1)}, bf16[40,1024]{1,0:T(8,128)(2,1)S(1)}, u32[]{:S(2)}, u32[]{:S(2)}) %collective-permute-start.5) | collective-permute-done | bytes 81952 | tf_op jit(solution)/shard_map/ppermute | solution.py:25
  64.6 6.3 %collective-permute-done.6.refs_4_ = bf16[40,1024]{1,0:T(8,128)(2,1)S(1)} collective-permute-done((bf16[40,1024]{1,0:T(8,128)(2,1)S(1)}, bf16[40,1024]{1,0:T(8,128)(2,1)S(1)}, u32[]{:S(2)}, u32[]{:S(2)}) %collective-permute-start.6) | collective-permute-done | bytes 81952 | tf_op jit(solution)/shard_map/ppermute | solution.py:25
  70.8 0.5 shard_map.78
  71.4 5.5 %collective-permute-done.22.refs_5_ = bf16[32,1024]{1,0:T(8,128)(2,1)S(1)} collective-permute-done((bf16[32,1024]{1,0:T(8,128)(2,1)S(1)}, bf16[32,1024]{1,0:T(8,128)(2,1)S(1)}, u32[]{:S(2)}, u32[]{:S(2)}) %collective-permute-start.22) | collective-permute-done | bytes 65568 | tf_op jit(solution)/shard_map/ppermute | solution.py:25
  76.9 0.5 shard_map.82.refs_3_
  77.4 0.1 collective-permute-start.23
  77.5 0.6 collective-permute-start.24
  78.2 4.2 %collective-permute-done.23.refs_4_ = bf16[32,1024]{1,0:T(8,128)(2,1)S(1)} collective-permute-done((bf16[32,1024]{1,0:T(8,128)(2,1)S(1)}, bf16[32,1024]{1,0:T(8,128)(2,1)S(1)}, u32[]{:S(2)}, u32[]{:S(2)}) %collective-permute-start.23) | collective-permute-done | bytes 65568 | tf_op jit(solution)/shard_map/ppermute | solution.py:25
  82.4 2.8 %collective-permute-done.24.refs_5_ = bf16[32,1024]{1,0:T(8,128)(2,1)S(1)} collective-permute-done((bf16[32,1024]{1,0:T(8,128)(2,1)S(1)}, bf16[32,1024]{1,0:T(8,128)(2,1)S(1)}, u32[]{:S(2)}, u32[]{:S(2)}) %collective-permute-start.24) | collective-permute-done | bytes 65568 | tf_op jit(solution)/shard_map/ppermute | solution.py:25
  85.2 3.2 %collective-permute-done.25.refs_6_ = bf16[32,1024]{1,0:T(8,128)(2,1)S(1)} collective-permute-done((bf16[32,1024]{1,0:T(8,128)(2,1)S(1)}, bf16[32,1024]{1,0:T(8,128)(2,1)S(1)}, u32[]{:S(2)}, u32[]{:S(2)}) %collective-permute-start.25) | collective-permute-done | bytes 65568 | tf_op jit(solution)/shard_map/ppermute | solution.py:25
  88.4 1.2 %collective-permute-start.13 = (bf16[32,1024]{1,0:T(8,128)(2,1)S(1)}, bf16[32,1024]{1,0:T(8,128)(2,1)S(1)}, u32[]{:S(2)}, u32[]{:S(2)}) collective-permute-start(bf16[32,1024]{1,0:T(8,128)(2,1)S(1)} %get-tuple-element.40.refs_3_), channel_id=1, source_target_pairs={{0,3},{1,2},{2,1},{3,0},{4,7},{5,6},{6,5},{7,4},{8,11},{9,10},{10,... | collective-permute-start | bytes 196616 | tf_op jit(solution)/shard_map/ppermute | solution.py:25
  89.6 0.7 shard_map.83
  90.3 3.3 %collective-permute-done.12.refs_5_ = bf16[32,1024]{1,0:T(8,128)(2,1)S(1)} collective-permute-done((bf16[32,1024]{1,0:T(8,128)(2,1)S(1)}, bf16[32,1024]{1,0:T(8,128)(2,1)S(1)}, u32[]{:S(2)}, u32[]{:S(2)}) %collective-permute-start.12) | collective-permute-done | bytes 65568 | tf_op jit(solution)/shard_map/ppermute | solution.py:25
  93.6 1.0 %collective-permute-done.13.refs_6_ = bf16[32,1024]{1,0:T(8,128)(2,1)S(1)} collective-permute-done((bf16[32,1024]{1,0:T(8,128)(2,1)S(1)}, bf16[32,1024]{1,0:T(8,128)(2,1)S(1)}, u32[]{:S(2)}, u32[]{:S(2)}) %collective-permute-start.13) | collective-permute-done | bytes 65568 | tf_op jit(solution)/shard_map/ppermute | solution.py:25
  94.6 0.7 shard_map.80
  95.3 1.6 %shard_map.84 = bf16[256,1024]{1,0:T(8,128)(2,1)} custom-call(bf16[1024,1024]{1,0:T(8,128)(2,1)S(1)} %copy-done, f32[128,1024]{1,0:T(8,128)S(1)} %get-tuple-element.41.refs_1_, f32[128,1024]{1,0:T(8,128)S(1)} %get-tuple-element.50.refs_2_, bf16[4,128,256]{2,1,0:T(8,128)(2,1)S(1)} %get-tuple-element.51.refs_3_, ...), custom_call_target="tpu_custom_call" | custom-call | tf_op jit(solution)/shard_map/pallas_call | solution.py:39
  (38 shorter events, 0.1 us)
Async XLA Ops:
  0.0 9.3 %collective-permute-start.7 = (bf16[2,128,256]{2,1,0:T(8,128)(2,1)}, bf16[2,128,256]{2,1,0:T(8,128)(2,1)S(1)}, u32[]{:S(2)}, u32[]{:S(2)}) collective-permute-start(bf16[2,128,256]{2,1,0:T(8,128)(2,1)} %refs_0_.7), channel_id=1, source_target_pairs={{0,4},{4,0},{8,12},{12,8},{1,5},{5,1},{9,13},{13,9},{2,6},{6,2},{1... | collective-permute-start | bytes 393224 | tf_op jit(solution)/shard_map/ppermute | solution.py:25
  3.0 8.0 %collective-permute-start.8 = (bf16[2,128,256]{2,1,0:T(8,128)(2,1)}, bf16[2,128,256]{2,1,0:T(8,128)(2,1)S(1)}, u32[]{:S(2)}, u32[]{:S(2)}) collective-permute-start(bf16[2,128,256]{2,1,0:T(8,128)(2,1)} %refs_0_.7), channel_id=1, source_target_pairs={{0,8},{4,12},{8,0},{12,4},{1,9},{5,13},{9,1},{13,5},{2,10},{6,14},... | collective-permute-start | bytes 393224 | tf_op jit(solution)/shard_map/ppermute | solution.py:25
  4.5 7.5 %collective-permute-start.9 = (bf16[2,128,256]{2,1,0:T(8,128)(2,1)}, bf16[2,128,256]{2,1,0:T(8,128)(2,1)S(1)}, u32[]{:S(2)}, u32[]{:S(2)}) collective-permute-start(bf16[2,128,256]{2,1,0:T(8,128)(2,1)} %refs_0_.7), channel_id=1, source_target_pairs={{0,12},{4,8},{8,4},{12,0},{1,13},{5,9},{9,5},{13,1},{2,14},{6,10},... | collective-permute-start | bytes 393224 | tf_op jit(solution)/shard_map/ppermute | solution.py:25
  4.5 1.0 %copy-start.2 = (bf16[2,512,256]{2,1,0:T(8,128)(2,1)S(1)}, bf16[2,512,256]{2,1,0:T(8,128)(2,1)}, u32[]{:S(2)}) copy-start(bf16[2,512,256]{2,1,0:T(8,128)(2,1)} %refs_0_.8) | copy-start | bytes 1572868
  5.7 6.3 %copy-start.3 = (bf16[2,128,256]{2,1,0:T(8,128)(2,1)S(1)}, bf16[2,128,256]{2,1,0:T(8,128)(2,1)}, u32[]{:S(2)}) copy-start(bf16[2,128,256]{2,1,0:T(8,128)(2,1)} %refs_0_.7) | copy-start | bytes 393220
  5.7 6.6 %copy-start = (bf16[1024,1024]{1,0:T(8,128)(2,1)S(1)}, bf16[1024,1024]{1,0:T(8,128)(2,1)}, u32[]{:S(2)}) copy-start(bf16[1024,1024]{1,0:T(8,128)(2,1)} %refs_0_.9) | copy-start | bytes 6291460
  5.7 6.6 %copy-start.5 = (bf16[2,512,256]{2,1,0:T(8,128)(2,1)S(1)}, bf16[2,512,256]{2,1,0:T(8,128)(2,1)}, u32[]{:S(2)}) copy-start(bf16[2,512,256]{2,1,0:T(8,128)(2,1)} %refs_1_.3) | copy-start | bytes 1572868
  5.8 6.6 %copy-start.6 = (bf16[1024,8]{0,1:T(8,128)(2,1)S(1)}, bf16[1024,8]{0,1:T(8,128)(2,1)}, u32[]{:S(2)}) copy-start(bf16[1024,8]{0,1:T(8,128)(2,1)} %param.9) | copy-start | bytes 49156
  5.8 16.5 %collective-permute-start.15 = (bf16[2,256,512]{2,1,0:T(8,128)(2,1)S(1)}, bf16[2,256,512]{2,1,0:T(8,128)(2,1)S(1)}, u32[]{:S(2)}, u32[]{:S(2)}) collective-permute-start(bf16[2,256,512]{2,1,0:T(8,128)(2,1)S(1)} %shard_map.79.refs_7_), channel_id=1, source_target_pairs={{0,4},{4,0},{8,12},{12,8},{1,5},{5,1},{9,13},{13,9},{2,6},{6,2},{1... | collective-permute-start | bytes 1572872 | tf_op jit(solution)/shard_map/ppermute | solution.py:25
  7.8 26.0 %collective-permute-start.26 = (bf16[2,256,512]{2,1,0:T(8,128)(2,1)S(1)}, bf16[2,256,512]{2,1,0:T(8,128)(2,1)S(1)}, u32[]{:S(2)}, u32[]{:S(2)}) collective-permute-start(bf16[2,256,512]{2,1,0:T(8,128)(2,1)S(1)} %shard_map.79.refs_7_), channel_id=1, source_target_pairs={{0,8},{4,12},{8,0},{12,4},{1,9},{5,13},{9,1},{13,5},{2,10},{6,14},... | collective-permute-start | bytes 1572872 | tf_op jit(solution)/shard_map/ppermute | solution.py:25
  9.3 3.0 %collective-permute-start = (bf16[2,512,256]{2,1,0:T(8,128)(2,1)}, bf16[2,512,256]{2,1,0:T(8,128)(2,1)S(1)}, u32[]{:S(2)}, u32[]{:S(2)}) collective-permute-start(bf16[2,512,256]{2,1,0:T(8,128)(2,1)} %refs_1_.3), channel_id=1, source_target_pairs={{0,16},{16,0},{1,17},{17,1},{2,18},{18,2},{3,19},{19,3},{4,20},{20... | collective-permute-start | bytes 1572872 | tf_op jit(solution)/shard_map/ppermute | solution.py:346
  11.0 24.2 %collective-permute-start.28 = (bf16[2,256,512]{2,1,0:T(8,128)(2,1)S(1)}, bf16[2,256,512]{2,1,0:T(8,128)(2,1)S(1)}, u32[]{:S(2)}, u32[]{:S(2)}) collective-permute-start(bf16[2,256,512]{2,1,0:T(8,128)(2,1)S(1)} %shard_map.79.refs_7_), channel_id=1, source_target_pairs={{0,12},{4,8},{8,4},{12,0},{1,13},{5,9},{9,5},{13,1},{2,14},{6,10},... | collective-permute-start | bytes 1572872 | tf_op jit(solution)/shard_map/ppermute | solution.py:25
  12.2 37.0 %collective-permute-start.10 = (bf16[8,256,128]{2,1,0:T(8,128)(2,1)S(1)}, bf16[8,256,128]{2,1,0:T(8,128)(2,1)S(1)}, u32[]{:S(2)}, u32[]{:S(2)}) collective-permute-start(bf16[8,256,128]{2,1,0:T(8,128)(2,1)S(1)} %shard_map.77.refs_5_.refs_6_), channel_id=1, source_target_pairs={{0,16},{16,0},{1,17},{17,1},{2,18},{18,2},{3,19},{19,3},{4,20},{20... | collective-permute-start | bytes 1572872 | tf_op jit(solution)/shard_map/ppermute | solution.py:346
  13.1 25.1 %collective-permute-start.17 = (bf16[128,512]{1,0:T(8,128)(2,1)S(1)}, bf16[128,512]{1,0:T(8,128)(2,1)S(1)}, u32[]{:S(2)}, u32[]{:S(2)}) collective-permute-start(bf16[128,512]{1,0:T(8,128)(2,1)S(1)} %get-tuple-element.43), channel_id=1, source_target_pairs={{0,4},{4,0},{8,12},{12,8},{1,5},{5,1},{9,13},{13,9},{2,6},{6,2},{1... | collective-permute-start | bytes 393224 | tf_op jit(solution)/shard_map/ppermute | solution.py:25
  22.2 15.9 %collective-permute-start.18 = (bf16[128,512]{1,0:T(8,128)(2,1)S(1)}, bf16[128,512]{1,0:T(8,128)(2,1)S(1)}, u32[]{:S(2)}, u32[]{:S(2)}) collective-permute-start(bf16[128,512]{1,0:T(8,128)(2,1)S(1)} %get-tuple-element.44), channel_id=1, source_target_pairs={{0,8},{4,12},{8,0},{12,4},{1,9},{5,13},{9,1},{13,5},{2,10},{6,14},... | collective-permute-start | bytes 393224 | tf_op jit(solution)/shard_map/ppermute | solution.py:25
  33.8 7.0 %copy-start.1 = (s32[1024,4]{0,1:T(4,128)S(1)}, s32[1024,4]{0,1:T(4,128)}, u32[]{:S(2)}) copy-start(s32[1024,4]{0,1:T(4,128)} %param.8) | copy-start | bytes 49156
  33.8 7.0 %collective-permute-start.19 = (bf16[128,512]{1,0:T(8,128)(2,1)S(1)}, bf16[128,512]{1,0:T(8,128)(2,1)S(1)}, u32[]{:S(2)}, u32[]{:S(2)}) collective-permute-start(bf16[128,512]{1,0:T(8,128)(2,1)S(1)} %get-tuple-element.45), channel_id=1, source_target_pairs={{0,12},{4,8},{8,4},{12,0},{1,13},{5,9},{9,5},{13,1},{2,14},{6,10},... | collective-permute-start | bytes 393224 | tf_op jit(solution)/shard_map/ppermute | solution.py:25
  35.2 54.4 %copy-start.4 = (f32[1024]{0:T(1024)S(1)}, f32[1024]{0:T(1024)}, u32[]{:S(2)}) copy-start(f32[1024]{0:T(1024)} %param.13) | copy-start | bytes 12292
  35.2 7.8 %collective-permute-start.1 = (bf16[128,512]{1,0:T(8,128)(2,1)S(1)}, bf16[128,512]{1,0:T(8,128)(2,1)S(1)}, u32[]{:S(2)}, u32[]{:S(2)}) collective-permute-start(bf16[128,512]{1,0:T(8,128)(2,1)S(1)} %get-tuple-element.30), channel_id=1, source_target_pairs={{0,4},{4,0},{8,12},{12,8},{1,5},{5,1},{9,13},{13,9},{2,6},{6,2},{1... | collective-permute-start | bytes 393224 | tf_op jit(solution)/shard_map/ppermute | solution.py:25
  38.2 6.8 %collective-permute-start.2 = (bf16[128,512]{1,0:T(8,128)(2,1)S(1)}, bf16[128,512]{1,0:T(8,128)(2,1)S(1)}, u32[]{:S(2)}, u32[]{:S(2)}) collective-permute-start(bf16[128,512]{1,0:T(8,128)(2,1)S(1)} %get-tuple-element.31), channel_id=1, source_target_pairs={{0,8},{4,12},{8,0},{12,4},{1,9},{5,13},{9,1},{13,5},{2,10},{6,14},... | collective-permute-start | bytes 393224 | tf_op jit(solution)/shard_map/ppermute | solution.py:25
  38.2 8.5 %collective-permute-start.3 = (bf16[128,512]{1,0:T(8,128)(2,1)S(1)}, bf16[128,512]{1,0:T(8,128)(2,1)S(1)}, u32[]{:S(2)}, u32[]{:S(2)}) collective-permute-start(bf16[128,512]{1,0:T(8,128)(2,1)S(1)} %get-tuple-element.32), channel_id=1, source_target_pairs={{0,12},{4,8},{8,4},{12,0},{1,13},{5,9},{9,5},{13,1},{2,14},{6,10},... | collective-permute-start | bytes 393224 | tf_op jit(solution)/shard_map/ppermute | solution.py:25
  40.8 36.7 %collective-permute-start.14 = (bf16[2,256,512]{2,1,0:T(8,128)(2,1)S(1)}, bf16[2,256,512]{2,1,0:T(8,128)(2,1)S(1)}, u32[]{:S(2)}, u32[]{:S(2)}) collective-permute-start(bf16[2,256,512]{2,1,0:T(8,128)(2,1)S(1)} %shard_map.79.refs_7_), channel_id=1, source_target_pairs={{0,16},{16,0},{1,17},{17,1},{2,18},{18,2},{3,19},{19,3},{4,20},{20... | collective-permute-start | bytes 1572872 | tf_op jit(solution)/shard_map/ppermute | solution.py:346
  43.0 45.4 %collective-permute-start.16 = (bf16[2,256,512]{2,1,0:T(8,128)(2,1)S(1)}, bf16[2,256,512]{2,1,0:T(8,128)(2,1)S(1)}, u32[]{:S(2)}, u32[]{:S(2)}) collective-permute-start(bf16[2,256,512]{2,1,0:T(8,128)(2,1)S(1)} %collective-permute-done.15.refs_9_), channel_id=1, source_target_pairs={{0,16},{16,0},{1,17},{17,1},{2,18},{18,2},{3,19},{19,3},{4,20},{20... | collective-permute-start | bytes 1572872 | tf_op jit(solution)/shard_map/ppermute | solution.py:346
  45.0 4.6 %collective-permute-start.20 = (bf16[32,1024]{1,0:T(8,128)(2,1)S(1)}, bf16[32,1024]{1,0:T(8,128)(2,1)S(1)}, u32[]{:S(2)}, u32[]{:S(2)}) collective-permute-start(bf16[32,1024]{1,0:T(8,128)(2,1)S(1)} %get-tuple-element.47), channel_id=1, source_target_pairs={{0,1},{1,0},{2,3},{3,2},{4,5},{5,4},{6,7},{7,6},{8,9},{9,8},{10,11... | collective-permute-start | bytes 196616 | tf_op jit(solution)/shard_map/ppermute | solution.py:25
  46.7 5.9 %collective-permute-start.21 = (bf16[32,1024]{1,0:T(8,128)(2,1)S(1)}, bf16[32,1024]{1,0:T(8,128)(2,1)S(1)}, u32[]{:S(2)}, u32[]{:S(2)}) collective-permute-start(bf16[32,1024]{1,0:T(8,128)(2,1)S(1)} %get-tuple-element.48), channel_id=1, source_target_pairs={{0,2},{1,3},{2,0},{3,1},{4,6},{5,7},{6,4},{7,5},{8,10},{9,11},{10,... | collective-permute-start | bytes 196616 | tf_op jit(solution)/shard_map/ppermute | solution.py:25
  49.3 46.0 %collective-permute-start.27 = (bf16[2,256,512]{2,1,0:T(8,128)(2,1)S(1)}, bf16[2,256,512]{2,1,0:T(8,128)(2,1)S(1)}, u32[]{:S(2)}, u32[]{:S(2)}) collective-permute-start(bf16[2,256,512]{2,1,0:T(8,128)(2,1)S(1)} %collective-permute-done.26.refs_5_), channel_id=1, source_target_pairs={{0,16},{16,0},{1,17},{17,1},{2,18},{18,2},{3,19},{19,3},{4,20},{20... | collective-permute-start | bytes 1572872 | tf_op jit(solution)/shard_map/ppermute | solution.py:346
  49.6 45.7 %collective-permute-start.29 = (bf16[2,256,512]{2,1,0:T(8,128)(2,1)S(1)}, bf16[2,256,512]{2,1,0:T(8,128)(2,1)S(1)}, u32[]{:S(2)}, u32[]{:S(2)}) collective-permute-start(bf16[2,256,512]{2,1,0:T(8,128)(2,1)S(1)} %collective-permute-done.28.refs_7_), channel_id=1, source_target_pairs={{0,16},{16,0},{1,17},{17,1},{2,18},{18,2},{3,19},{19,3},{4,20},{20... | collective-permute-start | bytes 1572872 | tf_op jit(solution)/shard_map/ppermute | solution.py:346
  52.5 4.4 %collective-permute-start.4 = (bf16[40,1024]{1,0:T(8,128)(2,1)S(1)}, bf16[40,1024]{1,0:T(8,128)(2,1)S(1)}, u32[]{:S(2)}, u32[]{:S(2)}) collective-permute-start(bf16[40,1024]{1,0:T(8,128)(2,1)S(1)} %get-tuple-element.36), channel_id=1, source_target_pairs={{0,1},{1,0},{2,3},{3,2},{4,5},{5,4},{6,7},{7,6},{8,9},{9,8},{10,11... | collective-permute-start | bytes 245768 | tf_op jit(solution)/shard_map/ppermute | solution.py:25
  57.0 7.6 %collective-permute-start.5 = (bf16[40,1024]{1,0:T(8,128)(2,1)S(1)}, bf16[40,1024]{1,0:T(8,128)(2,1)S(1)}, u32[]{:S(2)}, u32[]{:S(2)}) collective-permute-start(bf16[40,1024]{1,0:T(8,128)(2,1)S(1)} %get-tuple-element.37), channel_id=1, source_target_pairs={{0,2},{1,3},{2,0},{3,1},{4,6},{5,7},{6,4},{7,5},{8,10},{9,11},{10,... | collective-permute-start | bytes 245768 | tf_op jit(solution)/shard_map/ppermute | solution.py:25
  64.6 6.3 %collective-permute-start.6 = (bf16[40,1024]{1,0:T(8,128)(2,1)S(1)}, bf16[40,1024]{1,0:T(8,128)(2,1)S(1)}, u32[]{:S(2)}, u32[]{:S(2)}) collective-permute-start(bf16[40,1024]{1,0:T(8,128)(2,1)S(1)} %get-tuple-element.38), channel_id=1, source_target_pairs={{0,3},{1,2},{2,1},{3,0},{4,7},{5,6},{6,5},{7,4},{8,11},{9,10},{10,... | collective-permute-start | bytes 245768 | tf_op jit(solution)/shard_map/ppermute | solution.py:25
  70.8 6.1 %collective-permute-start.22 = (bf16[32,1024]{1,0:T(8,128)(2,1)S(1)}, bf16[32,1024]{1,0:T(8,128)(2,1)S(1)}, u32[]{:S(2)}, u32[]{:S(2)}) collective-permute-start(bf16[32,1024]{1,0:T(8,128)(2,1)S(1)} %get-tuple-element.49), channel_id=1, source_target_pairs={{0,3},{1,2},{2,1},{3,0},{4,7},{5,6},{6,5},{7,4},{8,11},{9,10},{10,... | collective-permute-start | bytes 196616 | tf_op jit(solution)/shard_map/ppermute | solution.py:25
  77.4 4.9 %collective-permute-start.23 = (bf16[32,1024]{1,0:T(8,128)(2,1)S(1)}, bf16[32,1024]{1,0:T(8,128)(2,1)S(1)}, u32[]{:S(2)}, u32[]{:S(2)}) collective-permute-start(bf16[32,1024]{1,0:T(8,128)(2,1)S(1)} %shard_map.82.refs_3_), channel_id=1, source_target_pairs={{0,1},{1,0},{2,3},{3,2},{4,5},{5,4},{6,7},{7,6},{8,9},{9,8},{10,11... | collective-permute-start | bytes 196616 | tf_op jit(solution)/shard_map/ppermute | solution.py:25
  77.5 7.7 %collective-permute-start.24 = (bf16[32,1024]{1,0:T(8,128)(2,1)S(1)}, bf16[32,1024]{1,0:T(8,128)(2,1)S(1)}, u32[]{:S(2)}, u32[]{:S(2)}) collective-permute-start(bf16[32,1024]{1,0:T(8,128)(2,1)S(1)} %shard_map.82.refs_3_), channel_id=1, source_target_pairs={{0,2},{1,3},{2,0},{3,1},{4,6},{5,7},{6,4},{7,5},{8,10},{9,11},{10,... | collective-permute-start | bytes 196616 | tf_op jit(solution)/shard_map/ppermute | solution.py:25
  82.4 6.1 %collective-permute-start.25 = (bf16[32,1024]{1,0:T(8,128)(2,1)S(1)}, bf16[32,1024]{1,0:T(8,128)(2,1)S(1)}, u32[]{:S(2)}, u32[]{:S(2)}) collective-permute-start(bf16[32,1024]{1,0:T(8,128)(2,1)S(1)} %shard_map.82.refs_3_), channel_id=1, source_target_pairs={{0,3},{1,2},{2,1},{3,0},{4,7},{5,6},{6,5},{7,4},{8,11},{9,10},{10,... | collective-permute-start | bytes 196616 | tf_op jit(solution)/shard_map/ppermute | solution.py:25
  85.2 5.1 %collective-permute-start.11 = (bf16[32,1024]{1,0:T(8,128)(2,1)S(1)}, bf16[32,1024]{1,0:T(8,128)(2,1)S(1)}, u32[]{:S(2)}, u32[]{:S(2)}) collective-permute-start(bf16[32,1024]{1,0:T(8,128)(2,1)S(1)} %get-tuple-element.40.refs_3_), channel_id=1, source_target_pairs={{0,1},{1,0},{2,3},{3,2},{4,5},{5,4},{6,7},{7,6},{8,9},{9,8},{10,11... | collective-permute-start | bytes 196616 | tf_op jit(solution)/shard_map/ppermute | solution.py:25
  88.4 5.2 %collective-permute-start.12 = (bf16[32,1024]{1,0:T(8,128)(2,1)S(1)}, bf16[32,1024]{1,0:T(8,128)(2,1)S(1)}, u32[]{:S(2)}, u32[]{:S(2)}) collective-permute-start(bf16[32,1024]{1,0:T(8,128)(2,1)S(1)} %get-tuple-element.40.refs_3_), channel_id=1, source_target_pairs={{0,2},{1,3},{2,0},{3,1},{4,6},{5,7},{6,4},{7,5},{8,10},{9,11},{10,... | collective-permute-start | bytes 196616 | tf_op jit(solution)/shard_map/ppermute | solution.py:25
  88.4 6.2 %collective-permute-start.13 = (bf16[32,1024]{1,0:T(8,128)(2,1)S(1)}, bf16[32,1024]{1,0:T(8,128)(2,1)S(1)}, u32[]{:S(2)}, u32[]{:S(2)}) collective-permute-start(bf16[32,1024]{1,0:T(8,128)(2,1)S(1)} %get-tuple-element.40.refs_3_), channel_id=1, source_target_pairs={{0,3},{1,2},{2,1},{3,0},{4,7},{5,6},{6,5},{7,4},{8,11},{9,10},{10,... | collective-permute-start | bytes 196616 | tf_op jit(solution)/shard_map/ppermute | solution.py:25

commit v3 on v2

--- a/solution.py
+++ b/solution.py
@@ -10,6 +10,7 @@
 BF16 = jnp.bfloat16
 LAST = (((1,), (1,)), ((), ()))
 MIB = 1 << 20
+LANES = 128
 SPLIT = 2
 
 
@@ -137,7 +138,9 @@
     top = ids_t.shape[0]
     n_part = len(parts)
     n_log = len(logits)
-    more = logits[0].shape[0] if logits else 0
+    high_at = sum(l.shape[1] for l in logits)
+    deep = logits[0].shape[0] if logits else 0
+    more = -(-2 * high_at * deep // (per * LANES)) * LANES
 
     def body(place_ref, ids_ref, *refs):
         p_refs, scratch = refs[:n_part], refs[-1]
@@ -155,29 +158,31 @@
                     )
             scratch[:, j * rank : (j + 1) * rank] = acc
         for m in range(n_dim):
-            outs[m][:per, :] = scratch[rows_at(peer_to(z_at, m, n_dim) * per, per), :]
+            outs[m][:, : top * rank] = scratch[rows_at(peer_to(z_at, m, n_dim) * per, per), :]
         if logits:
             full = jnp.concatenate([r[...] for r in l_refs], axis=1)
             n = full.shape[1]
             high = full.astype(BF16)
             low = (full - high.astype(F32)).astype(BF16)
+            both = jnp.concatenate([high, low], axis=1)
             for m in range(n_dim):
-                outs[m][per:, :n] = high
-                outs[m][per:, n : 2 * n] = low
-                outs[m][per:, 2 * n :] = jnp.zeros((more, top * rank - 2 * n), BF16)
+                outs[m][:, top * rank :] = jnp.zeros((per, more), BF16)
+                for k, col in enumerate(range(0, 2 * n, LANES)):
+                    row, lane = k * deep % per, top * rank + k * deep // per * LANES
+                    outs[m][row : row + deep, lane : lane + LANES] = both[:, col : col + LANES]
 
     return call(
         body,
         [ids_t, *parts, *logits],
-        [((per + more, top * rank), BF16)] * n_dim,
+        [((per, top * rank + more), BF16)] * n_dim,
         [pltpu.VMEM((rows, top * rank), BF16)],
     )
 
 
 def mix(ids_t, gates_t, parts, mids, at, block, n_expert, n_dim, pair):
-    wide = parts[0].shape[1]
     top, _ = ids_t.shape
-    rank = wide // top
+    rank = mids[0].shape[1]
+    wide = top * rank
     per = block // SPLIT // n_dim
     n_part = len(parts)
     n_piece = len(mids)
@@ -195,8 +200,12 @@
             out_ref, g_out, squash, ids_s, gate_s = refs
             logit = jnp.zeros((n_all, block), F32)
             for p in range(n_part):
-                logit = logit + p_refs[p][per:, :block].astype(F32)
-                logit = logit + p_refs[p][per:, block : 2 * block].astype(F32)
+                found = []
+                for k in range(2 * block // LANES):
+                    row, lane = k * n_all % per, wide + k * n_all // per * LANES
+                    found.append(p_refs[p][row : row + n_all, lane : lane + LANES].astype(F32))
+                found = jnp.concatenate(found, axis=1)
+                logit = logit + found[:, :block] + found[:, block:]
             gates_t = jax.nn.sigmoid(logit)
             g_out[...] = gates_t
         else:
@@ -304,32 +313,46 @@
     )
 
 
-def close(x, sums, lefts, wides, pair):
+def close(x, sums, lefts, wides, piece, so_far, pair):
     rows, feats = sums[0].shape
     block = rows * len(sums)
-    n_loc = wides[0][0].shape[0]
-    n_piece = len(wides[0])
-    half = wides[0][0].shape[2]
-    flat_w = [w for src in wides for w in src]
+    n_loc, _, half = wides[0].shape
     n = len(sums)
-
-    def body(place_ref, x_ref, *refs):
-        s_refs, l_refs, w_refs, out_ref = refs[:n], refs[n : 2 * n], refs[2 * n : -1], refs[-1]
+    n_w = len(wides)
+    n_first = 0 if so_far is None else 1
+
+    def body(place_ref, *refs):
+        refs = refs[n_first:]
+        x_ref, s_refs, l_refs = refs[0], refs[1 : n + 1], refs[n + 1 : 2 * n + 1]
+        w_refs = refs[2 * n + 1 : 2 * n + 1 + n_w]
+        out_ref, buf, sem = refs[2 * n + 1 + n_w :]
         first = [place_ref[0], 1 - place_ref[0]] if pair else [0]
         mine = rows_at(place_ref[1] * block, block)
-        for h in range(n_piece):
-            cols = rows_at(first[h] * half, half)
+        copies = []
+        for c in range(2):
+            cut = slice(c * half // 2, (c + 1) * half // 2)
+            cols = rows_at(first[piece] * half + c * (half // 2), half // 2)
             acc = jnp.concatenate([s[:, cols] for s in s_refs], axis=0)
-            for q in range(len(wides)):
+            for q in range(n_w):
                 for e in range(n_loc):
                     left = jnp.concatenate([r[q * n_loc + e] for r in l_refs], axis=0)
-                    w = w_refs[q * n_piece + h][e]
-                    acc = acc + jnp.dot(left, w, preferred_element_type=F32)
+                    acc = acc + jnp.dot(left, w_refs[q][e, :, cut], preferred_element_type=F32)
             xs = x_ref[mine, cols].astype(F32)
-            out_ref[:, cols] = (xs + xs * acc).astype(BF16)
-
-    args = [x, *sums, *lefts, *flat_w]
-    return call(body, args, [((block, feats), BF16)])[0]
+            buf[:, cut] = (xs + xs * acc).astype(BF16)
+            copies.append(pltpu.make_async_copy(buf.at[:, cut], out_ref.at[:, cols], sem.at[c]))
+            copies[-1].start()
+        for c in copies:
+            c.wait()
+
+    args = ([] if so_far is None else [so_far]) + [x, *sums, *lefts, *wides]
+    return call(
+        body,
+        args,
+        [((block, feats), BF16)],
+        [pltpu.VMEM((block, half), BF16), pltpu.SemaphoreType.DMA((2,))],
+        held=("out",) if so_far is None else ("out", 0),
+        alias=None if so_far is None else 0,
+    )[0]
 
 
 def on_device(
@@ -381,7 +404,7 @@
         gates_t = made[0] if made else gates_t
         hids.append([hid] + [send(hid, "dim", m, nz) for m in range(1, nz)])
     wides = [[w] + ([swap(w)] if pair else []) for w in wides]
-    n_src = (ne + 1) // 2
+    n_src = max(1, ne - 1)
     sums, lefts = [], []
     for h in range(SPLIT):
         total, left = expand(
@@ -389,7 +412,10 @@
         )
         sums.append(total)
         lefts.append(left)
-    return close(inputs, sums, lefts, wides[n_src:], pair)
+    out = None
+    for k in range(len(wides[0])):
+        out = close(inputs, sums, lefts, [w[k] for w in wides[n_src:]], k, out, pair)
+    return out
 
 
 def solution(mesh):

time: 97 us -> 98.2 us (1.012)
  starting transfers between devices: 27.1 us -> 31.1 us
  waiting for transfers between devices: 62 us -> 58.3 us
    ppermute x24, waiting for transfers between devices: 62 us -> 58.2 us  [send(): return lax.ppermute(x, axis, [(i, peer_to(i, m, n)) for i in range(n)])]
    ppermute x24, starting transfers between devices: 26.8 us -> 30.5 us  [send(): return lax.ppermute(x, axis, [(i, peer_to(i, m, n)) for i in range(n)])]
    pallas_call x12 -> x13, Pallas kernels: 6.45 us -> 7.39 us  [call(): pl.pallas_call(placed, in_specs=[space(k) for k in range(len(args))], out...]
  transfers between devices with their start and end apart: 30 -> 30, of which waited for: 17 -> 18; matrix products, arithmetic and copies ran while one was open for 0% -> 0% of each run, Pallas kernels for 5% -> 6%
where the time goes in v3:
time: 98.2 us; the launch traced here: 98 us
  waiting for transfers between devices  58.3 us (59%)
  starting transfers between devices  31.1 us (32%)
  Pallas kernels  7.39 us (8%)
  local copies, waits for them, and re-layouts  1.08 us (1%)
    ppermute x24, waiting for transfers between devices, send(): return lax.ppermute(x, axis, [(i, peer_to(i, m, n)) for i in range(n)])  58.2 us
    ppermute x24, starting transfers between devices, send(): return lax.ppermute(x, axis, [(i, peer_to(i, m, n)) for i in range(n)])  30.5 us
    pallas_call x13, Pallas kernels, call(): pl.pallas_call(placed, in_specs=[space(k) for k in range(len(args))], out...  7.39 us
  transfers between devices with their start and end apart: 30, of which 18 were waited for; matrix products, arithmetic and copies ran while one was open for 0% of the time, Pallas kernels for 6%

profile of v3, /device:TPU:0, one launch (start us, length us, event | category | flops | bytes accessed | tf_op | source)
XLA Modules:
  0.0 98.0 jit_solution(7459830586185084099)
XLA Ops:
  0.0 3.0 %collective-permute-start.7 = (bf16[2,128,256]{2,1,0:T(8,128)(2,1)}, bf16[2,128,256]{2,1,0:T(8,128)(2,1)S(1)}, u32[]{:S(2)}, u32[]{:S(2)}) collective-permute-start(bf16[2,128,256]{2,1,0:T(8,128)(2,1)} %refs_0_.7), channel_id=1, source_target_pairs={{0,4},{4,0},{8,12},{12,8},{1,5},{5,1},{9,13},{13,9},{2,6},{6,2},{1... | collective-permute-start | bytes 393224 | tf_op jit(solution)/shard_map/ppermute | solution.py:26
  3.0 1.5 %collective-permute-start.8 = (bf16[2,128,256]{2,1,0:T(8,128)(2,1)}, bf16[2,128,256]{2,1,0:T(8,128)(2,1)S(1)}, u32[]{:S(2)}, u32[]{:S(2)}) collective-permute-start(bf16[2,128,256]{2,1,0:T(8,128)(2,1)} %refs_0_.7), channel_id=1, source_target_pairs={{0,8},{4,12},{8,0},{12,4},{1,9},{5,13},{9,1},{13,5},{2,10},{6,14},... | collective-permute-start | bytes 393224 | tf_op jit(solution)/shard_map/ppermute | solution.py:26
  4.5 1.0 %copy-done.2 = bf16[2,512,256]{2,1,0:T(8,128)(2,1)S(1)} copy-done((bf16[2,512,256]{2,1,0:T(8,128)(2,1)S(1)}, bf16[2,512,256]{2,1,0:T(8,128)(2,1)}, u32[]{:S(2)}) %copy-start.2) | copy-done | bytes 524312
  5.8 2.0 %collective-permute-start.15 = (bf16[2,256,512]{2,1,0:T(8,128)(2,1)S(1)}, bf16[2,256,512]{2,1,0:T(8,128)(2,1)S(1)}, u32[]{:S(2)}, u32[]{:S(2)}) collective-permute-start(bf16[2,256,512]{2,1,0:T(8,128)(2,1)S(1)} %shard_map.79.refs_7_), channel_id=1, source_target_pairs={{0,4},{4,0},{8,12},{12,8},{1,5},{5,1},{9,13},{13,9},{2,6},{6,2},{1... | collective-permute-start | bytes 1572872 | tf_op jit(solution)/shard_map/ppermute | solution.py:26
  7.8 1.5 %collective-permute-start.17 = (bf16[2,256,512]{2,1,0:T(8,128)(2,1)S(1)}, bf16[2,256,512]{2,1,0:T(8,128)(2,1)S(1)}, u32[]{:S(2)}, u32[]{:S(2)}) collective-permute-start(bf16[2,256,512]{2,1,0:T(8,128)(2,1)S(1)} %shard_map.79.refs_7_), channel_id=1, source_target_pairs={{0,8},{4,12},{8,0},{12,4},{1,9},{5,13},{9,1},{13,5},{2,10},{6,14},... | collective-permute-start | bytes 1572872 | tf_op jit(solution)/shard_map/ppermute | solution.py:26
  9.3 1.6 %collective-permute-done.8.refs_2_ = bf16[2,128,256]{2,1,0:T(8,128)(2,1)S(1)} collective-permute-done((bf16[2,128,256]{2,1,0:T(8,128)(2,1)}, bf16[2,128,256]{2,1,0:T(8,128)(2,1)S(1)}, u32[]{:S(2)}, u32[]{:S(2)}) %collective-permute-start.8) | collective-permute-done | bytes 131104 | tf_op jit(solution)/shard_map/ppermute | solution.py:26
  11.0 1.6 %collective-permute-start.28 = (bf16[2,256,512]{2,1,0:T(8,128)(2,1)S(1)}, bf16[2,256,512]{2,1,0:T(8,128)(2,1)S(1)}, u32[]{:S(2)}, u32[]{:S(2)}) collective-permute-start(bf16[2,256,512]{2,1,0:T(8,128)(2,1)S(1)} %shard_map.79.refs_7_), channel_id=1, source_target_pairs={{0,12},{4,8},{8,4},{12,0},{1,13},{5,9},{9,5},{13,1},{2,14},{6,10},... | collective-permute-start | bytes 1572872 | tf_op jit(solution)/shard_map/ppermute | solution.py:26
  12.9 0.8 shard_map.74
  13.6 1.8 %collective-permute-start.1 = (bf16[128,512]{1,0:T(8,128)(2,1)S(1)}, bf16[128,512]{1,0:T(8,128)(2,1)S(1)}, u32[]{:S(2)}, u32[]{:S(2)}) collective-permute-start(bf16[128,512]{1,0:T(8,128)(2,1)S(1)} %get-tuple-element.30), channel_id=1, source_target_pairs={{0,4},{4,0},{8,12},{12,8},{1,5},{5,1},{9,13},{13,9},{2,6},{6,2},{1... | collective-permute-start | bytes 393224 | tf_op jit(solution)/shard_map/ppermute | solution.py:26
  15.4 0.8 shard_map.75
  16.2 5.1 %collective-permute-done.15.refs_9_ = bf16[2,256,512]{2,1,0:T(8,128)(2,1)S(1)} collective-permute-done((bf16[2,256,512]{2,1,0:T(8,128)(2,1)S(1)}, bf16[2,256,512]{2,1,0:T(8,128)(2,1)S(1)}, u32[]{:S(2)}, u32[]{:S(2)}) %collective-permute-start.15) | collective-permute-done | bytes 524320 | tf_op jit(solution)/shard_map/ppermute | solution.py:26
  21.3 1.6 %collective-permute-start.19 = (bf16[128,512]{1,0:T(8,128)(2,1)S(1)}, bf16[128,512]{1,0:T(8,128)(2,1)S(1)}, u32[]{:S(2)}, u32[]{:S(2)}) collective-permute-start(bf16[128,512]{1,0:T(8,128)(2,1)S(1)} %get-tuple-element.43), channel_id=1, source_target_pairs={{0,4},{4,0},{8,12},{12,8},{1,5},{5,1},{9,13},{13,9},{2,6},{6,2},{1... | collective-permute-start | bytes 393224 | tf_op jit(solution)/shard_map/ppermute | solution.py:26
  22.9 10.4 %collective-permute-done.17.refs_11_ = bf16[2,256,512]{2,1,0:T(8,128)(2,1)S(1)} collective-permute-done((bf16[2,256,512]{2,1,0:T(8,128)(2,1)S(1)}, bf16[2,256,512]{2,1,0:T(8,128)(2,1)S(1)}, u32[]{:S(2)}, u32[]{:S(2)}) %collective-permute-start.17) | collective-permute-done | bytes 524320 | tf_op jit(solution)/shard_map/ppermute | solution.py:26
  33.2 1.7 %collective-permute-start.20 = (bf16[128,512]{1,0:T(8,128)(2,1)S(1)}, bf16[128,512]{1,0:T(8,128)(2,1)S(1)}, u32[]{:S(2)}, u32[]{:S(2)}) collective-permute-start(bf16[128,512]{1,0:T(8,128)(2,1)S(1)} %get-tuple-element.44), channel_id=1, source_target_pairs={{0,8},{4,12},{8,0},{12,4},{1,9},{5,13},{9,1},{13,5},{2,10},{6,14},... | collective-permute-start | bytes 393224 | tf_op jit(solution)/shard_map/ppermute | solution.py:26
  35.1 0.3 collective-permute-done.1.refs_2_
  35.4 1.7 %collective-permute-start.2 = (bf16[128,512]{1,0:T(8,128)(2,1)S(1)}, bf16[128,512]{1,0:T(8,128)(2,1)S(1)}, u32[]{:S(2)}, u32[]{:S(2)}) collective-permute-start(bf16[128,512]{1,0:T(8,128)(2,1)S(1)} %get-tuple-element.31), channel_id=1, source_target_pairs={{0,8},{4,12},{8,0},{12,4},{1,9},{5,13},{9,1},{13,5},{2,10},{6,14},... | collective-permute-start | bytes 393224 | tf_op jit(solution)/shard_map/ppermute | solution.py:26
  37.1 1.1 %collective-permute-done.19.refs_2_ = bf16[128,512]{1,0:T(8,128)(2,1)S(1)} collective-permute-done((bf16[128,512]{1,0:T(8,128)(2,1)S(1)}, bf16[128,512]{1,0:T(8,128)(2,1)S(1)}, u32[]{:S(2)}, u32[]{:S(2)}) %collective-permute-start.19) | collective-permute-done | bytes 131104 | tf_op jit(solution)/shard_map/ppermute | solution.py:26
  38.2 2.4 %collective-permute-start.3 = (bf16[128,512]{1,0:T(8,128)(2,1)S(1)}, bf16[128,512]{1,0:T(8,128)(2,1)S(1)}, u32[]{:S(2)}, u32[]{:S(2)}) collective-permute-start(bf16[128,512]{1,0:T(8,128)(2,1)S(1)} %get-tuple-element.32), channel_id=1, source_target_pairs={{0,12},{4,8},{8,4},{12,0},{1,13},{5,9},{9,5},{13,1},{2,14},{6,10},... | collective-permute-start | bytes 393224 | tf_op jit(solution)/shard_map/ppermute | solution.py:26
  40.6 4.3 %collective-permute-done.20.refs_3_ = bf16[128,512]{1,0:T(8,128)(2,1)S(1)} collective-permute-done((bf16[128,512]{1,0:T(8,128)(2,1)S(1)}, bf16[128,512]{1,0:T(8,128)(2,1)S(1)}, u32[]{:S(2)}, u32[]{:S(2)}) %collective-permute-start.20) | collective-permute-done | bytes 131104 | tf_op jit(solution)/shard_map/ppermute | solution.py:26
  45.0 0.5 collective-permute-start.16
  45.5 0.3 shard_map.81
  45.8 0.9 collective-permute-done.2.refs_3_
  46.7 1.6 %collective-permute-start.22 = (bf16[32,1024]{1,0:T(8,128)(2,1)S(1)}, bf16[32,1024]{1,0:T(8,128)(2,1)S(1)}, u32[]{:S(2)}, u32[]{:S(2)}) collective-permute-start(bf16[32,1024]{1,0:T(8,128)(2,1)S(1)} %get-tuple-element.47), channel_id=1, source_target_pairs={{0,1},{1,0},{2,3},{3,2},{4,5},{5,4},{6,7},{7,6},{8,9},{9,8},{10,11... | collective-permute-start | bytes 196616 | tf_op jit(solution)/shard_map/ppermute | solution.py:26
  48.3 2.6 %collective-permute-start.23 = (bf16[32,1024]{1,0:T(8,128)(2,1)S(1)}, bf16[32,1024]{1,0:T(8,128)(2,1)S(1)}, u32[]{:S(2)}, u32[]{:S(2)}) collective-permute-start(bf16[32,1024]{1,0:T(8,128)(2,1)S(1)} %get-tuple-element.48), channel_id=1, source_target_pairs={{0,2},{1,3},{2,0},{3,1},{4,6},{5,7},{6,4},{7,5},{8,10},{9,11},{10,... | collective-permute-start | bytes 196616 | tf_op jit(solution)/shard_map/ppermute | solution.py:26
  50.9 0.7 collective-permute-done.22.refs_3_
  51.6 0.3 shard_map.76
  51.9 2.2 %collective-permute-done.23.refs_4_ = bf16[32,1024]{1,0:T(8,128)(2,1)S(1)} collective-permute-done((bf16[32,1024]{1,0:T(8,128)(2,1)S(1)}, bf16[32,1024]{1,0:T(8,128)(2,1)S(1)}, u32[]{:S(2)}, u32[]{:S(2)}) %collective-permute-start.23) | collective-permute-done | bytes 65568 | tf_op jit(solution)/shard_map/ppermute | solution.py:26
  54.4 4.1 %collective-permute-done.4.refs_2_ = bf16[32,1152]{1,0:T(8,128)(2,1)S(1)} collective-permute-done((bf16[32,1152]{1,0:T(8,128)(2,1)S(1)}, bf16[32,1152]{1,0:T(8,128)(2,1)S(1)}, u32[]{:S(2)}, u32[]{:S(2)}) %collective-permute-start.4) | collective-permute-done | bytes 73760 | tf_op jit(solution)/shard_map/ppermute | solution.py:26
  58.5 2.1 %collective-permute-start.5 = (bf16[32,1152]{1,0:T(8,128)(2,1)S(1)}, bf16[32,1152]{1,0:T(8,128)(2,1)S(1)}, u32[]{:S(2)}, u32[]{:S(2)}) collective-permute-start(bf16[32,1152]{1,0:T(8,128)(2,1)S(1)} %get-tuple-element.37), channel_id=1, source_target_pairs={{0,2},{1,3},{2,0},{3,1},{4,6},{5,7},{6,4},{7,5},{8,10},{9,11},{10,... | collective-permute-start | bytes 221192 | tf_op jit(solution)/shard_map/ppermute | solution.py:26
  60.6 4.4 %collective-permute-done.5.refs_3_ = bf16[32,1152]{1,0:T(8,128)(2,1)S(1)} collective-permute-done((bf16[32,1152]{1,0:T(8,128)(2,1)S(1)}, bf16[32,1152]{1,0:T(8,128)(2,1)S(1)}, u32[]{:S(2)}, u32[]{:S(2)}) %collective-permute-start.5) | collective-permute-done | bytes 73760 | tf_op jit(solution)/shard_map/ppermute | solution.py:26
  65.0 0.8 collective-permute-start.6
  65.8 5.7 %collective-permute-done.6.refs_4_ = bf16[32,1152]{1,0:T(8,128)(2,1)S(1)} collective-permute-done((bf16[32,1152]{1,0:T(8,128)(2,1)S(1)}, bf16[32,1152]{1,0:T(8,128)(2,1)S(1)}, u32[]{:S(2)}, u32[]{:S(2)}) %collective-permute-start.6) | collective-permute-done | bytes 73760 | tf_op jit(solution)/shard_map/ppermute | solution.py:26
  71.5 0.5 collective-permute-start.24
  72.0 0.5 shard_map.78
  72.5 5.4 %collective-permute-done.24.refs_5_ = bf16[32,1024]{1,0:T(8,128)(2,1)S(1)} collective-permute-done((bf16[32,1024]{1,0:T(8,128)(2,1)S(1)}, bf16[32,1024]{1,0:T(8,128)(2,1)S(1)}, u32[]{:S(2)}, u32[]{:S(2)}) %collective-permute-start.24) | collective-permute-done | bytes 65568 | tf_op jit(solution)/shard_map/ppermute | solution.py:26
  77.9 0.5 shard_map.82.refs_3_
  78.5 0.7 collective-permute-start.26
  79.3 3.5 %collective-permute-done.25.refs_4_ = bf16[32,1024]{1,0:T(8,128)(2,1)S(1)} collective-permute-done((bf16[32,1024]{1,0:T(8,128)(2,1)S(1)}, bf16[32,1024]{1,0:T(8,128)(2,1)S(1)}, u32[]{:S(2)}, u32[]{:S(2)}) %collective-permute-start.25) | collective-permute-done | bytes 65568 | tf_op jit(solution)/shard_map/ppermute | solution.py:26
  82.8 1.1 %collective-permute-start.27 = (bf16[32,1024]{1,0:T(8,128)(2,1)S(1)}, bf16[32,1024]{1,0:T(8,128)(2,1)S(1)}, u32[]{:S(2)}, u32[]{:S(2)}) collective-permute-start(bf16[32,1024]{1,0:T(8,128)(2,1)S(1)} %shard_map.82.refs_3_), channel_id=1, source_target_pairs={{0,3},{1,2},{2,1},{3,0},{4,7},{5,6},{6,5},{7,4},{8,11},{9,10},{10,... | collective-permute-start | bytes 196616 | tf_op jit(solution)/shard_map/ppermute | solution.py:26
  83.9 2.5 %collective-permute-done.26.refs_5_ = bf16[32,1024]{1,0:T(8,128)(2,1)S(1)} collective-permute-done((bf16[32,1024]{1,0:T(8,128)(2,1)S(1)}, bf16[32,1024]{1,0:T(8,128)(2,1)S(1)}, u32[]{:S(2)}, u32[]{:S(2)}) %collective-permute-start.26) | collective-permute-done | bytes 65568 | tf_op jit(solution)/shard_map/ppermute | solution.py:26
  86.3 2.5 %collective-permute-done.27.refs_6_ = bf16[32,1024]{1,0:T(8,128)(2,1)S(1)} collective-permute-done((bf16[32,1024]{1,0:T(8,128)(2,1)S(1)}, bf16[32,1024]{1,0:T(8,128)(2,1)S(1)}, u32[]{:S(2)}, u32[]{:S(2)}) %collective-permute-start.27) | collective-permute-done | bytes 65568 | tf_op jit(solution)/shard_map/ppermute | solution.py:26
  88.9 1.9 %collective-permute-start.13 = (bf16[32,1024]{1,0:T(8,128)(2,1)S(1)}, bf16[32,1024]{1,0:T(8,128)(2,1)S(1)}, u32[]{:S(2)}, u32[]{:S(2)}) collective-permute-start(bf16[32,1024]{1,0:T(8,128)(2,1)S(1)} %get-tuple-element.40.refs_3_), channel_id=1, source_target_pairs={{0,3},{1,2},{2,1},{3,0},{4,7},{5,6},{6,5},{7,4},{8,11},{9,10},{10,... | collective-permute-start | bytes 196616 | tf_op jit(solution)/shard_map/ppermute | solution.py:26
  90.7 0.9 shard_map.83
  91.6 2.4 %collective-permute-done.12.refs_5_ = bf16[32,1024]{1,0:T(8,128)(2,1)S(1)} collective-permute-done((bf16[32,1024]{1,0:T(8,128)(2,1)S(1)}, bf16[32,1024]{1,0:T(8,128)(2,1)S(1)}, u32[]{:S(2)}, u32[]{:S(2)}) %collective-permute-start.12) | collective-permute-done | bytes 65568 | tf_op jit(solution)/shard_map/ppermute | solution.py:26
  94.0 1.0 %collective-permute-done.13.refs_6_ = bf16[32,1024]{1,0:T(8,128)(2,1)S(1)} collective-permute-done((bf16[32,1024]{1,0:T(8,128)(2,1)S(1)}, bf16[32,1024]{1,0:T(8,128)(2,1)S(1)}, u32[]{:S(2)}, u32[]{:S(2)}) %collective-permute-start.13) | collective-permute-done | bytes 65568 | tf_op jit(solution)/shard_map/ppermute | solution.py:26
  95.0 0.9 shard_map.80
  95.9 1.0 %shard_map.84.refs_0_ = bf16[256,1024]{1,0:T(8,128)(2,1)} custom-call(bf16[1024,1024]{1,0:T(8,128)(2,1)S(1)} %copy-done, f32[128,1024]{1,0:T(8,128)S(1)} %get-tuple-element.41.refs_1_.refs_2_, f32[128,1024]{1,0:T(8,128)S(1)} %get-tuple-element.50.refs_2_.refs_3_, bf16[2,128,256]{2,1,0:T(8,128)(2,1)S(1)} %get-tuple-element.51.refs_3_.refs_4_, ...), custom_call_target="tpu_custom_call" | custom-call | tf_op jit(solution)/shard_map/pallas_call | solution.py:40
  97.0 1.0 %shard_map.85 = bf16[256,1024]{1,0:T(8,128)(2,1)} custom-call(bf16[256,1024]{1,0:T(8,128)(2,1)} %shard_map.84.refs_0_, bf16[1024,1024]{1,0:T(8,128)(2,1)S(1)} %copy-done, f32[128,1024]{1,0:T(8,128)S(1)} %get-tuple-element.41.refs_1_.refs_2_, f32[128,1024]{1,0:T(8,128)S(1)} %get-tuple-element.50.refs_2_.refs_3_, ...), custom_call_target="tpu_custom_call", output_to_operand_aliasing={{}: (0, {})} | custom-call | tf_op jit(solution)/shard_map/pallas_call | solution.py:40
  (39 shorter events, 1.0 us)
Async XLA Ops:
  0.0 7.8 %collective-permute-start.7 = (bf16[2,128,256]{2,1,0:T(8,128)(2,1)}, bf16[2,128,256]{2,1,0:T(8,128)(2,1)S(1)}, u32[]{:S(2)}, u32[]{:S(2)}) collective-permute-start(bf16[2,128,256]{2,1,0:T(8,128)(2,1)} %refs_0_.7), channel_id=1, source_target_pairs={{0,4},{4,0},{8,12},{12,8},{1,5},{5,1},{9,13},{13,9},{2,6},{6,2},{1... | collective-permute-start | bytes 393224 | tf_op jit(solution)/shard_map/ppermute | solution.py:26
  3.0 8.0 %collective-permute-start.8 = (bf16[2,128,256]{2,1,0:T(8,128)(2,1)}, bf16[2,128,256]{2,1,0:T(8,128)(2,1)S(1)}, u32[]{:S(2)}, u32[]{:S(2)}) collective-permute-start(bf16[2,128,256]{2,1,0:T(8,128)(2,1)} %refs_0_.7), channel_id=1, source_target_pairs={{0,8},{4,12},{8,0},{12,4},{1,9},{5,13},{9,1},{13,5},{2,10},{6,14},... | collective-permute-start | bytes 393224 | tf_op jit(solution)/shard_map/ppermute | solution.py:26
  4.5 8.1 %collective-permute-start.9 = (bf16[2,128,256]{2,1,0:T(8,128)(2,1)}, bf16[2,128,256]{2,1,0:T(8,128)(2,1)S(1)}, u32[]{:S(2)}, u32[]{:S(2)}) collective-permute-start(bf16[2,128,256]{2,1,0:T(8,128)(2,1)} %refs_0_.7), channel_id=1, source_target_pairs={{0,12},{4,8},{8,4},{12,0},{1,13},{5,9},{9,5},{13,1},{2,14},{6,10},... | collective-permute-start | bytes 393224 | tf_op jit(solution)/shard_map/ppermute | solution.py:26
  4.5 8.3 %collective-permute-start = (bf16[2,512,256]{2,1,0:T(8,128)(2,1)}, bf16[2,512,256]{2,1,0:T(8,128)(2,1)S(1)}, u32[]{:S(2)}, u32[]{:S(2)}) collective-permute-start(bf16[2,512,256]{2,1,0:T(8,128)(2,1)} %refs_1_.4), channel_id=1, source_target_pairs={{0,16},{16,0},{1,17},{17,1},{2,18},{18,2},{3,19},{19,3},{4,20},{20... | collective-permute-start | bytes 1572872 | tf_op jit(solution)/shard_map/ppermute | solution.py:369
  4.5 1.0 %copy-start.2 = (bf16[2,512,256]{2,1,0:T(8,128)(2,1)S(1)}, bf16[2,512,256]{2,1,0:T(8,128)(2,1)}, u32[]{:S(2)}) copy-start(bf16[2,512,256]{2,1,0:T(8,128)(2,1)} %refs_0_.8) | copy-start | bytes 1572868
  5.7 6.8 %copy-start.3 = (bf16[2,128,256]{2,1,0:T(8,128)(2,1)S(1)}, bf16[2,128,256]{2,1,0:T(8,128)(2,1)}, u32[]{:S(2)}) copy-start(bf16[2,128,256]{2,1,0:T(8,128)(2,1)} %refs_0_.7) | copy-start | bytes 393220
  5.7 7.1 %copy-start = (bf16[1024,1024]{1,0:T(8,128)(2,1)S(1)}, bf16[1024,1024]{1,0:T(8,128)(2,1)}, u32[]{:S(2)}) copy-start(bf16[1024,1024]{1,0:T(8,128)(2,1)} %refs_1_.5) | copy-start | bytes 6291460
  5.8 7.1 %copy-start.5 = (bf16[2,512,256]{2,1,0:T(8,128)(2,1)S(1)}, bf16[2,512,256]{2,1,0:T(8,128)(2,1)}, u32[]{:S(2)}) copy-start(bf16[2,512,256]{2,1,0:T(8,128)(2,1)} %refs_1_.4) | copy-start | bytes 1572868
  5.8 7.1 %copy-start.6 = (bf16[1024,8]{0,1:T(8,128)(2,1)S(1)}, bf16[1024,8]{0,1:T(8,128)(2,1)}, u32[]{:S(2)}) copy-start(bf16[1024,8]{0,1:T(8,128)(2,1)} %param.9) | copy-start | bytes 49156
  5.8 15.5 %collective-permute-start.15 = (bf16[2,256,512]{2,1,0:T(8,128)(2,1)S(1)}, bf16[2,256,512]{2,1,0:T(8,128)(2,1)S(1)}, u32[]{:S(2)}, u32[]{:S(2)}) collective-permute-start(bf16[2,256,512]{2,1,0:T(8,128)(2,1)S(1)} %shard_map.79.refs_7_), channel_id=1, source_target_pairs={{0,4},{4,0},{8,12},{12,8},{1,5},{5,1},{9,13},{13,9},{2,6},{6,2},{1... | collective-permute-start | bytes 1572872 | tf_op jit(solution)/shard_map/ppermute | solution.py:26
  7.8 25.4 %collective-permute-start.17 = (bf16[2,256,512]{2,1,0:T(8,128)(2,1)S(1)}, bf16[2,256,512]{2,1,0:T(8,128)(2,1)S(1)}, u32[]{:S(2)}, u32[]{:S(2)}) collective-permute-start(bf16[2,256,512]{2,1,0:T(8,128)(2,1)S(1)} %shard_map.79.refs_7_), channel_id=1, source_target_pairs={{0,8},{4,12},{8,0},{12,4},{1,9},{5,13},{9,1},{13,5},{2,10},{6,14},... | collective-permute-start | bytes 1572872 | tf_op jit(solution)/shard_map/ppermute | solution.py:26
  11.0 24.0 %collective-permute-start.28 = (bf16[2,256,512]{2,1,0:T(8,128)(2,1)S(1)}, bf16[2,256,512]{2,1,0:T(8,128)(2,1)S(1)}, u32[]{:S(2)}, u32[]{:S(2)}) collective-permute-start(bf16[2,256,512]{2,1,0:T(8,128)(2,1)S(1)} %shard_map.79.refs_7_), channel_id=1, source_target_pairs={{0,12},{4,8},{8,4},{12,0},{1,13},{5,9},{9,5},{13,1},{2,14},{6,10},... | collective-permute-start | bytes 1572872 | tf_op jit(solution)/shard_map/ppermute | solution.py:26
  12.7 38.1 %collective-permute-start.10 = (bf16[8,256,128]{2,1,0:T(8,128)(2,1)S(1)}, bf16[8,256,128]{2,1,0:T(8,128)(2,1)S(1)}, u32[]{:S(2)}, u32[]{:S(2)}) collective-permute-start(bf16[8,256,128]{2,1,0:T(8,128)(2,1)S(1)} %shard_map.77.refs_5_.refs_6_), channel_id=1, source_target_pairs={{0,16},{16,0},{1,17},{17,1},{2,18},{18,2},{3,19},{19,3},{4,20},{20... | collective-permute-start | bytes 1572872 | tf_op jit(solution)/shard_map/ppermute | solution.py:369
  13.6 31.8 %copy-start.1 = (s32[1024,4]{0,1:T(4,128)S(1)}, s32[1024,4]{0,1:T(4,128)}, u32[]{:S(2)}) copy-start(s32[1024,4]{0,1:T(4,128)} %param.8) | copy-start | bytes 49156
  13.6 21.7 %collective-permute-start.1 = (bf16[128,512]{1,0:T(8,128)(2,1)S(1)}, bf16[128,512]{1,0:T(8,128)(2,1)S(1)}, u32[]{:S(2)}, u32[]{:S(2)}) collective-permute-start(bf16[128,512]{1,0:T(8,128)(2,1)S(1)} %get-tuple-element.30), channel_id=1, source_target_pairs={{0,4},{4,0},{8,12},{12,8},{1,5},{5,1},{9,13},{13,9},{2,6},{6,2},{1... | collective-permute-start | bytes 393224 | tf_op jit(solution)/shard_map/ppermute | solution.py:26
  16.2 74.6 %copy-start.4 = (f32[1024]{0:T(1024)S(1)}, f32[1024]{0:T(1024)}, u32[]{:S(2)}) copy-start(f32[1024]{0:T(1024)} %param.13) | copy-start | bytes 12292
  21.3 16.9 %collective-permute-start.19 = (bf16[128,512]{1,0:T(8,128)(2,1)S(1)}, bf16[128,512]{1,0:T(8,128)(2,1)S(1)}, u32[]{:S(2)}, u32[]{:S(2)}) collective-permute-start(bf16[128,512]{1,0:T(8,128)(2,1)S(1)} %get-tuple-element.43), channel_id=1, source_target_pairs={{0,4},{4,0},{8,12},{12,8},{1,5},{5,1},{9,13},{13,9},{2,6},{6,2},{1... | collective-permute-start | bytes 393224 | tf_op jit(solution)/shard_map/ppermute | solution.py:26
  33.2 11.7 %collective-permute-start.20 = (bf16[128,512]{1,0:T(8,128)(2,1)S(1)}, bf16[128,512]{1,0:T(8,128)(2,1)S(1)}, u32[]{:S(2)}, u32[]{:S(2)}) collective-permute-start(bf16[128,512]{1,0:T(8,128)(2,1)S(1)} %get-tuple-element.44), channel_id=1, source_target_pairs={{0,8},{4,12},{8,0},{12,4},{1,9},{5,13},{9,1},{13,5},{2,10},{6,14},... | collective-permute-start | bytes 393224 | tf_op jit(solution)/shard_map/ppermute | solution.py:26
  34.9 10.0 %collective-permute-start.21 = (bf16[128,512]{1,0:T(8,128)(2,1)S(1)}, bf16[128,512]{1,0:T(8,128)(2,1)S(1)}, u32[]{:S(2)}, u32[]{:S(2)}) collective-permute-start(bf16[128,512]{1,0:T(8,128)(2,1)S(1)} %get-tuple-element.45), channel_id=1, source_target_pairs={{0,12},{4,8},{8,4},{12,0},{1,13},{5,9},{9,5},{13,1},{2,14},{6,10},... | collective-permute-start | bytes 393224 | tf_op jit(solution)/shard_map/ppermute | solution.py:26
  35.4 11.3 %collective-permute-start.2 = (bf16[128,512]{1,0:T(8,128)(2,1)S(1)}, bf16[128,512]{1,0:T(8,128)(2,1)S(1)}, u32[]{:S(2)}, u32[]{:S(2)}) collective-permute-start(bf16[128,512]{1,0:T(8,128)(2,1)S(1)} %get-tuple-element.31), channel_id=1, source_target_pairs={{0,8},{4,12},{8,0},{12,4},{1,9},{5,13},{9,1},{13,5},{2,10},{6,14},... | collective-permute-start | bytes 393224 | tf_op jit(solution)/shard_map/ppermute | solution.py:26
  38.2 10.1 %collective-permute-start.3 = (bf16[128,512]{1,0:T(8,128)(2,1)S(1)}, bf16[128,512]{1,0:T(8,128)(2,1)S(1)}, u32[]{:S(2)}, u32[]{:S(2)}) collective-permute-start(bf16[128,512]{1,0:T(8,128)(2,1)S(1)} %get-tuple-element.32), channel_id=1, source_target_pairs={{0,12},{4,8},{8,4},{12,0},{1,13},{5,9},{9,5},{13,1},{2,14},{6,10},... | collective-permute-start | bytes 393224 | tf_op jit(solution)/shard_map/ppermute | solution.py:26
  44.9 33.6 %collective-permute-start.14 = (bf16[2,256,512]{2,1,0:T(8,128)(2,1)S(1)}, bf16[2,256,512]{2,1,0:T(8,128)(2,1)S(1)}, u32[]{:S(2)}, u32[]{:S(2)}) collective-permute-start(bf16[2,256,512]{2,1,0:T(8,128)(2,1)S(1)} %shard_map.79.refs_7_), channel_id=1, source_target_pairs={{0,16},{16,0},{1,17},{17,1},{2,18},{18,2},{3,19},{19,3},{4,20},{20... | collective-permute-start | bytes 1572872 | tf_op jit(solution)/shard_map/ppermute | solution.py:369
  45.0 43.9 %collective-permute-start.16 = (bf16[2,256,512]{2,1,0:T(8,128)(2,1)S(1)}, bf16[2,256,512]{2,1,0:T(8,128)(2,1)S(1)}, u32[]{:S(2)}, u32[]{:S(2)}) collective-permute-start(bf16[2,256,512]{2,1,0:T(8,128)(2,1)S(1)} %collective-permute-done.15.refs_9_), channel_id=1, source_target_pairs={{0,16},{16,0},{1,17},{17,1},{2,18},{18,2},{3,19},{19,3},{4,20},{20... | collective-permute-start | bytes 1572872 | tf_op jit(solution)/shard_map/ppermute | solution.py:369
  46.7 4.9 %collective-permute-start.22 = (bf16[32,1024]{1,0:T(8,128)(2,1)S(1)}, bf16[32,1024]{1,0:T(8,128)(2,1)S(1)}, u32[]{:S(2)}, u32[]{:S(2)}) collective-permute-start(bf16[32,1024]{1,0:T(8,128)(2,1)S(1)} %get-tuple-element.47), channel_id=1, source_target_pairs={{0,1},{1,0},{2,3},{3,2},{4,5},{5,4},{6,7},{7,6},{8,9},{9,8},{10,11... | collective-permute-start | bytes 196616 | tf_op jit(solution)/shard_map/ppermute | solution.py:26
  48.3 5.9 %collective-permute-start.23 = (bf16[32,1024]{1,0:T(8,128)(2,1)S(1)}, bf16[32,1024]{1,0:T(8,128)(2,1)S(1)}, u32[]{:S(2)}, u32[]{:S(2)}) collective-permute-start(bf16[32,1024]{1,0:T(8,128)(2,1)S(1)} %get-tuple-element.48), channel_id=1, source_target_pairs={{0,2},{1,3},{2,0},{3,1},{4,6},{5,7},{6,4},{7,5},{8,10},{9,11},{10,... | collective-permute-start | bytes 196616 | tf_op jit(solution)/shard_map/ppermute | solution.py:26
  50.9 39.9 %collective-permute-start.18 = (bf16[2,256,512]{2,1,0:T(8,128)(2,1)S(1)}, bf16[2,256,512]{2,1,0:T(8,128)(2,1)S(1)}, u32[]{:S(2)}, u32[]{:S(2)}) collective-permute-start(bf16[2,256,512]{2,1,0:T(8,128)(2,1)S(1)} %collective-permute-done.17.refs_11_), channel_id=1, source_target_pairs={{0,16},{16,0},{1,17},{17,1},{2,18},{18,2},{3,19},{19,3},{4,20},{20... | collective-permute-start | bytes 1572872 | tf_op jit(solution)/shard_map/ppermute | solution.py:369
  51.6 45.4 %collective-permute-start.29 = (bf16[2,256,512]{2,1,0:T(8,128)(2,1)S(1)}, bf16[2,256,512]{2,1,0:T(8,128)(2,1)S(1)}, u32[]{:S(2)}, u32[]{:S(2)}) collective-permute-start(bf16[2,256,512]{2,1,0:T(8,128)(2,1)S(1)} %collective-permute-done.28.refs_5_), channel_id=1, source_target_pairs={{0,16},{16,0},{1,17},{17,1},{2,18},{18,2},{3,19},{19,3},{4,20},{20... | collective-permute-start | bytes 1572872 | tf_op jit(solution)/shard_map/ppermute | solution.py:369
  54.2 4.4 %collective-permute-start.4 = (bf16[32,1152]{1,0:T(8,128)(2,1)S(1)}, bf16[32,1152]{1,0:T(8,128)(2,1)S(1)}, u32[]{:S(2)}, u32[]{:S(2)}) collective-permute-start(bf16[32,1152]{1,0:T(8,128)(2,1)S(1)} %get-tuple-element.36), channel_id=1, source_target_pairs={{0,1},{1,0},{2,3},{3,2},{4,5},{5,4},{6,7},{7,6},{8,9},{9,8},{10,11... | collective-permute-start | bytes 221192 | tf_op jit(solution)/shard_map/ppermute | solution.py:26
  58.5 6.5 %collective-permute-start.5 = (bf16[32,1152]{1,0:T(8,128)(2,1)S(1)}, bf16[32,1152]{1,0:T(8,128)(2,1)S(1)}, u32[]{:S(2)}, u32[]{:S(2)}) collective-permute-start(bf16[32,1152]{1,0:T(8,128)(2,1)S(1)} %get-tuple-element.37), channel_id=1, source_target_pairs={{0,2},{1,3},{2,0},{3,1},{4,6},{5,7},{6,4},{7,5},{8,10},{9,11},{10,... | collective-permute-start | bytes 221192 | tf_op jit(solution)/shard_map/ppermute | solution.py:26
  65.0 6.5 %collective-permute-start.6 = (bf16[32,1152]{1,0:T(8,128)(2,1)S(1)}, bf16[32,1152]{1,0:T(8,128)(2,1)S(1)}, u32[]{:S(2)}, u32[]{:S(2)}) collective-permute-start(bf16[32,1152]{1,0:T(8,128)(2,1)S(1)} %get-tuple-element.38), channel_id=1, source_target_pairs={{0,3},{1,2},{2,1},{3,0},{4,7},{5,6},{6,5},{7,4},{8,11},{9,10},{10,... | collective-permute-start | bytes 221192 | tf_op jit(solution)/shard_map/ppermute | solution.py:26
  71.5 6.4 %collective-permute-start.24 = (bf16[32,1024]{1,0:T(8,128)(2,1)S(1)}, bf16[32,1024]{1,0:T(8,128)(2,1)S(1)}, u32[]{:S(2)}, u32[]{:S(2)}) collective-permute-start(bf16[32,1024]{1,0:T(8,128)(2,1)S(1)} %get-tuple-element.49), channel_id=1, source_target_pairs={{0,3},{1,2},{2,1},{3,0},{4,7},{5,6},{6,5},{7,4},{8,11},{9,10},{10,... | collective-permute-start | bytes 196616 | tf_op jit(solution)/shard_map/ppermute | solution.py:26
  78.4 4.3 %collective-permute-start.25 = (bf16[32,1024]{1,0:T(8,128)(2,1)S(1)}, bf16[32,1024]{1,0:T(8,128)(2,1)S(1)}, u32[]{:S(2)}, u32[]{:S(2)}) collective-permute-start(bf16[32,1024]{1,0:T(8,128)(2,1)S(1)} %shard_map.82.refs_3_), channel_id=1, source_target_pairs={{0,1},{1,0},{2,3},{3,2},{4,5},{5,4},{6,7},{7,6},{8,9},{9,8},{10,11... | collective-permute-start | bytes 196616 | tf_op jit(solution)/shard_map/ppermute | solution.py:26
  78.5 7.8 %collective-permute-start.26 = (bf16[32,1024]{1,0:T(8,128)(2,1)S(1)}, bf16[32,1024]{1,0:T(8,128)(2,1)S(1)}, u32[]{:S(2)}, u32[]{:S(2)}) collective-permute-start(bf16[32,1024]{1,0:T(8,128)(2,1)S(1)} %shard_map.82.refs_3_), channel_id=1, source_target_pairs={{0,2},{1,3},{2,0},{3,1},{4,6},{5,7},{6,4},{7,5},{8,10},{9,11},{10,... | collective-permute-start | bytes 196616 | tf_op jit(solution)/shard_map/ppermute | solution.py:26
  82.8 6.1 %collective-permute-start.27 = (bf16[32,1024]{1,0:T(8,128)(2,1)S(1)}, bf16[32,1024]{1,0:T(8,128)(2,1)S(1)}, u32[]{:S(2)}, u32[]{:S(2)}) collective-permute-start(bf16[32,1024]{1,0:T(8,128)(2,1)S(1)} %shard_map.82.refs_3_), channel_id=1, source_target_pairs={{0,3},{1,2},{2,1},{3,0},{4,7},{5,6},{6,5},{7,4},{8,11},{9,10},{10,... | collective-permute-start | bytes 196616 | tf_op jit(solution)/shard_map/ppermute | solution.py:26
  86.3 5.3 %collective-permute-start.11 = (bf16[32,1024]{1,0:T(8,128)(2,1)S(1)}, bf16[32,1024]{1,0:T(8,128)(2,1)S(1)}, u32[]{:S(2)}, u32[]{:S(2)}) collective-permute-start(bf16[32,1024]{1,0:T(8,128)(2,1)S(1)} %get-tuple-element.40.refs_3_), channel_id=1, source_target_pairs={{0,1},{1,0},{2,3},{3,2},{4,5},{5,4},{6,7},{7,6},{8,9},{9,8},{10,11... | collective-permute-start | bytes 196616 | tf_op jit(solution)/shard_map/ppermute | solution.py:26
  88.8 5.2 %collective-permute-start.12 = (bf16[32,1024]{1,0:T(8,128)(2,1)S(1)}, bf16[32,1024]{1,0:T(8,128)(2,1)S(1)}, u32[]{:S(2)}, u32[]{:S(2)}) collective-permute-start(bf16[32,1024]{1,0:T(8,128)(2,1)S(1)} %get-tuple-element.40.refs_3_), channel_id=1, source_target_pairs={{0,2},{1,3},{2,0},{3,1},{4,6},{5,7},{6,4},{7,5},{8,10},{9,11},{10,... | collective-permute-start | bytes 196616 | tf_op jit(solution)/shard_map/ppermute | solution.py:26
  88.9 6.2 %collective-permute-start.13 = (bf16[32,1024]{1,0:T(8,128)(2,1)S(1)}, bf16[32,1024]{1,0:T(8,128)(2,1)S(1)}, u32[]{:S(2)}, u32[]{:S(2)}) collective-permute-start(bf16[32,1024]{1,0:T(8,128)(2,1)S(1)} %get-tuple-element.40.refs_3_), channel_id=1, source_target_pairs={{0,3},{1,2},{2,1},{3,0},{4,7},{5,6},{6,5},{7,4},{8,11},{9,10},{10,... | collective-permute-start | bytes 196616 | tf_op jit(solution)/shard_map/ppermute | solution.py:26

commit v4 on v3

--- a/solution.py
+++ b/solution.py
@@ -66,14 +66,24 @@
     return call(body, [], [((8, 128), jnp.int32)], flops=6_000_000_000)[0]
 
 
-def project(x, pieces, gate_t, begun, h, n_row, n_expert, pair):
+def project(x, pieces, gate_t, begun, h, n_row, n_expert, pair, relayed=()):
     n_loc, width, rank = pieces[0].shape
     n_piece = len(pieces)
+    n_relay = len(relayed)
+    more = {m: mid.shape[1] // n_loc for m, mid in relayed}
     block = n_row * SPLIT
 
     def body(place_ref, x_ref, *refs):
         w_refs, g_ref = refs[:n_piece], refs[n_piece]
-        logit_ref, *outs = refs[n_piece + 2 :]
+        mid_refs = refs[n_piece + 2 : n_piece + 2 + n_relay]
+        logit_ref, *outs = refs[n_piece + 2 + n_relay :]
+        for (m, _), mid_ref in zip(relayed, mid_refs):
+            for k, e in enumerate(relayed_by(m, n_loc)):
+                at = n_row + k * more[m]
+                for c in range(n_loc):
+                    outs[m][at : at + more[m], c * rank : (c + 1) * rank] = mid_ref[
+                        e, c * more[m] : (c + 1) * more[m], :
+                    ]
         first = [place_ref[0], 1 - place_ref[0]] if pair else [0]
         starts = [
             peer_to(place_ref[1], m, n_expert) * block + h * n_row for m in range(n_expert)
@@ -88,7 +98,7 @@
                 acc = acc + jnp.dot(xs[p], w_refs[p][e], preferred_element_type=F32)
             acc = acc.astype(BF16)
             for m in range(n_expert):
-                outs[m][:, e * rank : (e + 1) * rank] = acc[m * n_row : (m + 1) * n_row]
+                outs[m][:n_row, e * rank : (e + 1) * rank] = acc[m * n_row : (m + 1) * n_row]
         logit = None
         for p in range(n_piece):
             gate = g_ref[:, rows_at(first[p] * width, width)]
@@ -98,8 +108,12 @@
 
     return call(
         body,
-        [x, *pieces, gate_t, begun],
-        [((gate_t.shape[0], n_row), F32)] + [((n_row, n_loc * rank), BF16)] * n_expert,
+        [x, *pieces, gate_t, begun] + [mid for _, mid in relayed],
+        [((gate_t.shape[0], n_row), F32)]
+        + [
+            ((n_row + more.get(m, 0) * len(relayed_by(m, n_loc)), n_loc * rank), BF16)
+            for m in range(n_expert)
+        ],
         flops=3_000_000_000,
     )
 
@@ -114,15 +128,25 @@
     return call(body, [wide], [((n_loc, rank, half), BF16)])[0]
 
 
-def turn(mids):
+def turn(mids, relayed, n_row):
     n_loc, half, rank = mids[0].shape
+    n = len(mids)
+    more = half // n_loc
 
     def body(place_ref, *refs):
-        for q in range(len(mids)):
+        out_ref = refs[-1]
+        for q in range(n):
             for e in range(n_loc):
-                refs[-1][q * n_loc + e] = refs[q][e].T
-
-    return call(body, [*mids], [((len(mids) * n_loc, rank, half), BF16)])[0]
+                out_ref[q * n_loc + e] = refs[q][e].T
+        for m in range(1, len(relayed) + 1):
+            part = refs[n + m - 1]
+            for k, e in enumerate(relayed_by(m, n_loc)):
+                at = n_row + k * more
+                rows = [part[at : at + more, c * rank : (c + 1) * rank] for c in range(n_loc)]
+                out_ref[n * n_loc + e] = jnp.concatenate(rows, axis=0).T
+
+    count = n * n_loc + (n_loc if relayed else 0)
+    return call(body, [*mids, *relayed], [((count, rank, half), BF16)])[0]
 
 
 def wide_ids(ids_ref, start, n, width):
@@ -154,7 +178,7 @@
                 for e in range(n_loc):
                     number = (base + e).astype(F32).astype(BF16)
                     acc = jnp.where(
-                        ids[j] == number, p_refs[q][:, e * rank : (e + 1) * rank], acc
+                        ids[j] == number, p_refs[q][:rows, e * rank : (e + 1) * rank], acc
                     )
             scratch[:, j * rank : (j + 1) * rank] = acc
         for m in range(n_dim):
@@ -355,6 +379,14 @@
     )[0]
 
 
+def relays(ne):
+    return ne == 4
+
+
+def relayed_by(m, n_loc):
+    return [e for e in range(n_loc) if e % 2 == m - 1]
+
+
 def on_device(
     nb, ne, nz, inputs, expert_ids, gate_weight, reduce_weight, middle_weight, expand_weight, bias
 ):
@@ -379,16 +411,21 @@
     far = list(range(1, ne))
     begun = begin()
     gate_t = gate_weight.T
-    mids = [middle_weight] + [send(middle_weight, "expert", m, ne) for m in far]
+    near = far[:-1] if relays(ne) else far
+    mids = [middle_weight] + [send(middle_weight, "expert", m, ne) for m in near]
     own, parts, logits = [], [], []
     for h in range(SPLIT):
-        logit, mine, *sent = project(inputs, pieces, gate_t, begun, h, n_row, ne, pair)
+        last = h == SPLIT - 1 and relays(ne)
+        logit, mine, *sent = project(
+            inputs, pieces, gate_t, begun, h, n_row, ne, pair,
+            [(m, mids[ne - 1 - m]) for m in near] if last else (),
+        )
         own.append(mine)
         logits.append(logit)
         parts.append([send(s, "expert", m, ne) for s, m in zip(sent, far)])
     wide = widen(expand_weight)
     wides = [wide] + [send(wide, "expert", m, ne) for m in far]
-    mids = [turn(mids)]
+    mids = [turn(mids, parts[-1][: len(near)] if relays(ne) else [], n_row)]
     if pair:
         mids.append(swap(mids[0]))
 
@@ -404,7 +441,7 @@
         gates_t = made[0] if made else gates_t
         hids.append([hid] + [send(hid, "dim", m, nz) for m in range(1, nz)])
     wides = [[w] + ([swap(w)] if pair else []) for w in wides]
-    n_src = max(1, ne - 1)
+    n_src = (ne + 1) // 2
     sums, lefts = [], []
     for h in range(SPLIT):
         total, left = expand(

time: 98.2 us -> 89.5 us (0.911)
  waiting for transfers between devices: 58.3 us -> 54.3 us
  starting transfers between devices: 31.1 us -> 27.6 us
  local copies, waits for them, and re-layouts: 1.08 us -> 0.03 us
    ppermute x24 -> x23, waiting for transfers between devices: 58.2 us -> 52.1 us  [send(): return lax.ppermute(x, axis, [(i, peer_to(i, m, n)) for i in range(n)])]
    ppermute x24 -> x23, starting transfers between devices: 30.5 us -> 27 us  [send(): return lax.ppermute(x, axis, [(i, peer_to(i, m, n)) for i in range(n)])]
    ppermute x6, waiting for transfers between devices: 0.02 us -> 2.13 us  [swap(): return lax.ppermute(w, 'batch', [(0, 1), (1, 0)])]
    unnamed x14, local copies, waits for them, and re-layouts: 1.08 us -> 0.03 us
  transfers between devices with their start and end apart: 30 -> 29, of which waited for: 18 -> 13; matrix products, arithmetic and copies ran while one was open for 0% -> 0% of each run, Pallas kernels for 6% -> 7%
where the time goes in v4:
time: 89.5 us; the launch traced here: 89.3 us
  waiting for transfers between devices  54.3 us (61%)
  starting transfers between devices  27.6 us (31%)
  Pallas kernels  7.25 us (8%)
    ppermute x23, waiting for transfers between devices, send(): return lax.ppermute(x, axis, [(i, peer_to(i, m, n)) for i in range(n)])  52.1 us
    ppermute x23, starting transfers between devices, send(): return lax.ppermute(x, axis, [(i, peer_to(i, m, n)) for i in range(n)])  27 us
    pallas_call x13, Pallas kernels, call(): pl.pallas_call(placed, in_specs=[space(k) for k in range(len(args))], out...  7.25 us
    ppermute x6, waiting for transfers between devices, swap(): return lax.ppermute(w, 'batch', [(0, 1), (1, 0)])  2.13 us
  transfers between devices with their start and end apart: 29, of which 13 were waited for; matrix products, arithmetic and copies ran while one was open for 0% of the time, Pallas kernels for 7%

profile of v4, /device:TPU:0, one launch (start us, length us, event | category | flops | bytes accessed | tf_op | source)
XLA Modules:
  0.0 89.3 jit_solution(4884247426947516671)
XLA Ops:
  0.0 3.1 %collective-permute-start.4 = (bf16[2,128,256]{2,1,0:T(8,128)(2,1)}, bf16[2,128,256]{2,1,0:T(8,128)(2,1)S(1)}, u32[]{:S(2)}, u32[]{:S(2)}) collective-permute-start(bf16[2,128,256]{2,1,0:T(8,128)(2,1)} %refs_0_.7), channel_id=1, source_target_pairs={{0,8},{4,12},{8,0},{12,4},{1,9},{5,13},{9,1},{13,5},{2,10},{6,14},... | collective-permute-start | bytes 393224 | tf_op jit(solution)/shard_map/ppermute | solution.py:26
  3.1 1.5 %collective-permute-start.5 = (bf16[2,128,256]{2,1,0:T(8,128)(2,1)}, bf16[2,128,256]{2,1,0:T(8,128)(2,1)S(1)}, u32[]{:S(2)}, u32[]{:S(2)}) collective-permute-start(bf16[2,128,256]{2,1,0:T(8,128)(2,1)} %refs_0_.7), channel_id=1, source_target_pairs={{0,4},{4,0},{8,12},{12,8},{1,5},{5,1},{9,13},{13,9},{2,6},{6,2},{1... | collective-permute-start | bytes 393224 | tf_op jit(solution)/shard_map/ppermute | solution.py:26
  4.6 2.1 %collective-permute-done.refs_2_ = bf16[2,512,256]{2,1,0:T(8,128)(2,1)S(1)} collective-permute-done((bf16[2,512,256]{2,1,0:T(8,128)(2,1)}, bf16[2,512,256]{2,1,0:T(8,128)(2,1)S(1)}, u32[]{:S(2)}, u32[]{:S(2)}) %collective-permute-start) | collective-permute-done | bytes 524320 | tf_op jit(solution)/shard_map/ppermute | solution.py:401
  6.7 0.8 shard_map.74
  7.5 0.6 collective-permute-start.1
  8.1 0.2 shard_map.79.refs_7_
  8.3 1.6 %collective-permute-start.16 = (bf16[2,256,512]{2,1,0:T(8,128)(2,1)S(1)}, bf16[2,256,512]{2,1,0:T(8,128)(2,1)S(1)}, u32[]{:S(2)}, u32[]{:S(2)}) collective-permute-start(bf16[2,256,512]{2,1,0:T(8,128)(2,1)S(1)} %shard_map.79.refs_7_), channel_id=1, source_target_pairs={{0,4},{4,0},{8,12},{12,8},{1,5},{5,1},{9,13},{13,9},{2,6},{6,2},{1... | collective-permute-start | bytes 1572872 | tf_op jit(solution)/shard_map/ppermute | solution.py:26
  9.8 0.5 collective-permute-start.25
  10.3 1.5 %collective-permute-start.26 = (bf16[2,256,512]{2,1,0:T(8,128)(2,1)S(1)}, bf16[2,256,512]{2,1,0:T(8,128)(2,1)S(1)}, u32[]{:S(2)}, u32[]{:S(2)}) collective-permute-start(bf16[2,256,512]{2,1,0:T(8,128)(2,1)S(1)} %shard_map.79.refs_7_), channel_id=1, source_target_pairs={{0,12},{4,8},{8,4},{12,0},{1,13},{5,9},{9,5},{13,1},{2,14},{6,10},... | collective-permute-start | bytes 1572872 | tf_op jit(solution)/shard_map/ppermute | solution.py:26
  11.8 0.2 collective-permute-start.2
  12.0 1.9 %collective-permute-done.1.refs_2_ = bf16[128,512]{1,0:T(8,128)(2,1)S(1)} collective-permute-done((bf16[128,512]{1,0:T(8,128)(2,1)S(1)}, bf16[128,512]{1,0:T(8,128)(2,1)S(1)}, u32[]{:S(2)}, u32[]{:S(2)}) %collective-permute-start.1) | collective-permute-done | bytes 131104 | tf_op jit(solution)/shard_map/ppermute | solution.py:26
  13.9 0.9 collective-permute-start.3
  14.8 0.8 shard_map.75
  15.6 24.5 %collective-permute-done.2.refs_3_ = bf16[128,512]{1,0:T(8,128)(2,1)S(1)} collective-permute-done((bf16[128,512]{1,0:T(8,128)(2,1)S(1)}, bf16[128,512]{1,0:T(8,128)(2,1)S(1)}, u32[]{:S(2)}, u32[]{:S(2)}) %collective-permute-start.2) | collective-permute-done | bytes 131104 | tf_op jit(solution)/shard_map/ppermute | solution.py:26
  40.1 0.5 collective-permute-start.10
  40.6 0.5 collective-permute-start.9
  41.1 4.7 %collective-permute-done.10.refs_4_.refs_3_ = bf16[192,512]{1,0:T(8,128)(2,1)S(1)} collective-permute-done((bf16[192,512]{1,0:T(8,128)(2,1)S(1)}, bf16[192,512]{1,0:T(8,128)(2,1)S(1)}, u32[]{:S(2)}, u32[]{:S(2)}) %collective-permute-start.10) | collective-permute-done | bytes 196640 | tf_op jit(solution)/shard_map/ppermute | solution.py:26
  45.8 0.4 collective-permute-start.18
  46.2 0.3 shard_map.76
  46.5 0.4 collective-permute-done.9.refs_3_.refs_2_
  46.9 1.6 %collective-permute-start.6 = (bf16[32,1152]{1,0:T(8,128)(2,1)S(1)}, bf16[32,1152]{1,0:T(8,128)(2,1)S(1)}, u32[]{:S(2)}, u32[]{:S(2)}) collective-permute-start(bf16[32,1152]{1,0:T(8,128)(2,1)S(1)} %get-tuple-element.36), channel_id=1, source_target_pairs={{0,1},{1,0},{2,3},{3,2},{4,5},{5,4},{6,7},{7,6},{8,9},{9,8},{10,11... | collective-permute-start | bytes 221192 | tf_op jit(solution)/shard_map/ppermute | solution.py:26
  48.5 0.2 shard_map.77.refs_5_.refs_6_
  48.7 0.1 collective-permute-start.11
  48.8 2.7 %collective-permute-start.7 = (bf16[32,1152]{1,0:T(8,128)(2,1)S(1)}, bf16[32,1152]{1,0:T(8,128)(2,1)S(1)}, u32[]{:S(2)}, u32[]{:S(2)}) collective-permute-start(bf16[32,1152]{1,0:T(8,128)(2,1)S(1)} %get-tuple-element.37), channel_id=1, source_target_pairs={{0,2},{1,3},{2,0},{3,1},{4,6},{5,7},{6,4},{7,5},{8,10},{9,11},{10,... | collective-permute-start | bytes 221192 | tf_op jit(solution)/shard_map/ppermute | solution.py:26
  51.4 0.2 collective-permute-start.8
  51.6 0.0 collective-permute-start.15
  51.7 0.5 collective-permute-start.17
  52.2 0.3 shard_map.81
  52.4 5.3 %collective-permute-done.7.refs_3_ = bf16[32,1152]{1,0:T(8,128)(2,1)S(1)} collective-permute-done((bf16[32,1152]{1,0:T(8,128)(2,1)S(1)}, bf16[32,1152]{1,0:T(8,128)(2,1)S(1)}, u32[]{:S(2)}, u32[]{:S(2)}) %collective-permute-start.7) | collective-permute-done | bytes 73760 | tf_op jit(solution)/shard_map/ppermute | solution.py:26
  57.7 3.4 %collective-permute-start.20 = (bf16[32,1024]{1,0:T(8,128)(2,1)S(1)}, bf16[32,1024]{1,0:T(8,128)(2,1)S(1)}, u32[]{:S(2)}, u32[]{:S(2)}) collective-permute-start(bf16[32,1024]{1,0:T(8,128)(2,1)S(1)} %get-tuple-element.48), channel_id=1, source_target_pairs={{0,2},{1,3},{2,0},{3,1},{4,6},{5,7},{6,4},{7,5},{8,10},{9,11},{10,... | collective-permute-start | bytes 196616 | tf_op jit(solution)/shard_map/ppermute | solution.py:26
  61.1 1.4 %collective-permute-done.19.refs_3_ = bf16[32,1024]{1,0:T(8,128)(2,1)S(1)} collective-permute-done((bf16[32,1024]{1,0:T(8,128)(2,1)S(1)}, bf16[32,1024]{1,0:T(8,128)(2,1)S(1)}, u32[]{:S(2)}, u32[]{:S(2)}) %collective-permute-start.19) | collective-permute-done | bytes 65568 | tf_op jit(solution)/shard_map/ppermute | solution.py:26
  62.5 2.1 %collective-permute-done.20.refs_4_ = bf16[32,1024]{1,0:T(8,128)(2,1)S(1)} collective-permute-done((bf16[32,1024]{1,0:T(8,128)(2,1)S(1)}, bf16[32,1024]{1,0:T(8,128)(2,1)S(1)}, u32[]{:S(2)}, u32[]{:S(2)}) %collective-permute-start.20) | collective-permute-done | bytes 65568 | tf_op jit(solution)/shard_map/ppermute | solution.py:26
  64.6 1.4 %collective-permute-start.21 = (bf16[32,1024]{1,0:T(8,128)(2,1)S(1)}, bf16[32,1024]{1,0:T(8,128)(2,1)S(1)}, u32[]{:S(2)}, u32[]{:S(2)}) collective-permute-start(bf16[32,1024]{1,0:T(8,128)(2,1)S(1)} %get-tuple-element.49), channel_id=1, source_target_pairs={{0,3},{1,2},{2,1},{3,0},{4,7},{5,6},{6,5},{7,4},{8,11},{9,10},{10,... | collective-permute-start | bytes 196616 | tf_op jit(solution)/shard_map/ppermute | solution.py:26
  66.0 0.5 shard_map.78
  66.6 4.3 %collective-permute-done.21.refs_5_ = bf16[32,1024]{1,0:T(8,128)(2,1)S(1)} collective-permute-done((bf16[32,1024]{1,0:T(8,128)(2,1)S(1)}, bf16[32,1024]{1,0:T(8,128)(2,1)S(1)}, u32[]{:S(2)}, u32[]{:S(2)}) %collective-permute-start.21) | collective-permute-done | bytes 65568 | tf_op jit(solution)/shard_map/ppermute | solution.py:26
  70.9 0.5 shard_map.82.refs_3_
  71.4 0.1 collective-permute-start.22
  71.5 2.1 %collective-permute-start.23 = (bf16[32,1024]{1,0:T(8,128)(2,1)S(1)}, bf16[32,1024]{1,0:T(8,128)(2,1)S(1)}, u32[]{:S(2)}, u32[]{:S(2)}) collective-permute-start(bf16[32,1024]{1,0:T(8,128)(2,1)S(1)} %shard_map.82.refs_3_), channel_id=1, source_target_pairs={{0,2},{1,3},{2,0},{3,1},{4,6},{5,7},{6,4},{7,5},{8,10},{9,11},{10,... | collective-permute-start | bytes 196616 | tf_op jit(solution)/shard_map/ppermute | solution.py:26
  73.6 2.3 %collective-permute-start.24 = (bf16[32,1024]{1,0:T(8,128)(2,1)S(1)}, bf16[32,1024]{1,0:T(8,128)(2,1)S(1)}, u32[]{:S(2)}, u32[]{:S(2)}) collective-permute-start(bf16[32,1024]{1,0:T(8,128)(2,1)S(1)} %shard_map.82.refs_3_), channel_id=1, source_target_pairs={{0,3},{1,2},{2,1},{3,0},{4,7},{5,6},{6,5},{7,4},{8,11},{9,10},{10,... | collective-permute-start | bytes 196616 | tf_op jit(solution)/shard_map/ppermute | solution.py:26
  75.9 0.3 collective-permute-done.22.refs_4_
  76.2 4.0 %collective-permute-done.23.refs_5_ = bf16[32,1024]{1,0:T(8,128)(2,1)S(1)} collective-permute-done((bf16[32,1024]{1,0:T(8,128)(2,1)S(1)}, bf16[32,1024]{1,0:T(8,128)(2,1)S(1)}, u32[]{:S(2)}, u32[]{:S(2)}) %collective-permute-start.23) | collective-permute-done | bytes 65568 | tf_op jit(solution)/shard_map/ppermute | solution.py:26
  80.2 2.2 %collective-permute-start.14 = (bf16[32,1024]{1,0:T(8,128)(2,1)S(1)}, bf16[32,1024]{1,0:T(8,128)(2,1)S(1)}, u32[]{:S(2)}, u32[]{:S(2)}) collective-permute-start(bf16[32,1024]{1,0:T(8,128)(2,1)S(1)} %get-tuple-element.42.refs_3_), channel_id=1, source_target_pairs={{0,3},{1,2},{2,1},{3,0},{4,7},{5,6},{6,5},{7,4},{8,11},{9,10},{10,... | collective-permute-start | bytes 196616 | tf_op jit(solution)/shard_map/ppermute | solution.py:26
  82.3 0.7 shard_map.83
  83.0 2.3 %collective-permute-done.13.refs_5_ = bf16[32,1024]{1,0:T(8,128)(2,1)S(1)} collective-permute-done((bf16[32,1024]{1,0:T(8,128)(2,1)S(1)}, bf16[32,1024]{1,0:T(8,128)(2,1)S(1)}, u32[]{:S(2)}, u32[]{:S(2)}) %collective-permute-start.13) | collective-permute-done | bytes 65568 | tf_op jit(solution)/shard_map/ppermute | solution.py:26
  85.3 0.9 %collective-permute-done.14.refs_6_ = bf16[32,1024]{1,0:T(8,128)(2,1)S(1)} collective-permute-done((bf16[32,1024]{1,0:T(8,128)(2,1)S(1)}, bf16[32,1024]{1,0:T(8,128)(2,1)S(1)}, u32[]{:S(2)}, u32[]{:S(2)}) %collective-permute-start.14) | collective-permute-done | bytes 65568 | tf_op jit(solution)/shard_map/ppermute | solution.py:26
  86.3 0.7 shard_map.80
  86.9 1.2 %shard_map.84.refs_0_ = bf16[256,1024]{1,0:T(8,128)(2,1)} custom-call(bf16[1024,1024]{1,0:T(8,128)(2,1)S(1)} %copy-done, f32[128,1024]{1,0:T(8,128)S(1)} %get-tuple-element.43.refs_1_.refs_2_, f32[128,1024]{1,0:T(8,128)S(1)} %get-tuple-element.50.refs_2_.refs_3_, bf16[4,128,256]{2,1,0:T(8,128)(2,1)S(1)} %get-tuple-element.51.refs_3_.refs_4_, ...), custom_call_target="tpu_custom_call" | custom-call | tf_op jit(solution)/shard_map/pallas_call | solution.py:40
  88.1 1.2 %shard_map.85 = bf16[256,1024]{1,0:T(8,128)(2,1)} custom-call(bf16[256,1024]{1,0:T(8,128)(2,1)} %shard_map.84.refs_0_, bf16[1024,1024]{1,0:T(8,128)(2,1)S(1)} %copy-done, f32[128,1024]{1,0:T(8,128)S(1)} %get-tuple-element.43.refs_1_.refs_2_, f32[128,1024]{1,0:T(8,128)S(1)} %get-tuple-element.50.refs_2_.refs_3_, ...), custom_call_target="tpu_custom_call", output_to_operand_aliasing={{}: (0, {})} | custom-call | tf_op jit(solution)/shard_map/pallas_call | solution.py:40
  (37 shorter events, 0.1 us)
Async XLA Ops:
  0.0 6.7 %copy-start.5 = (bf16[2,512,256]{2,1,0:T(8,128)(2,1)S(1)}, bf16[2,512,256]{2,1,0:T(8,128)(2,1)}, u32[]{:S(2)}) copy-start(bf16[2,512,256]{2,1,0:T(8,128)(2,1)} %refs_1_.4) | copy-start | bytes 1572868
  0.0 6.7 %copy-start.6 = (bf16[1024,8]{0,1:T(8,128)(2,1)S(1)}, bf16[1024,8]{0,1:T(8,128)(2,1)}, u32[]{:S(2)}) copy-start(bf16[1024,8]{0,1:T(8,128)(2,1)} %param.9) | copy-start | bytes 49156
  0.0 6.7 %copy-start = (bf16[1024,1024]{1,0:T(8,128)(2,1)S(1)}, bf16[1024,1024]{1,0:T(8,128)(2,1)}, u32[]{:S(2)}) copy-start(bf16[1024,1024]{1,0:T(8,128)(2,1)} %refs_1_.5) | copy-start | bytes 6291460
  0.0 10.3 %collective-permute-start.4 = (bf16[2,128,256]{2,1,0:T(8,128)(2,1)}, bf16[2,128,256]{2,1,0:T(8,128)(2,1)S(1)}, u32[]{:S(2)}, u32[]{:S(2)}) collective-permute-start(bf16[2,128,256]{2,1,0:T(8,128)(2,1)} %refs_0_.7), channel_id=1, source_target_pairs={{0,8},{4,12},{8,0},{12,4},{1,9},{5,13},{9,1},{13,5},{2,10},{6,14},... | collective-permute-start | bytes 393224 | tf_op jit(solution)/shard_map/ppermute | solution.py:26
  3.1 8.8 %collective-permute-start.5 = (bf16[2,128,256]{2,1,0:T(8,128)(2,1)}, bf16[2,128,256]{2,1,0:T(8,128)(2,1)S(1)}, u32[]{:S(2)}, u32[]{:S(2)}) collective-permute-start(bf16[2,128,256]{2,1,0:T(8,128)(2,1)} %refs_0_.7), channel_id=1, source_target_pairs={{0,4},{4,0},{8,12},{12,8},{1,5},{5,1},{9,13},{13,9},{2,6},{6,2},{1... | collective-permute-start | bytes 393224 | tf_op jit(solution)/shard_map/ppermute | solution.py:26
  4.6 2.1 %collective-permute-start = (bf16[2,512,256]{2,1,0:T(8,128)(2,1)}, bf16[2,512,256]{2,1,0:T(8,128)(2,1)S(1)}, u32[]{:S(2)}, u32[]{:S(2)}) collective-permute-start(bf16[2,512,256]{2,1,0:T(8,128)(2,1)} %refs_1_.4), channel_id=1, source_target_pairs={{0,16},{16,0},{1,17},{17,1},{2,18},{18,2},{3,19},{19,3},{4,20},{20... | collective-permute-start | bytes 1572872 | tf_op jit(solution)/shard_map/ppermute | solution.py:401
  6.7 1.4 %copy-start.2 = (bf16[2,512,256]{2,1,0:T(8,128)(2,1)S(1)}, bf16[2,512,256]{2,1,0:T(8,128)(2,1)}, u32[]{:S(2)}) copy-start(bf16[2,512,256]{2,1,0:T(8,128)(2,1)} %refs_0_.8) | copy-start | bytes 1572868
  7.5 6.4 %collective-permute-start.1 = (bf16[128,512]{1,0:T(8,128)(2,1)S(1)}, bf16[128,512]{1,0:T(8,128)(2,1)S(1)}, u32[]{:S(2)}, u32[]{:S(2)}) collective-permute-start(bf16[128,512]{1,0:T(8,128)(2,1)S(1)} %get-tuple-element.30), channel_id=1, source_target_pairs={{0,4},{4,0},{8,12},{12,8},{1,5},{5,1},{9,13},{13,9},{2,6},{6,2},{1... | collective-permute-start | bytes 393224 | tf_op jit(solution)/shard_map/ppermute | solution.py:26
  8.3 40.4 %collective-permute-start.16 = (bf16[2,256,512]{2,1,0:T(8,128)(2,1)S(1)}, bf16[2,256,512]{2,1,0:T(8,128)(2,1)S(1)}, u32[]{:S(2)}, u32[]{:S(2)}) collective-permute-start(bf16[2,256,512]{2,1,0:T(8,128)(2,1)S(1)} %shard_map.79.refs_7_), channel_id=1, source_target_pairs={{0,4},{4,0},{8,12},{12,8},{1,5},{5,1},{9,13},{13,9},{2,6},{6,2},{1... | collective-permute-start | bytes 1572872 | tf_op jit(solution)/shard_map/ppermute | solution.py:26
  9.8 38.9 %collective-permute-start.25 = (bf16[2,256,512]{2,1,0:T(8,128)(2,1)S(1)}, bf16[2,256,512]{2,1,0:T(8,128)(2,1)S(1)}, u32[]{:S(2)}, u32[]{:S(2)}) collective-permute-start(bf16[2,256,512]{2,1,0:T(8,128)(2,1)S(1)} %shard_map.79.refs_7_), channel_id=1, source_target_pairs={{0,8},{4,12},{8,0},{12,4},{1,9},{5,13},{9,1},{13,5},{2,10},{6,14},... | collective-permute-start | bytes 1572872 | tf_op jit(solution)/shard_map/ppermute | solution.py:26
  10.3 41.1 %collective-permute-start.26 = (bf16[2,256,512]{2,1,0:T(8,128)(2,1)S(1)}, bf16[2,256,512]{2,1,0:T(8,128)(2,1)S(1)}, u32[]{:S(2)}, u32[]{:S(2)}) collective-permute-start(bf16[2,256,512]{2,1,0:T(8,128)(2,1)S(1)} %shard_map.79.refs_7_), channel_id=1, source_target_pairs={{0,12},{4,8},{8,4},{12,0},{1,13},{5,9},{9,5},{13,1},{2,14},{6,10},... | collective-permute-start | bytes 1572872 | tf_op jit(solution)/shard_map/ppermute | solution.py:26
  11.8 28.3 %collective-permute-start.2 = (bf16[128,512]{1,0:T(8,128)(2,1)S(1)}, bf16[128,512]{1,0:T(8,128)(2,1)S(1)}, u32[]{:S(2)}, u32[]{:S(2)}) collective-permute-start(bf16[128,512]{1,0:T(8,128)(2,1)S(1)} %get-tuple-element.31), channel_id=1, source_target_pairs={{0,8},{4,12},{8,0},{12,4},{1,9},{5,13},{9,1},{13,5},{2,10},{6,14},... | collective-permute-start | bytes 393224 | tf_op jit(solution)/shard_map/ppermute | solution.py:26
  13.9 32.3 %copy-start.1 = (s32[1024,4]{0,1:T(4,128)S(1)}, s32[1024,4]{0,1:T(4,128)}, u32[]{:S(2)}) copy-start(s32[1024,4]{0,1:T(4,128)} %param.8) | copy-start | bytes 49156
  13.9 34.6 %copy-start.3 = (bf16[2,128,256]{2,1,0:T(8,128)(2,1)S(1)}, bf16[2,128,256]{2,1,0:T(8,128)(2,1)}, u32[]{:S(2)}) copy-start(bf16[2,128,256]{2,1,0:T(8,128)(2,1)} %refs_0_.7) | copy-start | bytes 393220
  13.9 26.7 %collective-permute-start.3 = (bf16[128,512]{1,0:T(8,128)(2,1)S(1)}, bf16[128,512]{1,0:T(8,128)(2,1)S(1)}, u32[]{:S(2)}, u32[]{:S(2)}) collective-permute-start(bf16[128,512]{1,0:T(8,128)(2,1)S(1)} %get-tuple-element.32), channel_id=1, source_target_pairs={{0,12},{4,8},{8,4},{12,0},{1,13},{5,9},{9,5},{13,1},{2,14},{6,10},... | collective-permute-start | bytes 393224 | tf_op jit(solution)/shard_map/ppermute | solution.py:26
  40.1 5.7 %collective-permute-start.10 = (bf16[192,512]{1,0:T(8,128)(2,1)S(1)}, bf16[192,512]{1,0:T(8,128)(2,1)S(1)}, u32[]{:S(2)}, u32[]{:S(2)}) collective-permute-start(bf16[192,512]{1,0:T(8,128)(2,1)S(1)} %get-tuple-element.40), channel_id=1, source_target_pairs={{0,8},{4,12},{8,0},{12,4},{1,9},{5,13},{9,1},{13,5},{2,10},{6,14},... | collective-permute-start | bytes 589832 | tf_op jit(solution)/shard_map/ppermute | solution.py:26
  40.6 6.3 %collective-permute-start.9 = (bf16[192,512]{1,0:T(8,128)(2,1)S(1)}, bf16[192,512]{1,0:T(8,128)(2,1)S(1)}, u32[]{:S(2)}, u32[]{:S(2)}) collective-permute-start(bf16[192,512]{1,0:T(8,128)(2,1)S(1)} %get-tuple-element.39), channel_id=1, source_target_pairs={{0,4},{4,0},{8,12},{12,8},{1,5},{5,1},{9,13},{13,9},{2,6},{6,2},{1... | collective-permute-start | bytes 589832 | tf_op jit(solution)/shard_map/ppermute | solution.py:26
  45.8 5.9 %collective-permute-start.18 = (bf16[128,512]{1,0:T(8,128)(2,1)S(1)}, bf16[128,512]{1,0:T(8,128)(2,1)S(1)}, u32[]{:S(2)}, u32[]{:S(2)}) collective-permute-start(bf16[128,512]{1,0:T(8,128)(2,1)S(1)} %get-tuple-element.45), channel_id=1, source_target_pairs={{0,12},{4,8},{8,4},{12,0},{1,13},{5,9},{9,5},{13,1},{2,14},{6,10},... | collective-permute-start | bytes 393224 | tf_op jit(solution)/shard_map/ppermute | solution.py:26
  46.9 35.5 %copy-start.4 = (f32[1024]{0:T(1024)S(1)}, f32[1024]{0:T(1024)}, u32[]{:S(2)}) copy-start(f32[1024]{0:T(1024)} %param.13) | copy-start | bytes 12292
  46.9 4.8 %collective-permute-start.6 = (bf16[32,1152]{1,0:T(8,128)(2,1)S(1)}, bf16[32,1152]{1,0:T(8,128)(2,1)S(1)}, u32[]{:S(2)}, u32[]{:S(2)}) collective-permute-start(bf16[32,1152]{1,0:T(8,128)(2,1)S(1)} %get-tuple-element.36), channel_id=1, source_target_pairs={{0,1},{1,0},{2,3},{3,2},{4,5},{5,4},{6,7},{7,6},{8,9},{9,8},{10,11... | collective-permute-start | bytes 221192 | tf_op jit(solution)/shard_map/ppermute | solution.py:26
  48.7 15.9 %collective-permute-start.11 = (bf16[8,256,128]{2,1,0:T(8,128)(2,1)S(1)}, bf16[8,256,128]{2,1,0:T(8,128)(2,1)S(1)}, u32[]{:S(2)}, u32[]{:S(2)}) collective-permute-start(bf16[8,256,128]{2,1,0:T(8,128)(2,1)S(1)} %shard_map.77.refs_5_.refs_6_), channel_id=1, source_target_pairs={{0,16},{16,0},{1,17},{17,1},{2,18},{18,2},{3,19},{19,3},{4,20},{20... | collective-permute-start | bytes 1572872 | tf_op jit(solution)/shard_map/ppermute | solution.py:401
  48.8 8.9 %collective-permute-start.7 = (bf16[32,1152]{1,0:T(8,128)(2,1)S(1)}, bf16[32,1152]{1,0:T(8,128)(2,1)S(1)}, u32[]{:S(2)}, u32[]{:S(2)}) collective-permute-start(bf16[32,1152]{1,0:T(8,128)(2,1)S(1)} %get-tuple-element.37), channel_id=1, source_target_pairs={{0,2},{1,3},{2,0},{3,1},{4,6},{5,7},{6,4},{7,5},{8,10},{9,11},{10,... | collective-permute-start | bytes 221192 | tf_op jit(solution)/shard_map/ppermute | solution.py:26
  51.4 6.3 %collective-permute-start.8 = (bf16[32,1152]{1,0:T(8,128)(2,1)S(1)}, bf16[32,1152]{1,0:T(8,128)(2,1)S(1)}, u32[]{:S(2)}, u32[]{:S(2)}) collective-permute-start(bf16[32,1152]{1,0:T(8,128)(2,1)S(1)} %get-tuple-element.38), channel_id=1, source_target_pairs={{0,3},{1,2},{2,1},{3,0},{4,7},{5,6},{6,5},{7,4},{8,11},{9,10},{10,... | collective-permute-start | bytes 221192 | tf_op jit(solution)/shard_map/ppermute | solution.py:26
  51.6 19.9 %collective-permute-start.15 = (bf16[2,256,512]{2,1,0:T(8,128)(2,1)S(1)}, bf16[2,256,512]{2,1,0:T(8,128)(2,1)S(1)}, u32[]{:S(2)}, u32[]{:S(2)}) collective-permute-start(bf16[2,256,512]{2,1,0:T(8,128)(2,1)S(1)} %shard_map.79.refs_7_), channel_id=1, source_target_pairs={{0,16},{16,0},{1,17},{17,1},{2,18},{18,2},{3,19},{19,3},{4,20},{20... | collective-permute-start | bytes 1572872 | tf_op jit(solution)/shard_map/ppermute | solution.py:401
  51.7 21.9 %collective-permute-start.17 = (bf16[2,256,512]{2,1,0:T(8,128)(2,1)S(1)}, bf16[2,256,512]{2,1,0:T(8,128)(2,1)S(1)}, u32[]{:S(2)}, u32[]{:S(2)}) collective-permute-start(bf16[2,256,512]{2,1,0:T(8,128)(2,1)S(1)} %collective-permute-done.16.refs_9_), channel_id=1, source_target_pairs={{0,16},{16,0},{1,17},{17,1},{2,18},{18,2},{3,19},{19,3},{4,20},{20... | collective-permute-start | bytes 1572872 | tf_op jit(solution)/shard_map/ppermute | solution.py:401
  57.7 4.8 %collective-permute-start.19 = (bf16[32,1024]{1,0:T(8,128)(2,1)S(1)}, bf16[32,1024]{1,0:T(8,128)(2,1)S(1)}, u32[]{:S(2)}, u32[]{:S(2)}) collective-permute-start(bf16[32,1024]{1,0:T(8,128)(2,1)S(1)} %get-tuple-element.47), channel_id=1, source_target_pairs={{0,1},{1,0},{2,3},{3,2},{4,5},{5,4},{6,7},{7,6},{8,9},{9,8},{10,11... | collective-permute-start | bytes 196616 | tf_op jit(solution)/shard_map/ppermute | solution.py:26
  57.7 6.9 %collective-permute-start.20 = (bf16[32,1024]{1,0:T(8,128)(2,1)S(1)}, bf16[32,1024]{1,0:T(8,128)(2,1)S(1)}, u32[]{:S(2)}, u32[]{:S(2)}) collective-permute-start(bf16[32,1024]{1,0:T(8,128)(2,1)S(1)} %get-tuple-element.48), channel_id=1, source_target_pairs={{0,2},{1,3},{2,0},{3,1},{4,6},{5,7},{6,4},{7,5},{8,10},{9,11},{10,... | collective-permute-start | bytes 196616 | tf_op jit(solution)/shard_map/ppermute | solution.py:26
  62.5 25.7 %collective-permute-start.27 = (bf16[2,256,512]{2,1,0:T(8,128)(2,1)S(1)}, bf16[2,256,512]{2,1,0:T(8,128)(2,1)S(1)}, u32[]{:S(2)}, u32[]{:S(2)}) collective-permute-start(bf16[2,256,512]{2,1,0:T(8,128)(2,1)S(1)} %collective-permute-done.25.refs_5_), channel_id=1, source_target_pairs={{0,16},{16,0},{1,17},{17,1},{2,18},{18,2},{3,19},{19,3},{4,20},{20... | collective-permute-start | bytes 1572872 | tf_op jit(solution)/shard_map/ppermute | solution.py:401
  64.6 23.6 %collective-permute-start.28 = (bf16[2,256,512]{2,1,0:T(8,128)(2,1)S(1)}, bf16[2,256,512]{2,1,0:T(8,128)(2,1)S(1)}, u32[]{:S(2)}, u32[]{:S(2)}) collective-permute-start(bf16[2,256,512]{2,1,0:T(8,128)(2,1)S(1)} %collective-permute-done.26.refs_6_), channel_id=1, source_target_pairs={{0,16},{16,0},{1,17},{17,1},{2,18},{18,2},{3,19},{19,3},{4,20},{20... | collective-permute-start | bytes 1572872 | tf_op jit(solution)/shard_map/ppermute | solution.py:401
  64.6 6.3 %collective-permute-start.21 = (bf16[32,1024]{1,0:T(8,128)(2,1)S(1)}, bf16[32,1024]{1,0:T(8,128)(2,1)S(1)}, u32[]{:S(2)}, u32[]{:S(2)}) collective-permute-start(bf16[32,1024]{1,0:T(8,128)(2,1)S(1)} %get-tuple-element.49), channel_id=1, source_target_pairs={{0,3},{1,2},{2,1},{3,0},{4,7},{5,6},{6,5},{7,4},{8,11},{9,10},{10,... | collective-permute-start | bytes 196616 | tf_op jit(solution)/shard_map/ppermute | solution.py:26
  71.4 4.7 %collective-permute-start.22 = (bf16[32,1024]{1,0:T(8,128)(2,1)S(1)}, bf16[32,1024]{1,0:T(8,128)(2,1)S(1)}, u32[]{:S(2)}, u32[]{:S(2)}) collective-permute-start(bf16[32,1024]{1,0:T(8,128)(2,1)S(1)} %shard_map.82.refs_3_), channel_id=1, source_target_pairs={{0,1},{1,0},{2,3},{3,2},{4,5},{5,4},{6,7},{7,6},{8,9},{9,8},{10,11... | collective-permute-start | bytes 196616 | tf_op jit(solution)/shard_map/ppermute | solution.py:26
  71.5 8.6 %collective-permute-start.23 = (bf16[32,1024]{1,0:T(8,128)(2,1)S(1)}, bf16[32,1024]{1,0:T(8,128)(2,1)S(1)}, u32[]{:S(2)}, u32[]{:S(2)}) collective-permute-start(bf16[32,1024]{1,0:T(8,128)(2,1)S(1)} %shard_map.82.refs_3_), channel_id=1, source_target_pairs={{0,2},{1,3},{2,0},{3,1},{4,6},{5,7},{6,4},{7,5},{8,10},{9,11},{10,... | collective-permute-start | bytes 196616 | tf_op jit(solution)/shard_map/ppermute | solution.py:26
  73.6 6.6 %collective-permute-start.24 = (bf16[32,1024]{1,0:T(8,128)(2,1)S(1)}, bf16[32,1024]{1,0:T(8,128)(2,1)S(1)}, u32[]{:S(2)}, u32[]{:S(2)}) collective-permute-start(bf16[32,1024]{1,0:T(8,128)(2,1)S(1)} %shard_map.82.refs_3_), channel_id=1, source_target_pairs={{0,3},{1,2},{2,1},{3,0},{4,7},{5,6},{6,5},{7,4},{8,11},{9,10},{10,... | collective-permute-start | bytes 196616 | tf_op jit(solution)/shard_map/ppermute | solution.py:26
  76.2 6.9 %collective-permute-start.12 = (bf16[32,1024]{1,0:T(8,128)(2,1)S(1)}, bf16[32,1024]{1,0:T(8,128)(2,1)S(1)}, u32[]{:S(2)}, u32[]{:S(2)}) collective-permute-start(bf16[32,1024]{1,0:T(8,128)(2,1)S(1)} %get-tuple-element.42.refs_3_), channel_id=1, source_target_pairs={{0,1},{1,0},{2,3},{3,2},{4,5},{5,4},{6,7},{7,6},{8,9},{9,8},{10,11... | collective-permute-start | bytes 196616 | tf_op jit(solution)/shard_map/ppermute | solution.py:26
  80.1 5.2 %collective-permute-start.13 = (bf16[32,1024]{1,0:T(8,128)(2,1)S(1)}, bf16[32,1024]{1,0:T(8,128)(2,1)S(1)}, u32[]{:S(2)}, u32[]{:S(2)}) collective-permute-start(bf16[32,1024]{1,0:T(8,128)(2,1)S(1)} %get-tuple-element.42.refs_3_), channel_id=1, source_target_pairs={{0,2},{1,3},{2,0},{3,1},{4,6},{5,7},{6,4},{7,5},{8,10},{9,11},{10,... | collective-permute-start | bytes 196616 | tf_op jit(solution)/shard_map/ppermute | solution.py:26
  80.2 6.1 %collective-permute-start.14 = (bf16[32,1024]{1,0:T(8,128)(2,1)S(1)}, bf16[32,1024]{1,0:T(8,128)(2,1)S(1)}, u32[]{:S(2)}, u32[]{:S(2)}) collective-permute-start(bf16[32,1024]{1,0:T(8,128)(2,1)S(1)} %get-tuple-element.42.refs_3_), channel_id=1, source_target_pairs={{0,3},{1,2},{2,1},{3,0},{4,7},{5,6},{6,5},{7,4},{8,11},{9,10},{10,... | collective-permute-start | bytes 196616 | tf_op jit(solution)/shard_map/ppermute | solution.py:26

commit v5 on v4

--- a/solution.py
+++ b/solution.py
@@ -379,6 +379,68 @@
     )[0]
 
 
+def add_up(sums, lefts, wides, first, piece, x=None):
+    rows = sums[0].shape[0]
+    block = rows * len(sums)
+    n_loc, _, half = wides[0].shape
+    n, n_w = len(sums), len(wides)
+
+    def body(place_ref, *refs):
+        if x is not None:
+            x_ref, *refs = refs
+        s_refs, l_refs, w_refs, out_ref = refs[:n], refs[n : 2 * n], refs[2 * n : -1], refs[-1]
+        at = [place_ref[0], 1 - place_ref[0]][piece] * half
+        cols = rows_at(at, half)
+        acc = jnp.concatenate([s[:, cols] for s in s_refs], axis=0)
+        for q in range(n_w):
+            for e in range(n_loc):
+                left = jnp.concatenate([r[(first + q) * n_loc + e] for r in l_refs], axis=0)
+                acc = acc + jnp.dot(left, w_refs[q][e], preferred_element_type=F32)
+        if x is None:
+            out_ref[...] = acc
+        else:
+            xs = x_ref[rows_at(place_ref[1] * block, block), cols].astype(F32)
+            out_ref[...] = (xs + xs * acc).astype(BF16)
+
+    kind = F32 if x is None else BF16
+    args = ([] if x is None else [x]) + [*sums, *lefts, *wides]
+    return call(body, args, [((block, half), kind)])[0]
+
+
+def finish(x, own, acc, lefts, wide, first):
+    block, half = own.shape
+    n_loc = wide.shape[0]
+    cut = half // 2
+
+    def body(place_ref, x_ref, own_ref, acc_ref, *refs):
+        l_refs, (w_ref, out_ref, buf, sems) = refs[:-4], refs[-4:]
+        here, there = place_ref[0] * half, (1 - place_ref[0]) * half
+        mine = rows_at(place_ref[1] * block, block)
+        copies = [pltpu.make_async_copy(own_ref, out_ref.at[:, rows_at(here, half)], sems.at[2])]
+        copies[0].start()
+        for c in range(2):
+            part = slice(c * cut, (c + 1) * cut)
+            acc = acc_ref[:, part]
+            for e in range(n_loc):
+                left = jnp.concatenate([r[first * n_loc + e] for r in l_refs], axis=0)
+                acc = acc + jnp.dot(left, w_ref[e, :, part], preferred_element_type=F32)
+            cols = rows_at(there + c * cut, cut)
+            xs = x_ref[mine, cols].astype(F32)
+            buf[:, part] = (xs + xs * acc).astype(BF16)
+            copies.append(pltpu.make_async_copy(buf.at[:, part], out_ref.at[:, cols], sems.at[c]))
+            copies[-1].start()
+        for c in copies:
+            c.wait()
+
+    return call(
+        body,
+        [x, own, acc, *lefts, wide],
+        [((block, 2 * half), BF16)],
+        [pltpu.VMEM((block, half), BF16), pltpu.SemaphoreType.DMA((3,))],
+        held=("out",),
+    )[0]
+
+
 def relays(ne):
     return ne == 4
 
@@ -449,10 +511,12 @@
         )
         sums.append(total)
         lefts.append(left)
-    out = None
-    for k in range(len(wides[0])):
-        out = close(inputs, sums, lefts, [w[k] for w in wides[n_src:]], k, out, pair)
-    return out
+    later = wides[n_src:]
+    if not pair:
+        return close(inputs, sums, lefts, [w[0] for w in later], 0, None, pair)
+    near_cols = add_up(sums, lefts, [w[0] for w in later], 0, 0, inputs)
+    acc = add_up(sums, lefts, [w[1] for w in later[:-1]], 0, 1)
+    return finish(inputs, near_cols, acc, lefts, later[-1][1], len(later) - 1)
 
 
 def solution(mesh):

time: 89.5 us -> 88.9 us (level)
    pallas_call x13 -> x14, Pallas kernels: 7.25 us -> 6.69 us  [call(): pl.pallas_call(placed, in_specs=[space(k) for k in range(len(args))], out...]
  transfers between devices with their start and end apart: 29 -> 29, of which waited for: 13 -> 13; matrix products, arithmetic and copies ran while one was open for 0% -> 0% of each run, Pallas kernels for 7% -> 6%
where the time goes in v5:
time: 88.9 us; the launch traced here: 88.8 us
  waiting for transfers between devices  54.3 us (61%)
  starting transfers between devices  27.6 us (31%)
  Pallas kernels  6.69 us (8%)
    ppermute x23, waiting for transfers between devices, send(): return lax.ppermute(x, axis, [(i, peer_to(i, m, n)) for i in range(n)])  52.2 us
    ppermute x23, starting transfers between devices, send(): return lax.ppermute(x, axis, [(i, peer_to(i, m, n)) for i in range(n)])  27 us
    pallas_call x14, Pallas kernels, call(): pl.pallas_call(placed, in_specs=[space(k) for k in range(len(args))], out...  6.69 us
    ppermute x6, waiting for transfers between devices, swap(): return lax.ppermute(w, 'batch', [(0, 1), (1, 0)])  2.13 us
  transfers between devices with their start and end apart: 29, of which 13 were waited for; matrix products, arithmetic and copies ran while one was open for 0% of the time, Pallas kernels for 6%

profile of v5, /device:TPU:0, one launch (start us, length us, event | category | flops | bytes accessed | tf_op | source)
XLA Modules:
  0.0 88.8 jit_solution(18231421712912074277)
XLA Ops:
  0.0 3.1 %collective-permute-start.4 = (bf16[2,128,256]{2,1,0:T(8,128)(2,1)}, bf16[2,128,256]{2,1,0:T(8,128)(2,1)S(1)}, u32[]{:S(2)}, u32[]{:S(2)}) collective-permute-start(bf16[2,128,256]{2,1,0:T(8,128)(2,1)} %refs_0_.8), channel_id=1, source_target_pairs={{0,8},{4,12},{8,0},{12,4},{1,9},{5,13},{9,1},{13,5},{2,10},{6,14},... | collective-permute-start | bytes 393224 | tf_op jit(solution)/shard_map/ppermute | solution.py:26
  3.1 1.5 %collective-permute-start.5 = (bf16[2,128,256]{2,1,0:T(8,128)(2,1)}, bf16[2,128,256]{2,1,0:T(8,128)(2,1)S(1)}, u32[]{:S(2)}, u32[]{:S(2)}) collective-permute-start(bf16[2,128,256]{2,1,0:T(8,128)(2,1)} %refs_0_.8), channel_id=1, source_target_pairs={{0,4},{4,0},{8,12},{12,8},{1,5},{5,1},{9,13},{13,9},{2,6},{6,2},{1... | collective-permute-start | bytes 393224 | tf_op jit(solution)/shard_map/ppermute | solution.py:26
  4.6 2.1 %collective-permute-done.refs_2_ = bf16[2,512,256]{2,1,0:T(8,128)(2,1)S(1)} collective-permute-done((bf16[2,512,256]{2,1,0:T(8,128)(2,1)}, bf16[2,512,256]{2,1,0:T(8,128)(2,1)S(1)}, u32[]{:S(2)}, u32[]{:S(2)}) %collective-permute-start) | collective-permute-done | bytes 524320 | tf_op jit(solution)/shard_map/ppermute | solution.py:463
  6.7 0.8 shard_map.74
  7.5 0.6 collective-permute-start.1
  8.1 0.2 shard_map.79.refs_7_
  8.3 1.6 %collective-permute-start.16 = (bf16[2,256,512]{2,1,0:T(8,128)(2,1)S(1)}, bf16[2,256,512]{2,1,0:T(8,128)(2,1)S(1)}, u32[]{:S(2)}, u32[]{:S(2)}) collective-permute-start(bf16[2,256,512]{2,1,0:T(8,128)(2,1)S(1)} %shard_map.79.refs_7_), channel_id=1, source_target_pairs={{0,4},{4,0},{8,12},{12,8},{1,5},{5,1},{9,13},{13,9},{2,6},{6,2},{1... | collective-permute-start | bytes 1572872 | tf_op jit(solution)/shard_map/ppermute | solution.py:26
  9.8 0.5 collective-permute-start.25
  10.3 1.5 %collective-permute-start.26 = (bf16[2,256,512]{2,1,0:T(8,128)(2,1)S(1)}, bf16[2,256,512]{2,1,0:T(8,128)(2,1)S(1)}, u32[]{:S(2)}, u32[]{:S(2)}) collective-permute-start(bf16[2,256,512]{2,1,0:T(8,128)(2,1)S(1)} %shard_map.79.refs_7_), channel_id=1, source_target_pairs={{0,12},{4,8},{8,4},{12,0},{1,13},{5,9},{9,5},{13,1},{2,14},{6,10},... | collective-permute-start | bytes 1572872 | tf_op jit(solution)/shard_map/ppermute | solution.py:26
  11.8 0.2 collective-permute-start.2
  12.0 1.9 %collective-permute-done.1.refs_2_ = bf16[128,512]{1,0:T(8,128)(2,1)S(1)} collective-permute-done((bf16[128,512]{1,0:T(8,128)(2,1)S(1)}, bf16[128,512]{1,0:T(8,128)(2,1)S(1)}, u32[]{:S(2)}, u32[]{:S(2)}) %collective-permute-start.1) | collective-permute-done | bytes 131104 | tf_op jit(solution)/shard_map/ppermute | solution.py:26
  13.9 0.9 collective-permute-start.3
  14.8 0.8 shard_map.75
  15.6 24.5 %collective-permute-done.2.refs_3_ = bf16[128,512]{1,0:T(8,128)(2,1)S(1)} collective-permute-done((bf16[128,512]{1,0:T(8,128)(2,1)S(1)}, bf16[128,512]{1,0:T(8,128)(2,1)S(1)}, u32[]{:S(2)}, u32[]{:S(2)}) %collective-permute-start.2) | collective-permute-done | bytes 131104 | tf_op jit(solution)/shard_map/ppermute | solution.py:26
  40.1 0.5 collective-permute-start.10
  40.6 0.5 collective-permute-start.9
  41.1 4.7 %collective-permute-done.10.refs_4_.refs_3_ = bf16[192,512]{1,0:T(8,128)(2,1)S(1)} collective-permute-done((bf16[192,512]{1,0:T(8,128)(2,1)S(1)}, bf16[192,512]{1,0:T(8,128)(2,1)S(1)}, u32[]{:S(2)}, u32[]{:S(2)}) %collective-permute-start.10) | collective-permute-done | bytes 196640 | tf_op jit(solution)/shard_map/ppermute | solution.py:26
  45.8 0.4 collective-permute-start.18
  46.2 0.3 shard_map.76
  46.5 0.4 collective-permute-done.9.refs_3_.refs_2_
  46.9 1.6 %collective-permute-start.6 = (bf16[32,1152]{1,0:T(8,128)(2,1)S(1)}, bf16[32,1152]{1,0:T(8,128)(2,1)S(1)}, u32[]{:S(2)}, u32[]{:S(2)}) collective-permute-start(bf16[32,1152]{1,0:T(8,128)(2,1)S(1)} %get-tuple-element.36), channel_id=1, source_target_pairs={{0,1},{1,0},{2,3},{3,2},{4,5},{5,4},{6,7},{7,6},{8,9},{9,8},{10,11... | collective-permute-start | bytes 221192 | tf_op jit(solution)/shard_map/ppermute | solution.py:26
  48.5 0.2 shard_map.77.refs_5_.refs_6_
  48.7 0.1 collective-permute-start.11
  48.8 2.7 %collective-permute-start.7 = (bf16[32,1152]{1,0:T(8,128)(2,1)S(1)}, bf16[32,1152]{1,0:T(8,128)(2,1)S(1)}, u32[]{:S(2)}, u32[]{:S(2)}) collective-permute-start(bf16[32,1152]{1,0:T(8,128)(2,1)S(1)} %get-tuple-element.37), channel_id=1, source_target_pairs={{0,2},{1,3},{2,0},{3,1},{4,6},{5,7},{6,4},{7,5},{8,10},{9,11},{10,... | collective-permute-start | bytes 221192 | tf_op jit(solution)/shard_map/ppermute | solution.py:26
  51.4 0.2 collective-permute-start.8
  51.7 0.5 collective-permute-start.17
  52.2 0.3 shard_map.81
  52.4 5.3 %collective-permute-done.7.refs_3_ = bf16[32,1152]{1,0:T(8,128)(2,1)S(1)} collective-permute-done((bf16[32,1152]{1,0:T(8,128)(2,1)S(1)}, bf16[32,1152]{1,0:T(8,128)(2,1)S(1)}, u32[]{:S(2)}, u32[]{:S(2)}) %collective-permute-start.7) | collective-permute-done | bytes 73760 | tf_op jit(solution)/shard_map/ppermute | solution.py:26
  57.7 3.4 %collective-permute-start.20 = (bf16[32,1024]{1,0:T(8,128)(2,1)S(1)}, bf16[32,1024]{1,0:T(8,128)(2,1)S(1)}, u32[]{:S(2)}, u32[]{:S(2)}) collective-permute-start(bf16[32,1024]{1,0:T(8,128)(2,1)S(1)} %get-tuple-element.48), channel_id=1, source_target_pairs={{0,2},{1,3},{2,0},{3,1},{4,6},{5,7},{6,4},{7,5},{8,10},{9,11},{10,... | collective-permute-start | bytes 196616 | tf_op jit(solution)/shard_map/ppermute | solution.py:26
  61.1 1.4 %collective-permute-done.19.refs_3_ = bf16[32,1024]{1,0:T(8,128)(2,1)S(1)} collective-permute-done((bf16[32,1024]{1,0:T(8,128)(2,1)S(1)}, bf16[32,1024]{1,0:T(8,128)(2,1)S(1)}, u32[]{:S(2)}, u32[]{:S(2)}) %collective-permute-start.19) | collective-permute-done | bytes 65568 | tf_op jit(solution)/shard_map/ppermute | solution.py:26
  62.5 2.1 %collective-permute-done.20.refs_4_ = bf16[32,1024]{1,0:T(8,128)(2,1)S(1)} collective-permute-done((bf16[32,1024]{1,0:T(8,128)(2,1)S(1)}, bf16[32,1024]{1,0:T(8,128)(2,1)S(1)}, u32[]{:S(2)}, u32[]{:S(2)}) %collective-permute-start.20) | collective-permute-done | bytes 65568 | tf_op jit(solution)/shard_map/ppermute | solution.py:26
  64.6 1.4 %collective-permute-start.21 = (bf16[32,1024]{1,0:T(8,128)(2,1)S(1)}, bf16[32,1024]{1,0:T(8,128)(2,1)S(1)}, u32[]{:S(2)}, u32[]{:S(2)}) collective-permute-start(bf16[32,1024]{1,0:T(8,128)(2,1)S(1)} %get-tuple-element.49), channel_id=1, source_target_pairs={{0,3},{1,2},{2,1},{3,0},{4,7},{5,6},{6,5},{7,4},{8,11},{9,10},{10,... | collective-permute-start | bytes 196616 | tf_op jit(solution)/shard_map/ppermute | solution.py:26
  66.0 0.5 shard_map.78
  66.6 4.3 %collective-permute-done.21.refs_5_ = bf16[32,1024]{1,0:T(8,128)(2,1)S(1)} collective-permute-done((bf16[32,1024]{1,0:T(8,128)(2,1)S(1)}, bf16[32,1024]{1,0:T(8,128)(2,1)S(1)}, u32[]{:S(2)}, u32[]{:S(2)}) %collective-permute-start.21) | collective-permute-done | bytes 65568 | tf_op jit(solution)/shard_map/ppermute | solution.py:26
  70.9 0.5 shard_map.82.refs_3_
  71.4 0.1 collective-permute-start.22
  71.5 2.1 %collective-permute-start.23 = (bf16[32,1024]{1,0:T(8,128)(2,1)S(1)}, bf16[32,1024]{1,0:T(8,128)(2,1)S(1)}, u32[]{:S(2)}, u32[]{:S(2)}) collective-permute-start(bf16[32,1024]{1,0:T(8,128)(2,1)S(1)} %shard_map.82.refs_3_), channel_id=1, source_target_pairs={{0,2},{1,3},{2,0},{3,1},{4,6},{5,7},{6,4},{7,5},{8,10},{9,11},{10,... | collective-permute-start | bytes 196616 | tf_op jit(solution)/shard_map/ppermute | solution.py:26
  73.6 2.3 %collective-permute-start.24 = (bf16[32,1024]{1,0:T(8,128)(2,1)S(1)}, bf16[32,1024]{1,0:T(8,128)(2,1)S(1)}, u32[]{:S(2)}, u32[]{:S(2)}) collective-permute-start(bf16[32,1024]{1,0:T(8,128)(2,1)S(1)} %shard_map.82.refs_3_), channel_id=1, source_target_pairs={{0,3},{1,2},{2,1},{3,0},{4,7},{5,6},{6,5},{7,4},{8,11},{9,10},{10,... | collective-permute-start | bytes 196616 | tf_op jit(solution)/shard_map/ppermute | solution.py:26
  75.9 0.3 collective-permute-done.22.refs_4_
  76.2 4.0 %collective-permute-done.23.refs_5_ = bf16[32,1024]{1,0:T(8,128)(2,1)S(1)} collective-permute-done((bf16[32,1024]{1,0:T(8,128)(2,1)S(1)}, bf16[32,1024]{1,0:T(8,128)(2,1)S(1)}, u32[]{:S(2)}, u32[]{:S(2)}) %collective-permute-start.23) | collective-permute-done | bytes 65568 | tf_op jit(solution)/shard_map/ppermute | solution.py:26
  80.2 2.2 %collective-permute-start.14 = (bf16[32,1024]{1,0:T(8,128)(2,1)S(1)}, bf16[32,1024]{1,0:T(8,128)(2,1)S(1)}, u32[]{:S(2)}, u32[]{:S(2)}) collective-permute-start(bf16[32,1024]{1,0:T(8,128)(2,1)S(1)} %get-tuple-element.42.refs_3_), channel_id=1, source_target_pairs={{0,3},{1,2},{2,1},{3,0},{4,7},{5,6},{6,5},{7,4},{8,11},{9,10},{10,... | collective-permute-start | bytes 196616 | tf_op jit(solution)/shard_map/ppermute | solution.py:26
  82.3 0.7 shard_map.83
  83.0 2.3 %collective-permute-done.13.refs_5_ = bf16[32,1024]{1,0:T(8,128)(2,1)S(1)} collective-permute-done((bf16[32,1024]{1,0:T(8,128)(2,1)S(1)}, bf16[32,1024]{1,0:T(8,128)(2,1)S(1)}, u32[]{:S(2)}, u32[]{:S(2)}) %collective-permute-start.13) | collective-permute-done | bytes 65568 | tf_op jit(solution)/shard_map/ppermute | solution.py:26
  85.3 0.9 %collective-permute-done.14.refs_6_ = bf16[32,1024]{1,0:T(8,128)(2,1)S(1)} collective-permute-done((bf16[32,1024]{1,0:T(8,128)(2,1)S(1)}, bf16[32,1024]{1,0:T(8,128)(2,1)S(1)}, u32[]{:S(2)}, u32[]{:S(2)}) %collective-permute-start.14) | collective-permute-done | bytes 65568 | tf_op jit(solution)/shard_map/ppermute | solution.py:26
  86.3 0.7 shard_map.80
  86.9 0.5 shard_map.84.refs_1_
  87.4 0.3 shard_map.85.refs_2_
  87.7 1.1 %shard_map.86 = bf16[256,1024]{1,0:T(8,128)(2,1)} custom-call(bf16[1024,1024]{1,0:T(8,128)(2,1)S(1)} %copy-done, bf16[256,512]{1,0:T(8,128)(2,1)S(1)} %shard_map.84.refs_1_, f32[256,512]{1,0:T(8,128)S(1)} %shard_map.85.refs_2_, bf16[4,128,256]{2,1,0:T(8,128)(2,1)S(1)} %get-tuple-element.51.refs_3_.refs_2_, ...), custom_call_target="tpu_custom_call" | custom-call | tf_op jit(solution)/shard_map/pallas_call | solution.py:40
  (38 shorter events, 0.1 us)
Async XLA Ops:
  0.0 6.7 %copy-start.5 = (bf16[2,512,256]{2,1,0:T(8,128)(2,1)S(1)}, bf16[2,512,256]{2,1,0:T(8,128)(2,1)}, u32[]{:S(2)}) copy-start(bf16[2,512,256]{2,1,0:T(8,128)(2,1)} %refs_1_.3) | copy-start | bytes 1572868
  0.0 6.7 %copy-start.6 = (bf16[1024,8]{0,1:T(8,128)(2,1)S(1)}, bf16[1024,8]{0,1:T(8,128)(2,1)}, u32[]{:S(2)}) copy-start(bf16[1024,8]{0,1:T(8,128)(2,1)} %param.9) | copy-start | bytes 49156
  0.0 6.7 %copy-start = (bf16[1024,1024]{1,0:T(8,128)(2,1)S(1)}, bf16[1024,1024]{1,0:T(8,128)(2,1)}, u32[]{:S(2)}) copy-start(bf16[1024,1024]{1,0:T(8,128)(2,1)} %refs_0_.11) | copy-start | bytes 6291460
  0.0 10.3 %collective-permute-start.4 = (bf16[2,128,256]{2,1,0:T(8,128)(2,1)}, bf16[2,128,256]{2,1,0:T(8,128)(2,1)S(1)}, u32[]{:S(2)}, u32[]{:S(2)}) collective-permute-start(bf16[2,128,256]{2,1,0:T(8,128)(2,1)} %refs_0_.8), channel_id=1, source_target_pairs={{0,8},{4,12},{8,0},{12,4},{1,9},{5,13},{9,1},{13,5},{2,10},{6,14},... | collective-permute-start | bytes 393224 | tf_op jit(solution)/shard_map/ppermute | solution.py:26
  3.1 8.8 %collective-permute-start.5 = (bf16[2,128,256]{2,1,0:T(8,128)(2,1)}, bf16[2,128,256]{2,1,0:T(8,128)(2,1)S(1)}, u32[]{:S(2)}, u32[]{:S(2)}) collective-permute-start(bf16[2,128,256]{2,1,0:T(8,128)(2,1)} %refs_0_.8), channel_id=1, source_target_pairs={{0,4},{4,0},{8,12},{12,8},{1,5},{5,1},{9,13},{13,9},{2,6},{6,2},{1... | collective-permute-start | bytes 393224 | tf_op jit(solution)/shard_map/ppermute | solution.py:26
  4.6 2.1 %collective-permute-start = (bf16[2,512,256]{2,1,0:T(8,128)(2,1)}, bf16[2,512,256]{2,1,0:T(8,128)(2,1)S(1)}, u32[]{:S(2)}, u32[]{:S(2)}) collective-permute-start(bf16[2,512,256]{2,1,0:T(8,128)(2,1)} %refs_1_.3), channel_id=1, source_target_pairs={{0,16},{16,0},{1,17},{17,1},{2,18},{18,2},{3,19},{19,3},{4,20},{20... | collective-permute-start | bytes 1572872 | tf_op jit(solution)/shard_map/ppermute | solution.py:463
  6.7 1.4 %copy-start.2 = (bf16[2,512,256]{2,1,0:T(8,128)(2,1)S(1)}, bf16[2,512,256]{2,1,0:T(8,128)(2,1)}, u32[]{:S(2)}) copy-start(bf16[2,512,256]{2,1,0:T(8,128)(2,1)} %refs_0_.9) | copy-start | bytes 1572868
  7.5 6.4 %collective-permute-start.1 = (bf16[128,512]{1,0:T(8,128)(2,1)S(1)}, bf16[128,512]{1,0:T(8,128)(2,1)S(1)}, u32[]{:S(2)}, u32[]{:S(2)}) collective-permute-start(bf16[128,512]{1,0:T(8,128)(2,1)S(1)} %get-tuple-element.30), channel_id=1, source_target_pairs={{0,4},{4,0},{8,12},{12,8},{1,5},{5,1},{9,13},{13,9},{2,6},{6,2},{1... | collective-permute-start | bytes 393224 | tf_op jit(solution)/shard_map/ppermute | solution.py:26
  8.3 40.4 %collective-permute-start.16 = (bf16[2,256,512]{2,1,0:T(8,128)(2,1)S(1)}, bf16[2,256,512]{2,1,0:T(8,128)(2,1)S(1)}, u32[]{:S(2)}, u32[]{:S(2)}) collective-permute-start(bf16[2,256,512]{2,1,0:T(8,128)(2,1)S(1)} %shard_map.79.refs_7_), channel_id=1, source_target_pairs={{0,4},{4,0},{8,12},{12,8},{1,5},{5,1},{9,13},{13,9},{2,6},{6,2},{1... | collective-permute-start | bytes 1572872 | tf_op jit(solution)/shard_map/ppermute | solution.py:26
  9.8 38.9 %collective-permute-start.25 = (bf16[2,256,512]{2,1,0:T(8,128)(2,1)S(1)}, bf16[2,256,512]{2,1,0:T(8,128)(2,1)S(1)}, u32[]{:S(2)}, u32[]{:S(2)}) collective-permute-start(bf16[2,256,512]{2,1,0:T(8,128)(2,1)S(1)} %shard_map.79.refs_7_), channel_id=1, source_target_pairs={{0,8},{4,12},{8,0},{12,4},{1,9},{5,13},{9,1},{13,5},{2,10},{6,14},... | collective-permute-start | bytes 1572872 | tf_op jit(solution)/shard_map/ppermute | solution.py:26
  10.3 41.1 %collective-permute-start.26 = (bf16[2,256,512]{2,1,0:T(8,128)(2,1)S(1)}, bf16[2,256,512]{2,1,0:T(8,128)(2,1)S(1)}, u32[]{:S(2)}, u32[]{:S(2)}) collective-permute-start(bf16[2,256,512]{2,1,0:T(8,128)(2,1)S(1)} %shard_map.79.refs_7_), channel_id=1, source_target_pairs={{0,12},{4,8},{8,4},{12,0},{1,13},{5,9},{9,5},{13,1},{2,14},{6,10},... | collective-permute-start | bytes 1572872 | tf_op jit(solution)/shard_map/ppermute | solution.py:26
  11.8 28.3 %collective-permute-start.2 = (bf16[128,512]{1,0:T(8,128)(2,1)S(1)}, bf16[128,512]{1,0:T(8,128)(2,1)S(1)}, u32[]{:S(2)}, u32[]{:S(2)}) collective-permute-start(bf16[128,512]{1,0:T(8,128)(2,1)S(1)} %get-tuple-element.31), channel_id=1, source_target_pairs={{0,8},{4,12},{8,0},{12,4},{1,9},{5,13},{9,1},{13,5},{2,10},{6,14},... | collective-permute-start | bytes 393224 | tf_op jit(solution)/shard_map/ppermute | solution.py:26
  13.9 32.3 %copy-start.1 = (s32[1024,4]{0,1:T(4,128)S(1)}, s32[1024,4]{0,1:T(4,128)}, u32[]{:S(2)}) copy-start(s32[1024,4]{0,1:T(4,128)} %param.8) | copy-start | bytes 49156
  13.9 34.6 %copy-start.3 = (bf16[2,128,256]{2,1,0:T(8,128)(2,1)S(1)}, bf16[2,128,256]{2,1,0:T(8,128)(2,1)}, u32[]{:S(2)}) copy-start(bf16[2,128,256]{2,1,0:T(8,128)(2,1)} %refs_0_.8) | copy-start | bytes 393220
  13.9 26.7 %collective-permute-start.3 = (bf16[128,512]{1,0:T(8,128)(2,1)S(1)}, bf16[128,512]{1,0:T(8,128)(2,1)S(1)}, u32[]{:S(2)}, u32[]{:S(2)}) collective-permute-start(bf16[128,512]{1,0:T(8,128)(2,1)S(1)} %get-tuple-element.32), channel_id=1, source_target_pairs={{0,12},{4,8},{8,4},{12,0},{1,13},{5,9},{9,5},{13,1},{2,14},{6,10},... | collective-permute-start | bytes 393224 | tf_op jit(solution)/shard_map/ppermute | solution.py:26
  40.1 5.7 %collective-permute-start.10 = (bf16[192,512]{1,0:T(8,128)(2,1)S(1)}, bf16[192,512]{1,0:T(8,128)(2,1)S(1)}, u32[]{:S(2)}, u32[]{:S(2)}) collective-permute-start(bf16[192,512]{1,0:T(8,128)(2,1)S(1)} %get-tuple-element.40), channel_id=1, source_target_pairs={{0,8},{4,12},{8,0},{12,4},{1,9},{5,13},{9,1},{13,5},{2,10},{6,14},... | collective-permute-start | bytes 589832 | tf_op jit(solution)/shard_map/ppermute | solution.py:26
  40.6 6.3 %collective-permute-start.9 = (bf16[192,512]{1,0:T(8,128)(2,1)S(1)}, bf16[192,512]{1,0:T(8,128)(2,1)S(1)}, u32[]{:S(2)}, u32[]{:S(2)}) collective-permute-start(bf16[192,512]{1,0:T(8,128)(2,1)S(1)} %get-tuple-element.39), channel_id=1, source_target_pairs={{0,4},{4,0},{8,12},{12,8},{1,5},{5,1},{9,13},{13,9},{2,6},{6,2},{1... | collective-permute-start | bytes 589832 | tf_op jit(solution)/shard_map/ppermute | solution.py:26
  45.8 5.9 %collective-permute-start.18 = (bf16[128,512]{1,0:T(8,128)(2,1)S(1)}, bf16[128,512]{1,0:T(8,128)(2,1)S(1)}, u32[]{:S(2)}, u32[]{:S(2)}) collective-permute-start(bf16[128,512]{1,0:T(8,128)(2,1)S(1)} %get-tuple-element.45), channel_id=1, source_target_pairs={{0,12},{4,8},{8,4},{12,0},{1,13},{5,9},{9,5},{13,1},{2,14},{6,10},... | collective-permute-start | bytes 393224 | tf_op jit(solution)/shard_map/ppermute | solution.py:26
  46.9 35.4 %copy-start.4 = (f32[1024]{0:T(1024)S(1)}, f32[1024]{0:T(1024)}, u32[]{:S(2)}) copy-start(f32[1024]{0:T(1024)} %param.13) | copy-start | bytes 12292
  46.9 4.8 %collective-permute-start.6 = (bf16[32,1152]{1,0:T(8,128)(2,1)S(1)}, bf16[32,1152]{1,0:T(8,128)(2,1)S(1)}, u32[]{:S(2)}, u32[]{:S(2)}) collective-permute-start(bf16[32,1152]{1,0:T(8,128)(2,1)S(1)} %get-tuple-element.36), channel_id=1, source_target_pairs={{0,1},{1,0},{2,3},{3,2},{4,5},{5,4},{6,7},{7,6},{8,9},{9,8},{10,11... | collective-permute-start | bytes 221192 | tf_op jit(solution)/shard_map/ppermute | solution.py:26
  48.7 15.9 %collective-permute-start.11 = (bf16[8,256,128]{2,1,0:T(8,128)(2,1)S(1)}, bf16[8,256,128]{2,1,0:T(8,128)(2,1)S(1)}, u32[]{:S(2)}, u32[]{:S(2)}) collective-permute-start(bf16[8,256,128]{2,1,0:T(8,128)(2,1)S(1)} %shard_map.77.refs_5_.refs_6_), channel_id=1, source_target_pairs={{0,16},{16,0},{1,17},{17,1},{2,18},{18,2},{3,19},{19,3},{4,20},{20... | collective-permute-start | bytes 1572872 | tf_op jit(solution)/shard_map/ppermute | solution.py:463
  48.8 8.9 %collective-permute-start.7 = (bf16[32,1152]{1,0:T(8,128)(2,1)S(1)}, bf16[32,1152]{1,0:T(8,128)(2,1)S(1)}, u32[]{:S(2)}, u32[]{:S(2)}) collective-permute-start(bf16[32,1152]{1,0:T(8,128)(2,1)S(1)} %get-tuple-element.37), channel_id=1, source_target_pairs={{0,2},{1,3},{2,0},{3,1},{4,6},{5,7},{6,4},{7,5},{8,10},{9,11},{10,... | collective-permute-start | bytes 221192 | tf_op jit(solution)/shard_map/ppermute | solution.py:26
  51.4 6.3 %collective-permute-start.8 = (bf16[32,1152]{1,0:T(8,128)(2,1)S(1)}, bf16[32,1152]{1,0:T(8,128)(2,1)S(1)}, u32[]{:S(2)}, u32[]{:S(2)}) collective-permute-start(bf16[32,1152]{1,0:T(8,128)(2,1)S(1)} %get-tuple-element.38), channel_id=1, source_target_pairs={{0,3},{1,2},{2,1},{3,0},{4,7},{5,6},{6,5},{7,4},{8,11},{9,10},{10,... | collective-permute-start | bytes 221192 | tf_op jit(solution)/shard_map/ppermute | solution.py:26
  51.6 19.9 %collective-permute-start.15 = (bf16[2,256,512]{2,1,0:T(8,128)(2,1)S(1)}, bf16[2,256,512]{2,1,0:T(8,128)(2,1)S(1)}, u32[]{:S(2)}, u32[]{:S(2)}) collective-permute-start(bf16[2,256,512]{2,1,0:T(8,128)(2,1)S(1)} %shard_map.79.refs_7_), channel_id=1, source_target_pairs={{0,16},{16,0},{1,17},{17,1},{2,18},{18,2},{3,19},{19,3},{4,20},{20... | collective-permute-start | bytes 1572872 | tf_op jit(solution)/shard_map/ppermute | solution.py:463
  51.7 21.9 %collective-permute-start.17 = (bf16[2,256,512]{2,1,0:T(8,128)(2,1)S(1)}, bf16[2,256,512]{2,1,0:T(8,128)(2,1)S(1)}, u32[]{:S(2)}, u32[]{:S(2)}) collective-permute-start(bf16[2,256,512]{2,1,0:T(8,128)(2,1)S(1)} %collective-permute-done.16.refs_9_), channel_id=1, source_target_pairs={{0,16},{16,0},{1,17},{17,1},{2,18},{18,2},{3,19},{19,3},{4,20},{20... | collective-permute-start | bytes 1572872 | tf_op jit(solution)/shard_map/ppermute | solution.py:463
  57.7 4.8 %collective-permute-start.19 = (bf16[32,1024]{1,0:T(8,128)(2,1)S(1)}, bf16[32,1024]{1,0:T(8,128)(2,1)S(1)}, u32[]{:S(2)}, u32[]{:S(2)}) collective-permute-start(bf16[32,1024]{1,0:T(8,128)(2,1)S(1)} %get-tuple-element.47), channel_id=1, source_target_pairs={{0,1},{1,0},{2,3},{3,2},{4,5},{5,4},{6,7},{7,6},{8,9},{9,8},{10,11... | collective-permute-start | bytes 196616 | tf_op jit(solution)/shard_map/ppermute | solution.py:26
  57.7 6.9 %collective-permute-start.20 = (bf16[32,1024]{1,0:T(8,128)(2,1)S(1)}, bf16[32,1024]{1,0:T(8,128)(2,1)S(1)}, u32[]{:S(2)}, u32[]{:S(2)}) collective-permute-start(bf16[32,1024]{1,0:T(8,128)(2,1)S(1)} %get-tuple-element.48), channel_id=1, source_target_pairs={{0,2},{1,3},{2,0},{3,1},{4,6},{5,7},{6,4},{7,5},{8,10},{9,11},{10,... | collective-permute-start | bytes 196616 | tf_op jit(solution)/shard_map/ppermute | solution.py:26
  62.5 24.9 %collective-permute-start.27 = (bf16[2,256,512]{2,1,0:T(8,128)(2,1)S(1)}, bf16[2,256,512]{2,1,0:T(8,128)(2,1)S(1)}, u32[]{:S(2)}, u32[]{:S(2)}) collective-permute-start(bf16[2,256,512]{2,1,0:T(8,128)(2,1)S(1)} %collective-permute-done.25.refs_5_), channel_id=1, source_target_pairs={{0,16},{16,0},{1,17},{17,1},{2,18},{18,2},{3,19},{19,3},{4,20},{20... | collective-permute-start | bytes 1572872 | tf_op jit(solution)/shard_map/ppermute | solution.py:463
  64.6 23.1 %collective-permute-start.28 = (bf16[2,256,512]{2,1,0:T(8,128)(2,1)S(1)}, bf16[2,256,512]{2,1,0:T(8,128)(2,1)S(1)}, u32[]{:S(2)}, u32[]{:S(2)}) collective-permute-start(bf16[2,256,512]{2,1,0:T(8,128)(2,1)S(1)} %collective-permute-done.26.refs_6_), channel_id=1, source_target_pairs={{0,16},{16,0},{1,17},{17,1},{2,18},{18,2},{3,19},{19,3},{4,20},{20... | collective-permute-start | bytes 1572872 | tf_op jit(solution)/shard_map/ppermute | solution.py:463
  64.6 6.3 %collective-permute-start.21 = (bf16[32,1024]{1,0:T(8,128)(2,1)S(1)}, bf16[32,1024]{1,0:T(8,128)(2,1)S(1)}, u32[]{:S(2)}, u32[]{:S(2)}) collective-permute-start(bf16[32,1024]{1,0:T(8,128)(2,1)S(1)} %get-tuple-element.49), channel_id=1, source_target_pairs={{0,3},{1,2},{2,1},{3,0},{4,7},{5,6},{6,5},{7,4},{8,11},{9,10},{10,... | collective-permute-start | bytes 196616 | tf_op jit(solution)/shard_map/ppermute | solution.py:26
  71.4 4.7 %collective-permute-start.22 = (bf16[32,1024]{1,0:T(8,128)(2,1)S(1)}, bf16[32,1024]{1,0:T(8,128)(2,1)S(1)}, u32[]{:S(2)}, u32[]{:S(2)}) collective-permute-start(bf16[32,1024]{1,0:T(8,128)(2,1)S(1)} %shard_map.82.refs_3_), channel_id=1, source_target_pairs={{0,1},{1,0},{2,3},{3,2},{4,5},{5,4},{6,7},{7,6},{8,9},{9,8},{10,11... | collective-permute-start | bytes 196616 | tf_op jit(solution)/shard_map/ppermute | solution.py:26
  71.5 8.6 %collective-permute-start.23 = (bf16[32,1024]{1,0:T(8,128)(2,1)S(1)}, bf16[32,1024]{1,0:T(8,128)(2,1)S(1)}, u32[]{:S(2)}, u32[]{:S(2)}) collective-permute-start(bf16[32,1024]{1,0:T(8,128)(2,1)S(1)} %shard_map.82.refs_3_), channel_id=1, source_target_pairs={{0,2},{1,3},{2,0},{3,1},{4,6},{5,7},{6,4},{7,5},{8,10},{9,11},{10,... | collective-permute-start | bytes 196616 | tf_op jit(solution)/shard_map/ppermute | solution.py:26
  73.6 6.6 %collective-permute-start.24 = (bf16[32,1024]{1,0:T(8,128)(2,1)S(1)}, bf16[32,1024]{1,0:T(8,128)(2,1)S(1)}, u32[]{:S(2)}, u32[]{:S(2)}) collective-permute-start(bf16[32,1024]{1,0:T(8,128)(2,1)S(1)} %shard_map.82.refs_3_), channel_id=1, source_target_pairs={{0,3},{1,2},{2,1},{3,0},{4,7},{5,6},{6,5},{7,4},{8,11},{9,10},{10,... | collective-permute-start | bytes 196616 | tf_op jit(solution)/shard_map/ppermute | solution.py:26
  76.2 6.8 %collective-permute-start.12 = (bf16[32,1024]{1,0:T(8,128)(2,1)S(1)}, bf16[32,1024]{1,0:T(8,128)(2,1)S(1)}, u32[]{:S(2)}, u32[]{:S(2)}) collective-permute-start(bf16[32,1024]{1,0:T(8,128)(2,1)S(1)} %get-tuple-element.42.refs_3_), channel_id=1, source_target_pairs={{0,1},{1,0},{2,3},{3,2},{4,5},{5,4},{6,7},{7,6},{8,9},{9,8},{10,11... | collective-permute-start | bytes 196616 | tf_op jit(solution)/shard_map/ppermute | solution.py:26
  80.1 5.2 %collective-permute-start.13 = (bf16[32,1024]{1,0:T(8,128)(2,1)S(1)}, bf16[32,1024]{1,0:T(8,128)(2,1)S(1)}, u32[]{:S(2)}, u32[]{:S(2)}) collective-permute-start(bf16[32,1024]{1,0:T(8,128)(2,1)S(1)} %get-tuple-element.42.refs_3_), channel_id=1, source_target_pairs={{0,2},{1,3},{2,0},{3,1},{4,6},{5,7},{6,4},{7,5},{8,10},{9,11},{10,... | collective-permute-start | bytes 196616 | tf_op jit(solution)/shard_map/ppermute | solution.py:26
  80.2 6.1 %collective-permute-start.14 = (bf16[32,1024]{1,0:T(8,128)(2,1)S(1)}, bf16[32,1024]{1,0:T(8,128)(2,1)S(1)}, u32[]{:S(2)}, u32[]{:S(2)}) collective-permute-start(bf16[32,1024]{1,0:T(8,128)(2,1)S(1)} %get-tuple-element.42.refs_3_), channel_id=1, source_target_pairs={{0,3},{1,2},{2,1},{3,0},{4,7},{5,6},{6,5},{7,4},{8,11},{9,10},{10,... | collective-permute-start | bytes 196616 | tf_op jit(solution)/shard_map/ppermute | solution.py:26

commit v6 on v5

--- a/solution.py
+++ b/solution.py
@@ -410,21 +410,21 @@
 def finish(x, own, acc, lefts, wide, first):
     block, half = own.shape
     n_loc = wide.shape[0]
-    cut = half // 2
+    cuts = ((0, half // 2), (half // 2, half // 4), (3 * half // 4, half // 4))
 
     def body(place_ref, x_ref, own_ref, acc_ref, *refs):
         l_refs, (w_ref, out_ref, buf, sems) = refs[:-4], refs[-4:]
         here, there = place_ref[0] * half, (1 - place_ref[0]) * half
         mine = rows_at(place_ref[1] * block, block)
-        copies = [pltpu.make_async_copy(own_ref, out_ref.at[:, rows_at(here, half)], sems.at[2])]
+        copies = [pltpu.make_async_copy(own_ref, out_ref.at[:, rows_at(here, half)], sems.at[3])]
         copies[0].start()
-        for c in range(2):
-            part = slice(c * cut, (c + 1) * cut)
+        for c, (at, cut) in enumerate(cuts):
+            part = slice(at, at + cut)
             acc = acc_ref[:, part]
             for e in range(n_loc):
                 left = jnp.concatenate([r[first * n_loc + e] for r in l_refs], axis=0)
                 acc = acc + jnp.dot(left, w_ref[e, :, part], preferred_element_type=F32)
-            cols = rows_at(there + c * cut, cut)
+            cols = rows_at(there + at, cut)
             xs = x_ref[mine, cols].astype(F32)
             buf[:, part] = (xs + xs * acc).astype(BF16)
             copies.append(pltpu.make_async_copy(buf.at[:, part], out_ref.at[:, cols], sems.at[c]))
@@ -436,7 +436,7 @@
         body,
         [x, own, acc, *lefts, wide],
         [((block, 2 * half), BF16)],
-        [pltpu.VMEM((block, half), BF16), pltpu.SemaphoreType.DMA((3,))],
+        [pltpu.VMEM((block, half), BF16), pltpu.SemaphoreType.DMA((4,))],
         held=("out",),
     )[0]
 

time: 88.9 us -> 88.9 us (level)
  no operation moved by 1% of the time
where the time goes in v6:
time: 88.9 us; the launch traced here: 88.8 us
  waiting for transfers between devices  54.3 us (61%)
  starting transfers between devices  27.6 us (31%)
  Pallas kernels  6.69 us (8%)
    ppermute x23, waiting for transfers between devices, send(): return lax.ppermute(x, axis, [(i, peer_to(i, m, n)) for i in range(n)])  52.2 us
    ppermute x23, starting transfers between devices, send(): return lax.ppermute(x, axis, [(i, peer_to(i, m, n)) for i in range(n)])  27 us
    pallas_call x14, Pallas kernels, call(): pl.pallas_call(placed, in_specs=[space(k) for k in range(len(args))], out...  6.69 us
    ppermute x6, waiting for transfers between devices, swap(): return lax.ppermute(w, 'batch', [(0, 1), (1, 0)])  2.13 us
  transfers between devices with their start and end apart: 29, of which 13 were waited for; matrix products, arithmetic and copies ran while one was open for 0% of the time, Pallas kernels for 6%

profile of v6, /device:TPU:0, one launch (start us, length us, event | category | flops | bytes accessed | tf_op | source)
XLA Modules:
  0.0 88.8 jit_solution(3467113569275947332)
XLA Ops:
  0.0 3.1 %collective-permute-start.4 = (bf16[2,128,256]{2,1,0:T(8,128)(2,1)}, bf16[2,128,256]{2,1,0:T(8,128)(2,1)S(1)}, u32[]{:S(2)}, u32[]{:S(2)}) collective-permute-start(bf16[2,128,256]{2,1,0:T(8,128)(2,1)} %refs_0_.8), channel_id=1, source_target_pairs={{0,8},{4,12},{8,0},{12,4},{1,9},{5,13},{9,1},{13,5},{2,10},{6,14},... | collective-permute-start | bytes 393224 | tf_op jit(solution)/shard_map/ppermute | solution.py:26
  3.1 1.5 %collective-permute-start.5 = (bf16[2,128,256]{2,1,0:T(8,128)(2,1)}, bf16[2,128,256]{2,1,0:T(8,128)(2,1)S(1)}, u32[]{:S(2)}, u32[]{:S(2)}) collective-permute-start(bf16[2,128,256]{2,1,0:T(8,128)(2,1)} %refs_0_.8), channel_id=1, source_target_pairs={{0,4},{4,0},{8,12},{12,8},{1,5},{5,1},{9,13},{13,9},{2,6},{6,2},{1... | collective-permute-start | bytes 393224 | tf_op jit(solution)/shard_map/ppermute | solution.py:26
  4.6 2.1 %collective-permute-done.refs_2_ = bf16[2,512,256]{2,1,0:T(8,128)(2,1)S(1)} collective-permute-done((bf16[2,512,256]{2,1,0:T(8,128)(2,1)}, bf16[2,512,256]{2,1,0:T(8,128)(2,1)S(1)}, u32[]{:S(2)}, u32[]{:S(2)}) %collective-permute-start) | collective-permute-done | bytes 524320 | tf_op jit(solution)/shard_map/ppermute | solution.py:463
  6.7 0.8 shard_map.74
  7.5 0.6 collective-permute-start.1
  8.1 0.2 shard_map.79.refs_7_
  8.3 1.6 %collective-permute-start.16 = (bf16[2,256,512]{2,1,0:T(8,128)(2,1)S(1)}, bf16[2,256,512]{2,1,0:T(8,128)(2,1)S(1)}, u32[]{:S(2)}, u32[]{:S(2)}) collective-permute-start(bf16[2,256,512]{2,1,0:T(8,128)(2,1)S(1)} %shard_map.79.refs_7_), channel_id=1, source_target_pairs={{0,4},{4,0},{8,12},{12,8},{1,5},{5,1},{9,13},{13,9},{2,6},{6,2},{1... | collective-permute-start | bytes 1572872 | tf_op jit(solution)/shard_map/ppermute | solution.py:26
  9.8 0.5 collective-permute-start.25
  10.3 1.5 %collective-permute-start.26 = (bf16[2,256,512]{2,1,0:T(8,128)(2,1)S(1)}, bf16[2,256,512]{2,1,0:T(8,128)(2,1)S(1)}, u32[]{:S(2)}, u32[]{:S(2)}) collective-permute-start(bf16[2,256,512]{2,1,0:T(8,128)(2,1)S(1)} %shard_map.79.refs_7_), channel_id=1, source_target_pairs={{0,12},{4,8},{8,4},{12,0},{1,13},{5,9},{9,5},{13,1},{2,14},{6,10},... | collective-permute-start | bytes 1572872 | tf_op jit(solution)/shard_map/ppermute | solution.py:26
  11.8 0.2 collective-permute-start.2
  12.0 1.9 %collective-permute-done.1.refs_2_ = bf16[128,512]{1,0:T(8,128)(2,1)S(1)} collective-permute-done((bf16[128,512]{1,0:T(8,128)(2,1)S(1)}, bf16[128,512]{1,0:T(8,128)(2,1)S(1)}, u32[]{:S(2)}, u32[]{:S(2)}) %collective-permute-start.1) | collective-permute-done | bytes 131104 | tf_op jit(solution)/shard_map/ppermute | solution.py:26
  13.9 0.9 collective-permute-start.3
  14.8 0.8 shard_map.75
  15.6 24.5 %collective-permute-done.2.refs_3_ = bf16[128,512]{1,0:T(8,128)(2,1)S(1)} collective-permute-done((bf16[128,512]{1,0:T(8,128)(2,1)S(1)}, bf16[128,512]{1,0:T(8,128)(2,1)S(1)}, u32[]{:S(2)}, u32[]{:S(2)}) %collective-permute-start.2) | collective-permute-done | bytes 131104 | tf_op jit(solution)/shard_map/ppermute | solution.py:26
  40.1 0.5 collective-permute-start.10
  40.6 0.5 collective-permute-start.9
  41.1 4.7 %collective-permute-done.10.refs_4_.refs_3_ = bf16[192,512]{1,0:T(8,128)(2,1)S(1)} collective-permute-done((bf16[192,512]{1,0:T(8,128)(2,1)S(1)}, bf16[192,512]{1,0:T(8,128)(2,1)S(1)}, u32[]{:S(2)}, u32[]{:S(2)}) %collective-permute-start.10) | collective-permute-done | bytes 196640 | tf_op jit(solution)/shard_map/ppermute | solution.py:26
  45.8 0.4 collective-permute-start.18
  46.2 0.3 shard_map.76
  46.5 0.4 collective-permute-done.9.refs_3_.refs_2_
  46.9 1.6 %collective-permute-start.6 = (bf16[32,1152]{1,0:T(8,128)(2,1)S(1)}, bf16[32,1152]{1,0:T(8,128)(2,1)S(1)}, u32[]{:S(2)}, u32[]{:S(2)}) collective-permute-start(bf16[32,1152]{1,0:T(8,128)(2,1)S(1)} %get-tuple-element.36), channel_id=1, source_target_pairs={{0,1},{1,0},{2,3},{3,2},{4,5},{5,4},{6,7},{7,6},{8,9},{9,8},{10,11... | collective-permute-start | bytes 221192 | tf_op jit(solution)/shard_map/ppermute | solution.py:26
  48.5 0.2 shard_map.77.refs_5_.refs_6_
  48.7 0.1 collective-permute-start.11
  48.8 2.7 %collective-permute-start.7 = (bf16[32,1152]{1,0:T(8,128)(2,1)S(1)}, bf16[32,1152]{1,0:T(8,128)(2,1)S(1)}, u32[]{:S(2)}, u32[]{:S(2)}) collective-permute-start(bf16[32,1152]{1,0:T(8,128)(2,1)S(1)} %get-tuple-element.37), channel_id=1, source_target_pairs={{0,2},{1,3},{2,0},{3,1},{4,6},{5,7},{6,4},{7,5},{8,10},{9,11},{10,... | collective-permute-start | bytes 221192 | tf_op jit(solution)/shard_map/ppermute | solution.py:26
  51.4 0.2 collective-permute-start.8
  51.7 0.5 collective-permute-start.17
  52.2 0.3 shard_map.81
  52.4 5.3 %collective-permute-done.7.refs_3_ = bf16[32,1152]{1,0:T(8,128)(2,1)S(1)} collective-permute-done((bf16[32,1152]{1,0:T(8,128)(2,1)S(1)}, bf16[32,1152]{1,0:T(8,128)(2,1)S(1)}, u32[]{:S(2)}, u32[]{:S(2)}) %collective-permute-start.7) | collective-permute-done | bytes 73760 | tf_op jit(solution)/shard_map/ppermute | solution.py:26
  57.7 3.4 %collective-permute-start.20 = (bf16[32,1024]{1,0:T(8,128)(2,1)S(1)}, bf16[32,1024]{1,0:T(8,128)(2,1)S(1)}, u32[]{:S(2)}, u32[]{:S(2)}) collective-permute-start(bf16[32,1024]{1,0:T(8,128)(2,1)S(1)} %get-tuple-element.48), channel_id=1, source_target_pairs={{0,2},{1,3},{2,0},{3,1},{4,6},{5,7},{6,4},{7,5},{8,10},{9,11},{10,... | collective-permute-start | bytes 196616 | tf_op jit(solution)/shard_map/ppermute | solution.py:26
  61.1 1.4 %collective-permute-done.19.refs_3_ = bf16[32,1024]{1,0:T(8,128)(2,1)S(1)} collective-permute-done((bf16[32,1024]{1,0:T(8,128)(2,1)S(1)}, bf16[32,1024]{1,0:T(8,128)(2,1)S(1)}, u32[]{:S(2)}, u32[]{:S(2)}) %collective-permute-start.19) | collective-permute-done | bytes 65568 | tf_op jit(solution)/shard_map/ppermute | solution.py:26
  62.5 2.1 %collective-permute-done.20.refs_4_ = bf16[32,1024]{1,0:T(8,128)(2,1)S(1)} collective-permute-done((bf16[32,1024]{1,0:T(8,128)(2,1)S(1)}, bf16[32,1024]{1,0:T(8,128)(2,1)S(1)}, u32[]{:S(2)}, u32[]{:S(2)}) %collective-permute-start.20) | collective-permute-done | bytes 65568 | tf_op jit(solution)/shard_map/ppermute | solution.py:26
  64.6 1.4 %collective-permute-start.21 = (bf16[32,1024]{1,0:T(8,128)(2,1)S(1)}, bf16[32,1024]{1,0:T(8,128)(2,1)S(1)}, u32[]{:S(2)}, u32[]{:S(2)}) collective-permute-start(bf16[32,1024]{1,0:T(8,128)(2,1)S(1)} %get-tuple-element.49), channel_id=1, source_target_pairs={{0,3},{1,2},{2,1},{3,0},{4,7},{5,6},{6,5},{7,4},{8,11},{9,10},{10,... | collective-permute-start | bytes 196616 | tf_op jit(solution)/shard_map/ppermute | solution.py:26
  66.0 0.5 shard_map.78
  66.6 4.3 %collective-permute-done.21.refs_5_ = bf16[32,1024]{1,0:T(8,128)(2,1)S(1)} collective-permute-done((bf16[32,1024]{1,0:T(8,128)(2,1)S(1)}, bf16[32,1024]{1,0:T(8,128)(2,1)S(1)}, u32[]{:S(2)}, u32[]{:S(2)}) %collective-permute-start.21) | collective-permute-done | bytes 65568 | tf_op jit(solution)/shard_map/ppermute | solution.py:26
  70.9 0.5 shard_map.82.refs_3_
  71.4 0.1 collective-permute-start.22
  71.5 2.1 %collective-permute-start.23 = (bf16[32,1024]{1,0:T(8,128)(2,1)S(1)}, bf16[32,1024]{1,0:T(8,128)(2,1)S(1)}, u32[]{:S(2)}, u32[]{:S(2)}) collective-permute-start(bf16[32,1024]{1,0:T(8,128)(2,1)S(1)} %shard_map.82.refs_3_), channel_id=1, source_target_pairs={{0,2},{1,3},{2,0},{3,1},{4,6},{5,7},{6,4},{7,5},{8,10},{9,11},{10,... | collective-permute-start | bytes 196616 | tf_op jit(solution)/shard_map/ppermute | solution.py:26
  73.6 2.3 %collective-permute-start.24 = (bf16[32,1024]{1,0:T(8,128)(2,1)S(1)}, bf16[32,1024]{1,0:T(8,128)(2,1)S(1)}, u32[]{:S(2)}, u32[]{:S(2)}) collective-permute-start(bf16[32,1024]{1,0:T(8,128)(2,1)S(1)} %shard_map.82.refs_3_), channel_id=1, source_target_pairs={{0,3},{1,2},{2,1},{3,0},{4,7},{5,6},{6,5},{7,4},{8,11},{9,10},{10,... | collective-permute-start | bytes 196616 | tf_op jit(solution)/shard_map/ppermute | solution.py:26
  75.9 0.3 collective-permute-done.22.refs_4_
  76.2 4.0 %collective-permute-done.23.refs_5_ = bf16[32,1024]{1,0:T(8,128)(2,1)S(1)} collective-permute-done((bf16[32,1024]{1,0:T(8,128)(2,1)S(1)}, bf16[32,1024]{1,0:T(8,128)(2,1)S(1)}, u32[]{:S(2)}, u32[]{:S(2)}) %collective-permute-start.23) | collective-permute-done | bytes 65568 | tf_op jit(solution)/shard_map/ppermute | solution.py:26
  80.2 2.2 %collective-permute-start.14 = (bf16[32,1024]{1,0:T(8,128)(2,1)S(1)}, bf16[32,1024]{1,0:T(8,128)(2,1)S(1)}, u32[]{:S(2)}, u32[]{:S(2)}) collective-permute-start(bf16[32,1024]{1,0:T(8,128)(2,1)S(1)} %get-tuple-element.42.refs_3_), channel_id=1, source_target_pairs={{0,3},{1,2},{2,1},{3,0},{4,7},{5,6},{6,5},{7,4},{8,11},{9,10},{10,... | collective-permute-start | bytes 196616 | tf_op jit(solution)/shard_map/ppermute | solution.py:26
  82.3 0.7 shard_map.83
  83.0 2.3 %collective-permute-done.13.refs_5_ = bf16[32,1024]{1,0:T(8,128)(2,1)S(1)} collective-permute-done((bf16[32,1024]{1,0:T(8,128)(2,1)S(1)}, bf16[32,1024]{1,0:T(8,128)(2,1)S(1)}, u32[]{:S(2)}, u32[]{:S(2)}) %collective-permute-start.13) | collective-permute-done | bytes 65568 | tf_op jit(solution)/shard_map/ppermute | solution.py:26
  85.3 0.9 %collective-permute-done.14.refs_6_ = bf16[32,1024]{1,0:T(8,128)(2,1)S(1)} collective-permute-done((bf16[32,1024]{1,0:T(8,128)(2,1)S(1)}, bf16[32,1024]{1,0:T(8,128)(2,1)S(1)}, u32[]{:S(2)}, u32[]{:S(2)}) %collective-permute-start.14) | collective-permute-done | bytes 65568 | tf_op jit(solution)/shard_map/ppermute | solution.py:26
  86.3 0.7 shard_map.80
  86.9 0.5 shard_map.84.refs_1_
  87.4 0.3 shard_map.85.refs_2_
  87.7 1.0 %shard_map.86 = bf16[256,1024]{1,0:T(8,128)(2,1)} custom-call(bf16[1024,1024]{1,0:T(8,128)(2,1)S(1)} %copy-done, bf16[256,512]{1,0:T(8,128)(2,1)S(1)} %shard_map.84.refs_1_, f32[256,512]{1,0:T(8,128)S(1)} %shard_map.85.refs_2_, bf16[4,128,256]{2,1,0:T(8,128)(2,1)S(1)} %get-tuple-element.51.refs_3_.refs_2_, ...), custom_call_target="tpu_custom_call" | custom-call | tf_op jit(solution)/shard_map/pallas_call | solution.py:40
  (38 shorter events, 0.1 us)
Async XLA Ops:
  0.0 6.7 %copy-start.5 = (bf16[2,512,256]{2,1,0:T(8,128)(2,1)S(1)}, bf16[2,512,256]{2,1,0:T(8,128)(2,1)}, u32[]{:S(2)}) copy-start(bf16[2,512,256]{2,1,0:T(8,128)(2,1)} %refs_1_.3) | copy-start | bytes 1572868
  0.0 6.7 %copy-start.6 = (bf16[1024,8]{0,1:T(8,128)(2,1)S(1)}, bf16[1024,8]{0,1:T(8,128)(2,1)}, u32[]{:S(2)}) copy-start(bf16[1024,8]{0,1:T(8,128)(2,1)} %param.9) | copy-start | bytes 49156
  0.0 6.7 %copy-start = (bf16[1024,1024]{1,0:T(8,128)(2,1)S(1)}, bf16[1024,1024]{1,0:T(8,128)(2,1)}, u32[]{:S(2)}) copy-start(bf16[1024,1024]{1,0:T(8,128)(2,1)} %refs_0_.11) | copy-start | bytes 6291460
  0.0 10.3 %collective-permute-start.4 = (bf16[2,128,256]{2,1,0:T(8,128)(2,1)}, bf16[2,128,256]{2,1,0:T(8,128)(2,1)S(1)}, u32[]{:S(2)}, u32[]{:S(2)}) collective-permute-start(bf16[2,128,256]{2,1,0:T(8,128)(2,1)} %refs_0_.8), channel_id=1, source_target_pairs={{0,8},{4,12},{8,0},{12,4},{1,9},{5,13},{9,1},{13,5},{2,10},{6,14},... | collective-permute-start | bytes 393224 | tf_op jit(solution)/shard_map/ppermute | solution.py:26
  3.1 8.8 %collective-permute-start.5 = (bf16[2,128,256]{2,1,0:T(8,128)(2,1)}, bf16[2,128,256]{2,1,0:T(8,128)(2,1)S(1)}, u32[]{:S(2)}, u32[]{:S(2)}) collective-permute-start(bf16[2,128,256]{2,1,0:T(8,128)(2,1)} %refs_0_.8), channel_id=1, source_target_pairs={{0,4},{4,0},{8,12},{12,8},{1,5},{5,1},{9,13},{13,9},{2,6},{6,2},{1... | collective-permute-start | bytes 393224 | tf_op jit(solution)/shard_map/ppermute | solution.py:26
  4.6 2.1 %collective-permute-start = (bf16[2,512,256]{2,1,0:T(8,128)(2,1)}, bf16[2,512,256]{2,1,0:T(8,128)(2,1)S(1)}, u32[]{:S(2)}, u32[]{:S(2)}) collective-permute-start(bf16[2,512,256]{2,1,0:T(8,128)(2,1)} %refs_1_.3), channel_id=1, source_target_pairs={{0,16},{16,0},{1,17},{17,1},{2,18},{18,2},{3,19},{19,3},{4,20},{20... | collective-permute-start | bytes 1572872 | tf_op jit(solution)/shard_map/ppermute | solution.py:463
  6.7 1.4 %copy-start.2 = (bf16[2,512,256]{2,1,0:T(8,128)(2,1)S(1)}, bf16[2,512,256]{2,1,0:T(8,128)(2,1)}, u32[]{:S(2)}) copy-start(bf16[2,512,256]{2,1,0:T(8,128)(2,1)} %refs_0_.9) | copy-start | bytes 1572868
  7.5 6.4 %collective-permute-start.1 = (bf16[128,512]{1,0:T(8,128)(2,1)S(1)}, bf16[128,512]{1,0:T(8,128)(2,1)S(1)}, u32[]{:S(2)}, u32[]{:S(2)}) collective-permute-start(bf16[128,512]{1,0:T(8,128)(2,1)S(1)} %get-tuple-element.30), channel_id=1, source_target_pairs={{0,4},{4,0},{8,12},{12,8},{1,5},{5,1},{9,13},{13,9},{2,6},{6,2},{1... | collective-permute-start | bytes 393224 | tf_op jit(solution)/shard_map/ppermute | solution.py:26
  8.3 40.4 %collective-permute-start.16 = (bf16[2,256,512]{2,1,0:T(8,128)(2,1)S(1)}, bf16[2,256,512]{2,1,0:T(8,128)(2,1)S(1)}, u32[]{:S(2)}, u32[]{:S(2)}) collective-permute-start(bf16[2,256,512]{2,1,0:T(8,128)(2,1)S(1)} %shard_map.79.refs_7_), channel_id=1, source_target_pairs={{0,4},{4,0},{8,12},{12,8},{1,5},{5,1},{9,13},{13,9},{2,6},{6,2},{1... | collective-permute-start | bytes 1572872 | tf_op jit(solution)/shard_map/ppermute | solution.py:26
  9.8 38.9 %collective-permute-start.25 = (bf16[2,256,512]{2,1,0:T(8,128)(2,1)S(1)}, bf16[2,256,512]{2,1,0:T(8,128)(2,1)S(1)}, u32[]{:S(2)}, u32[]{:S(2)}) collective-permute-start(bf16[2,256,512]{2,1,0:T(8,128)(2,1)S(1)} %shard_map.79.refs_7_), channel_id=1, source_target_pairs={{0,8},{4,12},{8,0},{12,4},{1,9},{5,13},{9,1},{13,5},{2,10},{6,14},... | collective-permute-start | bytes 1572872 | tf_op jit(solution)/shard_map/ppermute | solution.py:26
  10.3 41.1 %collective-permute-start.26 = (bf16[2,256,512]{2,1,0:T(8,128)(2,1)S(1)}, bf16[2,256,512]{2,1,0:T(8,128)(2,1)S(1)}, u32[]{:S(2)}, u32[]{:S(2)}) collective-permute-start(bf16[2,256,512]{2,1,0:T(8,128)(2,1)S(1)} %shard_map.79.refs_7_), channel_id=1, source_target_pairs={{0,12},{4,8},{8,4},{12,0},{1,13},{5,9},{9,5},{13,1},{2,14},{6,10},... | collective-permute-start | bytes 1572872 | tf_op jit(solution)/shard_map/ppermute | solution.py:26
  11.8 28.3 %collective-permute-start.2 = (bf16[128,512]{1,0:T(8,128)(2,1)S(1)}, bf16[128,512]{1,0:T(8,128)(2,1)S(1)}, u32[]{:S(2)}, u32[]{:S(2)}) collective-permute-start(bf16[128,512]{1,0:T(8,128)(2,1)S(1)} %get-tuple-element.31), channel_id=1, source_target_pairs={{0,8},{4,12},{8,0},{12,4},{1,9},{5,13},{9,1},{13,5},{2,10},{6,14},... | collective-permute-start | bytes 393224 | tf_op jit(solution)/shard_map/ppermute | solution.py:26
  13.9 32.3 %copy-start.1 = (s32[1024,4]{0,1:T(4,128)S(1)}, s32[1024,4]{0,1:T(4,128)}, u32[]{:S(2)}) copy-start(s32[1024,4]{0,1:T(4,128)} %param.8) | copy-start | bytes 49156
  13.9 34.6 %copy-start.3 = (bf16[2,128,256]{2,1,0:T(8,128)(2,1)S(1)}, bf16[2,128,256]{2,1,0:T(8,128)(2,1)}, u32[]{:S(2)}) copy-start(bf16[2,128,256]{2,1,0:T(8,128)(2,1)} %refs_0_.8) | copy-start | bytes 393220
  13.9 26.7 %collective-permute-start.3 = (bf16[128,512]{1,0:T(8,128)(2,1)S(1)}, bf16[128,512]{1,0:T(8,128)(2,1)S(1)}, u32[]{:S(2)}, u32[]{:S(2)}) collective-permute-start(bf16[128,512]{1,0:T(8,128)(2,1)S(1)} %get-tuple-element.32), channel_id=1, source_target_pairs={{0,12},{4,8},{8,4},{12,0},{1,13},{5,9},{9,5},{13,1},{2,14},{6,10},... | collective-permute-start | bytes 393224 | tf_op jit(solution)/shard_map/ppermute | solution.py:26
  40.1 5.7 %collective-permute-start.10 = (bf16[192,512]{1,0:T(8,128)(2,1)S(1)}, bf16[192,512]{1,0:T(8,128)(2,1)S(1)}, u32[]{:S(2)}, u32[]{:S(2)}) collective-permute-start(bf16[192,512]{1,0:T(8,128)(2,1)S(1)} %get-tuple-element.40), channel_id=1, source_target_pairs={{0,8},{4,12},{8,0},{12,4},{1,9},{5,13},{9,1},{13,5},{2,10},{6,14},... | collective-permute-start | bytes 589832 | tf_op jit(solution)/shard_map/ppermute | solution.py:26
  40.6 6.3 %collective-permute-start.9 = (bf16[192,512]{1,0:T(8,128)(2,1)S(1)}, bf16[192,512]{1,0:T(8,128)(2,1)S(1)}, u32[]{:S(2)}, u32[]{:S(2)}) collective-permute-start(bf16[192,512]{1,0:T(8,128)(2,1)S(1)} %get-tuple-element.39), channel_id=1, source_target_pairs={{0,4},{4,0},{8,12},{12,8},{1,5},{5,1},{9,13},{13,9},{2,6},{6,2},{1... | collective-permute-start | bytes 589832 | tf_op jit(solution)/shard_map/ppermute | solution.py:26
  45.8 5.9 %collective-permute-start.18 = (bf16[128,512]{1,0:T(8,128)(2,1)S(1)}, bf16[128,512]{1,0:T(8,128)(2,1)S(1)}, u32[]{:S(2)}, u32[]{:S(2)}) collective-permute-start(bf16[128,512]{1,0:T(8,128)(2,1)S(1)} %get-tuple-element.45), channel_id=1, source_target_pairs={{0,12},{4,8},{8,4},{12,0},{1,13},{5,9},{9,5},{13,1},{2,14},{6,10},... | collective-permute-start | bytes 393224 | tf_op jit(solution)/shard_map/ppermute | solution.py:26
  46.9 35.4 %copy-start.4 = (f32[1024]{0:T(1024)S(1)}, f32[1024]{0:T(1024)}, u32[]{:S(2)}) copy-start(f32[1024]{0:T(1024)} %param.13) | copy-start | bytes 12292
  46.9 4.8 %collective-permute-start.6 = (bf16[32,1152]{1,0:T(8,128)(2,1)S(1)}, bf16[32,1152]{1,0:T(8,128)(2,1)S(1)}, u32[]{:S(2)}, u32[]{:S(2)}) collective-permute-start(bf16[32,1152]{1,0:T(8,128)(2,1)S(1)} %get-tuple-element.36), channel_id=1, source_target_pairs={{0,1},{1,0},{2,3},{3,2},{4,5},{5,4},{6,7},{7,6},{8,9},{9,8},{10,11... | collective-permute-start | bytes 221192 | tf_op jit(solution)/shard_map/ppermute | solution.py:26
  48.7 15.9 %collective-permute-start.11 = (bf16[8,256,128]{2,1,0:T(8,128)(2,1)S(1)}, bf16[8,256,128]{2,1,0:T(8,128)(2,1)S(1)}, u32[]{:S(2)}, u32[]{:S(2)}) collective-permute-start(bf16[8,256,128]{2,1,0:T(8,128)(2,1)S(1)} %shard_map.77.refs_5_.refs_6_), channel_id=1, source_target_pairs={{0,16},{16,0},{1,17},{17,1},{2,18},{18,2},{3,19},{19,3},{4,20},{20... | collective-permute-start | bytes 1572872 | tf_op jit(solution)/shard_map/ppermute | solution.py:463
  48.8 8.9 %collective-permute-start.7 = (bf16[32,1152]{1,0:T(8,128)(2,1)S(1)}, bf16[32,1152]{1,0:T(8,128)(2,1)S(1)}, u32[]{:S(2)}, u32[]{:S(2)}) collective-permute-start(bf16[32,1152]{1,0:T(8,128)(2,1)S(1)} %get-tuple-element.37), channel_id=1, source_target_pairs={{0,2},{1,3},{2,0},{3,1},{4,6},{5,7},{6,4},{7,5},{8,10},{9,11},{10,... | collective-permute-start | bytes 221192 | tf_op jit(solution)/shard_map/ppermute | solution.py:26
  51.4 6.3 %collective-permute-start.8 = (bf16[32,1152]{1,0:T(8,128)(2,1)S(1)}, bf16[32,1152]{1,0:T(8,128)(2,1)S(1)}, u32[]{:S(2)}, u32[]{:S(2)}) collective-permute-start(bf16[32,1152]{1,0:T(8,128)(2,1)S(1)} %get-tuple-element.38), channel_id=1, source_target_pairs={{0,3},{1,2},{2,1},{3,0},{4,7},{5,6},{6,5},{7,4},{8,11},{9,10},{10,... | collective-permute-start | bytes 221192 | tf_op jit(solution)/shard_map/ppermute | solution.py:26
  51.6 19.9 %collective-permute-start.15 = (bf16[2,256,512]{2,1,0:T(8,128)(2,1)S(1)}, bf16[2,256,512]{2,1,0:T(8,128)(2,1)S(1)}, u32[]{:S(2)}, u32[]{:S(2)}) collective-permute-start(bf16[2,256,512]{2,1,0:T(8,128)(2,1)S(1)} %shard_map.79.refs_7_), channel_id=1, source_target_pairs={{0,16},{16,0},{1,17},{17,1},{2,18},{18,2},{3,19},{19,3},{4,20},{20... | collective-permute-start | bytes 1572872 | tf_op jit(solution)/shard_map/ppermute | solution.py:463
  51.7 21.9 %collective-permute-start.17 = (bf16[2,256,512]{2,1,0:T(8,128)(2,1)S(1)}, bf16[2,256,512]{2,1,0:T(8,128)(2,1)S(1)}, u32[]{:S(2)}, u32[]{:S(2)}) collective-permute-start(bf16[2,256,512]{2,1,0:T(8,128)(2,1)S(1)} %collective-permute-done.16.refs_9_), channel_id=1, source_target_pairs={{0,16},{16,0},{1,17},{17,1},{2,18},{18,2},{3,19},{19,3},{4,20},{20... | collective-permute-start | bytes 1572872 | tf_op jit(solution)/shard_map/ppermute | solution.py:463
  57.7 4.8 %collective-permute-start.19 = (bf16[32,1024]{1,0:T(8,128)(2,1)S(1)}, bf16[32,1024]{1,0:T(8,128)(2,1)S(1)}, u32[]{:S(2)}, u32[]{:S(2)}) collective-permute-start(bf16[32,1024]{1,0:T(8,128)(2,1)S(1)} %get-tuple-element.47), channel_id=1, source_target_pairs={{0,1},{1,0},{2,3},{3,2},{4,5},{5,4},{6,7},{7,6},{8,9},{9,8},{10,11... | collective-permute-start | bytes 196616 | tf_op jit(solution)/shard_map/ppermute | solution.py:26
  57.7 6.9 %collective-permute-start.20 = (bf16[32,1024]{1,0:T(8,128)(2,1)S(1)}, bf16[32,1024]{1,0:T(8,128)(2,1)S(1)}, u32[]{:S(2)}, u32[]{:S(2)}) collective-permute-start(bf16[32,1024]{1,0:T(8,128)(2,1)S(1)} %get-tuple-element.48), channel_id=1, source_target_pairs={{0,2},{1,3},{2,0},{3,1},{4,6},{5,7},{6,4},{7,5},{8,10},{9,11},{10,... | collective-permute-start | bytes 196616 | tf_op jit(solution)/shard_map/ppermute | solution.py:26
  62.5 24.9 %collective-permute-start.27 = (bf16[2,256,512]{2,1,0:T(8,128)(2,1)S(1)}, bf16[2,256,512]{2,1,0:T(8,128)(2,1)S(1)}, u32[]{:S(2)}, u32[]{:S(2)}) collective-permute-start(bf16[2,256,512]{2,1,0:T(8,128)(2,1)S(1)} %collective-permute-done.25.refs_5_), channel_id=1, source_target_pairs={{0,16},{16,0},{1,17},{17,1},{2,18},{18,2},{3,19},{19,3},{4,20},{20... | collective-permute-start | bytes 1572872 | tf_op jit(solution)/shard_map/ppermute | solution.py:463
  64.6 23.1 %collective-permute-start.28 = (bf16[2,256,512]{2,1,0:T(8,128)(2,1)S(1)}, bf16[2,256,512]{2,1,0:T(8,128)(2,1)S(1)}, u32[]{:S(2)}, u32[]{:S(2)}) collective-permute-start(bf16[2,256,512]{2,1,0:T(8,128)(2,1)S(1)} %collective-permute-done.26.refs_6_), channel_id=1, source_target_pairs={{0,16},{16,0},{1,17},{17,1},{2,18},{18,2},{3,19},{19,3},{4,20},{20... | collective-permute-start | bytes 1572872 | tf_op jit(solution)/shard_map/ppermute | solution.py:463
  64.6 6.3 %collective-permute-start.21 = (bf16[32,1024]{1,0:T(8,128)(2,1)S(1)}, bf16[32,1024]{1,0:T(8,128)(2,1)S(1)}, u32[]{:S(2)}, u32[]{:S(2)}) collective-permute-start(bf16[32,1024]{1,0:T(8,128)(2,1)S(1)} %get-tuple-element.49), channel_id=1, source_target_pairs={{0,3},{1,2},{2,1},{3,0},{4,7},{5,6},{6,5},{7,4},{8,11},{9,10},{10,... | collective-permute-start | bytes 196616 | tf_op jit(solution)/shard_map/ppermute | solution.py:26
  71.4 4.7 %collective-permute-start.22 = (bf16[32,1024]{1,0:T(8,128)(2,1)S(1)}, bf16[32,1024]{1,0:T(8,128)(2,1)S(1)}, u32[]{:S(2)}, u32[]{:S(2)}) collective-permute-start(bf16[32,1024]{1,0:T(8,128)(2,1)S(1)} %shard_map.82.refs_3_), channel_id=1, source_target_pairs={{0,1},{1,0},{2,3},{3,2},{4,5},{5,4},{6,7},{7,6},{8,9},{9,8},{10,11... | collective-permute-start | bytes 196616 | tf_op jit(solution)/shard_map/ppermute | solution.py:26
  71.5 8.6 %collective-permute-start.23 = (bf16[32,1024]{1,0:T(8,128)(2,1)S(1)}, bf16[32,1024]{1,0:T(8,128)(2,1)S(1)}, u32[]{:S(2)}, u32[]{:S(2)}) collective-permute-start(bf16[32,1024]{1,0:T(8,128)(2,1)S(1)} %shard_map.82.refs_3_), channel_id=1, source_target_pairs={{0,2},{1,3},{2,0},{3,1},{4,6},{5,7},{6,4},{7,5},{8,10},{9,11},{10,... | collective-permute-start | bytes 196616 | tf_op jit(solution)/shard_map/ppermute | solution.py:26
  73.6 6.6 %collective-permute-start.24 = (bf16[32,1024]{1,0:T(8,128)(2,1)S(1)}, bf16[32,1024]{1,0:T(8,128)(2,1)S(1)}, u32[]{:S(2)}, u32[]{:S(2)}) collective-permute-start(bf16[32,1024]{1,0:T(8,128)(2,1)S(1)} %shard_map.82.refs_3_), channel_id=1, source_target_pairs={{0,3},{1,2},{2,1},{3,0},{4,7},{5,6},{6,5},{7,4},{8,11},{9,10},{10,... | collective-permute-start | bytes 196616 | tf_op jit(solution)/shard_map/ppermute | solution.py:26
  76.2 6.8 %collective-permute-start.12 = (bf16[32,1024]{1,0:T(8,128)(2,1)S(1)}, bf16[32,1024]{1,0:T(8,128)(2,1)S(1)}, u32[]{:S(2)}, u32[]{:S(2)}) collective-permute-start(bf16[32,1024]{1,0:T(8,128)(2,1)S(1)} %get-tuple-element.42.refs_3_), channel_id=1, source_target_pairs={{0,1},{1,0},{2,3},{3,2},{4,5},{5,4},{6,7},{7,6},{8,9},{9,8},{10,11... | collective-permute-start | bytes 196616 | tf_op jit(solution)/shard_map/ppermute | solution.py:26
  80.1 5.2 %collective-permute-start.13 = (bf16[32,1024]{1,0:T(8,128)(2,1)S(1)}, bf16[32,1024]{1,0:T(8,128)(2,1)S(1)}, u32[]{:S(2)}, u32[]{:S(2)}) collective-permute-start(bf16[32,1024]{1,0:T(8,128)(2,1)S(1)} %get-tuple-element.42.refs_3_), channel_id=1, source_target_pairs={{0,2},{1,3},{2,0},{3,1},{4,6},{5,7},{6,4},{7,5},{8,10},{9,11},{10,... | collective-permute-start | bytes 196616 | tf_op jit(solution)/shard_map/ppermute | solution.py:26
  80.2 6.1 %collective-permute-start.14 = (bf16[32,1024]{1,0:T(8,128)(2,1)S(1)}, bf16[32,1024]{1,0:T(8,128)(2,1)S(1)}, u32[]{:S(2)}, u32[]{:S(2)}) collective-permute-start(bf16[32,1024]{1,0:T(8,128)(2,1)S(1)} %get-tuple-element.42.refs_3_), channel_id=1, source_target_pairs={{0,3},{1,2},{2,1},{3,0},{4,7},{5,6},{6,5},{7,4},{8,11},{9,10},{10,... | collective-permute-start | bytes 196616 | tf_op jit(solution)/shard_map/ppermute | solution.py:26
